TPU v7x, 8 devices: a whole 2x2x1 slice. The times are simulated.
8 devices in a mesh: sp: 8 (over z, y, x, core).
Axes of the slice: x: 2, y: 2, z: 1, core: 2. Of those that a mesh axis runs over, the one named last changes fastest.
Arguments:
- x_in: bfloat16 [2048, 2048], P('sp')
- positions: int32 [2048], P('sp')
- d_out: bfloat16 [2048, 2048], P('sp')
- norm1_gain: bfloat16 [2048], P('sp')
- norm2_gain: bfloat16 [2048], P('sp')
- w_q: bfloat16 [2048, 32, 64], P('sp')
- w_k: bfloat16 [2048, 8, 64], P('sp')
- w_v: bfloat16 [2048, 8, 64], P('sp')
- w_o: bfloat16 [32, 64, 2048], P('sp')
- w_gate: bfloat16 [2048, 8192], P('sp')
- w_up: bfloat16 [2048, 8192], P('sp')
- w_down: bfloat16 [8192, 2048], P('sp')
Outputs:
- output 1: bfloat16 [2048, 2048], P('sp')
- output 2: bfloat16 [2048, 2048], P('sp')
- output 3: float32 [2048], P('sp')
- output 4: float32 [2048], P('sp')
- output 5: float32 [2048, 32, 64], P('sp')
- output 6: float32 [2048, 8, 64], P('sp')
- output 7: float32 [2048, 8, 64], P('sp')
- output 8: float32 [32, 64, 2048], P('sp')
- output 9: float32 [2048, 8192], P('sp')
- output 10: float32 [2048, 8192], P('sp')
- output 11: float32 [8192, 2048], P('sp')
All inputs are finite; a program needn't handle non-finite values.
Results may differ from a plain program's by a relative error of at most 0.0179383.
Values are sent between devices in bfloat16 or wider.
A program may use at most 1 GiB of HBM per device.

v0:
```python
import functools
import jax
import jax.numpy as jnp
from jax import lax
from jax.sharding import PartitionSpec as P

ROPE_BASE = 10000.0
NORM_EPS = 1e-5
NEG_LARGE = -1e30


def norm_forward(hidden, gain_vec):
    inv_rms = lax.rsqrt(jnp.mean(hidden * hidden, axis=-1, keepdims=True) + NORM_EPS)
    return hidden * inv_rms * gain_vec


def rope_tables(positions, head_dim):
    half_dim = head_dim // 2
    inv_freq = 1.0 / (ROPE_BASE ** (jnp.arange(half_dim, dtype=jnp.float32) * (2.0 / head_dim)))
    angles = positions.astype(jnp.float32)[:, None] * inv_freq[None, :]
    return jnp.cos(angles)[:, None, :], jnp.sin(angles)[:, None, :]


def rotate(values_in, cos_tab, sin_tab):
    half_dim = values_in.shape[-1] // 2
    first_half = values_in[..., :half_dim].astype(jnp.float32)
    second_half = values_in[..., half_dim:].astype(jnp.float32)
    return jnp.concatenate([first_half * cos_tab - second_half * sin_tab, second_half * cos_tab + first_half * sin_tab], axis=-1)


def gated_unit(gate_pre, up_pre):
    return jax.nn.silu(gate_pre) * up_pre


def attention_forward(queries, keys_all, values_all):
    seq_len = queries.shape[0]
    score_scale = queries.shape[-1] ** -0.5
    scores = jnp.einsum('skgd,tkd->kgst', queries, keys_all, preferred_element_type=jnp.float32) * score_scale
    causal = jnp.arange(seq_len)[:, None] >= jnp.arange(seq_len)[None, :]
    attn_probs = jax.nn.softmax(jnp.where(causal, scores, NEG_LARGE), axis=-1)
    attn_out = jnp.einsum('kgst,tkd->skgd', attn_probs.astype(jnp.bfloat16), values_all, preferred_element_type=jnp.float32)
    return attn_out.astype(jnp.bfloat16), attn_probs


def attention_backward(queries, keys_all, values_all, attn_probs, d_attn):
    score_scale = queries.shape[-1] ** -0.5
    probs_b16 = attn_probs.astype(jnp.bfloat16)
    d_probs = jnp.einsum('skgd,tkd->kgst', d_attn, values_all, preferred_element_type=jnp.float32)
    d_probs = d_probs.astype(jnp.bfloat16).astype(jnp.float32)
    row_dot = jnp.sum(d_probs * attn_probs, axis=-1, keepdims=True)
    d_scores = (attn_probs * (d_probs - row_dot) * score_scale).astype(jnp.bfloat16)
    d_queries = jnp.einsum('kgst,tkd->skgd', d_scores, keys_all, preferred_element_type=jnp.float32)
    d_keys = jnp.einsum('kgst,skgd->tkd', d_scores, queries, preferred_element_type=jnp.float32)
    d_values = jnp.einsum('kgst,skgd->tkd', probs_b16, d_attn, preferred_element_type=jnp.float32)
    return d_queries.astype(jnp.bfloat16), d_keys.astype(jnp.bfloat16), d_values.astype(jnp.bfloat16)


def solution(mesh):
    n_devices = mesh.shape['sp']
    gather_rows = functools.partial(lax.all_gather, axis_name='sp', axis=0, tiled=True)
    scatter_rows = functools.partial(lax.psum_scatter, axis_name='sp', scatter_dimension=0, tiled=True)
    to_heads = functools.partial(lax.all_to_all, axis_name='sp', split_axis=1, concat_axis=0, tiled=True)
    to_tokens = functools.partial(lax.all_to_all, axis_name='sp', split_axis=0, concat_axis=1, tiled=True)

    def layer_step(x_in, positions, d_out, norm1_gain, norm2_gain, w_q, w_k, w_v, w_o, w_gate, w_up, w_down):
        g1_full, g2_full, wq_full, wk_full, wv_full, wo_full, gate_full, up_full, down_full = [gather_rows(shard_w) for shard_w in (norm1_gain, norm2_gain, w_q, w_k, w_v, w_o, w_gate, w_up, w_down)]
        tokens = x_in.shape[0]
        seq_len = tokens * n_devices
        head_dim = w_q.shape[2]
        kv_heads = w_k.shape[1]
        kv_repeat = max(1, n_devices // kv_heads)
        cos_tab, sin_tab = rope_tables(positions, head_dim)

        x_f32 = x_in.astype(jnp.float32)
        normed_pre, norm1_pull = jax.vjp(norm_forward, x_f32, g1_full.astype(jnp.float32))
        normed = normed_pre.astype(jnp.bfloat16)
        q_lin = jnp.einsum('td,dhe->the', normed, wq_full, preferred_element_type=jnp.float32).astype(jnp.bfloat16)
        k_lin = jnp.einsum('td,dhe->the', normed, wk_full, preferred_element_type=jnp.float32).astype(jnp.bfloat16)
        v_lin = jnp.einsum('td,dhe->the', normed, wv_full, preferred_element_type=jnp.float32).astype(jnp.bfloat16)
        q_rot = rotate(q_lin, cos_tab, sin_tab).astype(jnp.bfloat16)
        k_rot = rotate(k_lin, cos_tab, sin_tab).astype(jnp.bfloat16)
        q_seq = to_heads(q_rot)
        k_seq = to_heads(jnp.repeat(k_rot, kv_repeat, axis=1))
        v_seq = to_heads(jnp.repeat(v_lin, kv_repeat, axis=1))
        kv_local = k_seq.shape[1]
        q_grouped = q_seq.reshape(seq_len, kv_local, -1, head_dim)
        attn_seq, attn_probs = attention_forward(q_grouped, k_seq, v_seq)
        attn_tok = to_tokens(attn_seq.reshape(seq_len, -1, head_dim))
        attn_proj = jnp.einsum('the,hed->td', attn_tok, wo_full, preferred_element_type=jnp.float32)
        hidden = (x_f32 + attn_proj).astype(jnp.bfloat16)
        hidden_f32 = hidden.astype(jnp.float32)
        mlp_pre, norm2_pull = jax.vjp(norm_forward, hidden_f32, g2_full.astype(jnp.float32))
        mlp_in = mlp_pre.astype(jnp.bfloat16)
        gate_act = jnp.dot(mlp_in, gate_full, preferred_element_type=jnp.float32).astype(jnp.bfloat16)
        up_act = jnp.dot(mlp_in, up_full, preferred_element_type=jnp.float32).astype(jnp.bfloat16)
        glu_pre, glu_pull = jax.vjp(gated_unit, gate_act.astype(jnp.float32), up_act.astype(jnp.float32))
        glu_out = glu_pre.astype(jnp.bfloat16)
        y_out = (hidden_f32 + jnp.dot(glu_out, down_full, preferred_element_type=jnp.float32)).astype(jnp.bfloat16)

        wq_back, wk_back, wv_back, wo_back, gate_back, up_back, down_back = [gather_rows(shard_w) for shard_w in (w_q, w_k, w_v, w_o, w_gate, w_up, w_down)]
        d_down = jnp.einsum('tf,td->fd', glu_out, d_out, preferred_element_type=jnp.float32)
        d_glu = jnp.einsum('td,fd->tf', d_out, down_back, preferred_element_type=jnp.float32).astype(jnp.bfloat16)
        d_gate_f, d_up_f = glu_pull(d_glu.astype(jnp.float32))
        d_gate_act = d_gate_f.astype(jnp.bfloat16)
        d_up_act = d_up_f.astype(jnp.bfloat16)
        d_gate = jnp.einsum('td,tf->df', mlp_in, d_gate_act, preferred_element_type=jnp.float32)
        d_up = jnp.einsum('td,tf->df', mlp_in, d_up_act, preferred_element_type=jnp.float32)
        d_mlp_in = (jnp.einsum('tf,df->td', d_gate_act, gate_back, preferred_element_type=jnp.float32) + jnp.einsum('tf,df->td', d_up_act, up_back, preferred_element_type=jnp.float32)).astype(jnp.bfloat16)
        d_hidden_norm, d_g2 = norm2_pull(d_mlp_in.astype(jnp.float32))
        d_hidden = (d_out.astype(jnp.float32) + d_hidden_norm).astype(jnp.bfloat16)
        d_wo = jnp.einsum('the,td->hed', attn_tok, d_hidden, preferred_element_type=jnp.float32)
        d_attn_tok = jnp.einsum('td,hed->the', d_hidden, wo_back, preferred_element_type=jnp.float32).astype(jnp.bfloat16)
        d_attn_seq = to_heads(d_attn_tok).reshape(seq_len, kv_local, -1, head_dim)
        d_q_seq, d_k_seq, d_v_seq = attention_backward(q_grouped, k_seq, v_seq, attn_probs, d_attn_seq)
        d_q_rot = to_tokens(d_q_seq.reshape(seq_len, -1, head_dim))
        d_k_rot = jnp.sum(to_tokens(d_k_seq).reshape(tokens, kv_heads, kv_repeat, head_dim), axis=2, dtype=jnp.float32).astype(jnp.bfloat16)
        d_v_lin = jnp.sum(to_tokens(d_v_seq).reshape(tokens, kv_heads, kv_repeat, head_dim), axis=2, dtype=jnp.float32).astype(jnp.bfloat16)
        d_q_lin = rotate(d_q_rot, cos_tab, -sin_tab).astype(jnp.bfloat16)
        d_k_lin = rotate(d_k_rot, cos_tab, -sin_tab).astype(jnp.bfloat16)
        d_wq = jnp.einsum('td,the->dhe', normed, d_q_lin, preferred_element_type=jnp.float32)
        d_wk = jnp.einsum('td,the->dhe', normed, d_k_lin, preferred_element_type=jnp.float32)
        d_wv = jnp.einsum('td,the->dhe', normed, d_v_lin, preferred_element_type=jnp.float32)
        d_normed = (jnp.einsum('the,dhe->td', d_q_lin, wq_back, preferred_element_type=jnp.float32) + jnp.einsum('the,dhe->td', d_k_lin, wk_back, preferred_element_type=jnp.float32) + jnp.einsum('the,dhe->td', d_v_lin, wv_back, preferred_element_type=jnp.float32)).astype(jnp.bfloat16)
        d_x_norm, d_g1 = norm1_pull(d_normed.astype(jnp.float32))
        d_x = (d_hidden.astype(jnp.float32) + d_x_norm).astype(jnp.bfloat16)
        grad_parts = (d_g1, d_g2, d_wq, d_wk, d_wv, d_wo, d_gate, d_up, d_down)
        return (y_out, d_x) + tuple(scatter_rows(grad_part) for grad_part in grad_parts)

    all_rows = P('sp')
    return jax.shard_map(layer_step, mesh=mesh, in_specs=(all_rows,) * 12, out_specs=(all_rows,) * 11, check_vma=False)
```

profile of v0, /device:TPU:0, one launch (start us, length us, event | category | flops | bytes accessed | tf_op | source)
XLA Modules:
  0.0 2309.1 jit_solution(1098064140440178439)
XLA Ops:
  11.9 13.6 all-gather
  40.3 20.7 all-gather.12.cloned.1.call-done
  64.3 48.5 %all-gather.14.cloned.1.call-done = bf16[2048,32,64]{0,2,1:T(8,128)(2,1)} async-done(((bf16[256,32,64]{0,2,1:T(8,128)(2,1)}), bf16[2048,32,64]{0,2,1:T(8,128)(2,1)}) %all-gather.14.cloned.1.call-update) | async-done | bytes 8388624 | tf_op jit(solution)/shard_map/all_gather | solution.py:66
  138.3 13.9 all-to-all-done.2
  152.4 26.0 %fusion.8 = (f32[4,2048]{1,0:T(4,128)S(1)}, f32[2048,2048,4]{1,0,2:T(8,128)}) fusion(pred[2048,2048]{0,1:T(8,128)(4,1)} %iota_compare_fusion, bf16[2048,64,1]{0,1,2:T(8,128)(2,1)S(1)} %reshape.244, bf16[2048,4,64]{0,2,1:T(8,128)(2,1)S(1)} %bitcast.214), kind=kOutput, calls=%fused_computation.11 | convolution fusion | flops 2197807104 | bytes 72646656 | tf_op jit(solution)/shard_map/skgd,tkd->kgst/dot_general | solution.py:38
  178.5 22.9 fusion.7
  201.4 28.2 %fusion.37 = bf16[2048,4,64]{0,2,1:T(8,128)(2,1)S(1)} fusion(bf16[2048,64,1]{0,1,2:T(8,128)(2,1)S(1)} %reshape.245, f32[4,2048]{1,0:T(4,128)S(1)} %fusion.7, f32[4,2048]{1,0:T(4,128)S(1)} %get-tuple-element.28, f32[2048,2048,4]{1,0,2:T(8,128)} %get-tuple-element.29, pred[2048,2048]{0,1:T(8,128)(4,1)} %iota_compare_fusion), kind=kOutput, calls=%fused_computation.72 | convolution fusion | flops 2231894016 | bytes 72679424 | tf_op jit(solution)/shard_map/kgst,tkd->skgd/dot_general | solution.py:41
  236.2 31.1 %all-gather.1 = bf16[8,1,256]{2,1,0:T(2,128)(2,1)S(1)} all-gather(bf16[1,1,256]{2,1,0:T(2,128)(2,1)S(1)} %reshape.234), channel_id=1, replica_groups=mesh['sp'=8] {'sp'}, dimensions={0}, use_global_device_ids=true | all-gather | bytes 4608 | tf_op jit(solution)/shard_map/all_gather | solution.py:66
  279.1 61.3 %all-gather.20.cloned.1.call-done = bf16[2048,8192]{1,0:T(8,128)(2,1)} async-done(((bf16[256,8192]{1,0:T(8,128)(2,1)}), bf16[2048,8192]{1,0:T(8,128)(2,1)}) %all-gather.20.cloned.1.call-update) | async-done | bytes 33554448 | tf_op jit(solution)/shard_map/all_gather | solution.py:66
  340.4 16.5 convolution_convert_fusion.2
  356.8 140.4 %all-gather.18.cloned.1.call-done = bf16[2048,8192]{1,0:T(8,128)(2,1)} async-done(((bf16[256,8192]{1,0:T(8,128)(2,1)}), bf16[2048,8192]{1,0:T(8,128)(2,1)}) %all-gather.18.cloned.1.call-update) | async-done | bytes 33554448 | tf_op jit(solution)/shard_map/all_gather | solution.py:66
  497.3 16.5 convolution_convert_fusion.3
  513.7 140.6 %all-gather.22.cloned.1.call-done = bf16[8192,2048]{1,0:T(8,128)(2,1)} async-done(((bf16[1024,2048]{1,0:T(8,128)(2,1)}), bf16[8192,2048]{1,0:T(8,128)(2,1)}) %all-gather.22.cloned.1.call-update) | async-done | bytes 33554448 | tf_op jit(solution)/shard_map/all_gather | solution.py:66
  654.3 16.9 convolution_convert_fusion.1
  671.2 20.0 fusion.113
  691.2 18.7 fusion.53
  716.8 17.2 all_to_all.114
  734.1 40.3 %fusion.2 = (f32[4,2048]{1,0:T(4,128)S(1)}, bf16[2048,2048,4]{1,0,2:T(8,128)(2,1)}) fusion(f32[4,2048]{1,0:T(4,128)S(1)} %fusion.7, f32[4,2048]{1,0:T(4,128)S(1)} %get-tuple-element.28, f32[2048,2048,4]{1,0,2:T(8,128)} %get-tuple-element.29, pred[2048,2048]{0,1:T(8,128)(4,1)S(1)} %copy-done, bf16[2048,64,1]{0,1,2:T(8,128)(2,1)S(1)} %reshape.245, ...), kind=kOutput, calls=%fused_computation.4 | convolution fusion | flops 2281693184 | bytes 106266624 | tf_op jit(solution)/shard_map/skgd,tkd->kgst/dot_general | solution.py:48
  774.4 44.1 %fusion.9 = bf16[4,2048,2048]{1,2,0:T(8,128)(2,1)} fusion(bf16[2048,2048,4]{1,0,2:T(8,128)(2,1)} %get-tuple-element.34, f32[4,2048]{1,0:T(4,128)S(1)} %get-tuple-element.33, f32[4,2048]{1,0:T(4,128)S(1)} %fusion.7, f32[4,2048]{1,0:T(4,128)S(1)} %get-tuple-element.28, f32[2048,2048,4]{1,0,2:T(8,128)} %get-tuple-element.29, pred[2048,2048]{0,1:T(8,128)(4,1)S(1)} %copy-done), kind=kLoop, calls=%fused_computation.12 | loop fusion | flops 150994944 | bytes 138510336 | tf_op jit(solution)/shard_map/reshape.26
  818.6 14.9 fusion.50
  848.4 27.3 %fusion.47 = bf16[2048,1,64]{0,2,1:T(8,128)(2,1)S(1)} fusion(bf16[2048,4,64]{0,2,1:T(8,128)(2,1)S(1)} %bitcast.233, f32[4,2048]{1,0:T(4,128)S(1)} %fusion.7, f32[4,2048]{1,0:T(4,128)S(1)} %get-tuple-element.28, f32[2048,2048,4]{1,0,2:T(8,128)} %get-tuple-element.29, pred[2048,2048]{0,1:T(8,128)(4,1)} %iota_compare_fusion), kind=kOutput, calls=%fused_computation.77 | convolution fusion | flops 2231500800 | bytes 72679424 | tf_op jit(solution)/shard_map/kgst,skgd->tkd/dot_general | solution.py:54
  900.9 13.7 fusion.36
  920.4 22.7 all_to_all.117
  960.5 28.6 %fusion.89 = f32[2048,8192]{1,0:T(8,128)} fusion(bf16[256,2048]{1,0:T(8,128)(2,1)S(1)} %copy-done.8, f32[2048]{0:T(1024)S(1)} %bitcast.224, f32[256]{0:T(256)S(1)} %copy-done.31, bf16[256,8192]{1,0:T(8,128)(2,1)} %convolution_convert_fusion.3, bf16[256,8192]{1,0:T(8,128)(2,1)} %convolution_convert_fusion.2, bf16[256,8192]{1,0:T(8,128)(2,1)} %convolution_convert_fusion.1), kind=kOutput, calls=%fused_computation.144 | convolution fusion | flops 8621391872 | bytes 80749568 | tf_op jit(solution)/shard_map/td,tf->df/dot_general | solution.py:106
  989.1 27.5 %fusion.87 = f32[2048,8192]{1,0:T(8,128)} fusion(bf16[256,2048]{1,0:T(8,128)(2,1)S(1)} %copy-done.8, f32[2048]{0:T(1024)S(1)} %bitcast.225, f32[256]{0:T(256)S(1)} %copy-done.31, bf16[256,8192]{1,0:T(8,128)(2,1)} %convolution_convert_fusion.1, bf16[256,8192]{1,0:T(8,128)(2,1)} %convolution_convert_fusion.3), kind=kOutput, calls=%fused_computation.143 | convolution fusion | flops 8608808960 | bytes 76555264 | tf_op jit(solution)/shard_map/td,tf->df/dot_general | solution.py:107
  1017.8 27.1 %fusion.109 = f32[8192,2048]{1,0:T(8,128)} fusion(bf16[256,2048]{1,0:T(8,128)(2,1)S(1)} %copy-done.17, bf16[256,8192]{1,0:T(8,128)(2,1)} %convolution_convert_fusion.2, bf16[256,8192]{1,0:T(8,128)(2,1)} %convolution_convert_fusion.3), kind=kOutput, calls=%fused_computation.151 | convolution fusion | flops 8606711808 | bytes 76546048 | tf_op jit(solution)/shard_map/tf,td->fd/dot_general | solution.py:101
  1045.0 19.7 fusion.26
  1073.6 22.6 all-reduce.2
  1099.3 66.7 %reduce-scatter.8.cloned.1.call-done = f32[256,32,64]{0,2,1:T(8,128)} async-done(((f32[2048,32,64]{0,2,1:T(8,128)}), f32[256,32,64]{0,2,1:T(8,128)}) %reduce-scatter.8.cloned.1.call-update) | async-done | bytes 2097168 | tf_op jit(solution)/shard_map/reduce_scatter | solution.py:127
  1165.9 378.7 %reduce-scatter.16.cloned.1.call-done = f32[256,8192]{1,0:T(8,128)} async-done(((f32[2048,8192]{1,0:T(8,128)}), f32[256,8192]{1,0:T(8,128)}) %reduce-scatter.16.cloned.1.call-update) | async-done | bytes 8388624 | tf_op jit(solution)/shard_map/reduce_scatter | solution.py:127
  1544.6 378.8 %reduce-scatter.18.cloned.1.call-done = f32[256,8192]{1,0:T(8,128)} async-done(((f32[2048,8192]{1,0:T(8,128)}), f32[256,8192]{1,0:T(8,128)}) %reduce-scatter.18.cloned.1.call-update) | async-done | bytes 8388624 | tf_op jit(solution)/shard_map/reduce_scatter | solution.py:127
  1923.4 378.7 %reduce-scatter.20.cloned.1.call-done = f32[1024,2048]{1,0:T(8,128)} async-done(((f32[8192,2048]{1,0:T(8,128)}), f32[1024,2048]{1,0:T(8,128)}) %reduce-scatter.20.cloned.1.call-update) | async-done | bytes 8388624 | tf_op jit(solution)/shard_map/reduce_scatter | solution.py:127
  (212 shorter events, 149.4 us)
Async XLA Ops:
  7.2 27.9 %all-gather.10.cloned.1.call-start = ((), (), s32[]{:S(2)}) async-start(), calls=%async_computation.15 | async-start | bytes 2359296 | tf_op jit(solution)/shard_map/all_gather | solution.py:66
  7.9 53.1 %all-gather.12.cloned.1.call-start = ((), (), s32[]{:S(2)}) async-start(), calls=%async_computation.16 | async-start | bytes 2359296 | tf_op jit(solution)/shard_map/all_gather | solution.py:66
  8.7 104.2 %all-gather.14.cloned.1.call-start = ((), (), s32[]{:S(2)}) async-start(), calls=%async_computation.17 | async-start | bytes 9437184 | tf_op jit(solution)/shard_map/all_gather | solution.py:66
  9.4 263.4 %all-gather.16.cloned.1.call-start = ((), (), s32[]{:S(2)}) async-start(), calls=%async_computation.18 | async-start | bytes 9437184 | tf_op jit(solution)/shard_map/all_gather | solution.py:66
  10.0 330.4 %all-gather.20.cloned.1.call-start = ((), (), s32[]{:S(2)}) async-start(), calls=%async_computation.20 | async-start | bytes 37748736 | tf_op jit(solution)/shard_map/all_gather | solution.py:66
  10.6 486.7 %all-gather.18.cloned.1.call-start = ((), (), s32[]{:S(2)}) async-start(), calls=%async_computation.19 | async-start | bytes 37748736 | tf_op jit(solution)/shard_map/all_gather | solution.py:66
  11.2 643.1 %all-gather.22.cloned.1.call-start = ((), (), s32[]{:S(2)}) async-start(), calls=%async_computation.21 | async-start | bytes 37748736 | tf_op jit(solution)/shard_map/all_gather | solution.py:66
  25.6 87.3 %copy-start.37 = (f32[8,1,256]{2,1,0:T(1,128)}, f32[8,1,256]{2,1,0:T(1,128)S(1)}, u32[]{:S(2)}) copy-start(f32[8,1,256]{2,1,0:T(1,128)S(1)} %convert_element_type.269) | copy-start | bytes 24580
  25.9 86.9 %copy-start.40 = (f32[256]{0:T(256)}, f32[256]{0:T(256)S(1)}, u32[]{:S(2)}) copy-start(f32[256]{0:T(256)S(1)} %fusion.84) | copy-start | bytes 3076
  26.7 94.3 %copy-start.28 = (f32[256,32]{0,1:T(8,128)}, f32[256,32]{0,1:T(8,128)S(1)}, u32[]{:S(2)}) copy-start(f32[256,32]{0,1:T(8,128)S(1)} %get-tuple-element.27) | copy-start | bytes 98308
  38.2 80.6 %all-to-all-start = ((bf16[256,8,64]{0,2,1:T(8,128)(2,1)}), bf16[256,8,64]{0,2,1:T(8,128)(2,1)S(1)}, u32[]{:S(2)}, u32[]{:S(2)}) async-start(bf16[256,8,64]{0,2,1:T(8,128)(2,1)} %convert_element_type.208), calls=%async_computation | async-start | bytes 524288 | tf_op jit(solution)/shard_map/all_to_all | solution.py:84
  118.8 12.0 all-to-all-start.1
  130.8 21.4 all-to-all-start.2
  138.3 40.1 %copy-start.22 = (bf16[2048,64,1]{0,1,2:T(8,128)(2,1)}, bf16[2048,64,1]{0,1,2:T(8,128)(2,1)S(1)}, u32[]{:S(2)}) copy-start(bf16[2048,64,1]{0,1,2:T(8,128)(2,1)S(1)} %reshape.244) | copy-start | bytes 786436
  152.4 26.1 %copy-start.18 = (bf16[8,4,8,8,256]{4,3,0,2,1:T(8,128)(2,1)}, bf16[8,4,8,8,256]{4,3,0,2,1:T(8,128)(2,1)S(1)}, u32[]{:S(2)}) copy-start(bf16[8,4,8,8,256]{4,3,0,2,1:T(8,128)(2,1)S(1)} %copy.70) | copy-start | bytes 3145732
  233.7 39.1 %copy-start.2 = (bf16[256,2048]{1,0:T(8,128)(2,1)S(1)}, bf16[256,2048]{1,0:T(8,128)(2,1)}, u32[]{:S(2)}) copy-start(bf16[256,2048]{1,0:T(8,128)(2,1)} %param.12) | copy-start | bytes 3145732
  233.7 33.6 %all-to-all-start.3 = ((bf16[8,2,32768]{2,1,0:T(2,128)(2,1)}), bf16[8,2,32768]{2,1,0:T(2,128)(2,1)S(1)}, u32[]{:S(2)}, u32[]{:S(2)}) async-start(bf16[8,2,32768]{2,1,0:T(2,128)(2,1)} %reshape.262), calls=%async_computation.3 | async-start | bytes 2097152 | tf_op jit(solution)/shard_map/all_to_all | solution.py:88
  236.1 863.1 %reduce-scatter.10.cloned.1.call-start = ((), (), s32[]{:S(2)}) async-start(), calls=%async_computation.23 | async-start | bytes 4718592 | tf_op jit(solution)/shard_map/reduce_scatter | solution.py:127
  267.3 442.5 %copy-start.20 = (f32[8,1,256]{2,1,0:T(1,128)}, f32[8,1,256]{2,1,0:T(1,128)S(1)}, u32[]{:S(2)}) copy-start(f32[8,1,256]{2,1,0:T(1,128)S(1)} %convert_element_type.270) | copy-start | bytes 24580
  279.0 430.8 %copy-start.7 = (bf16[256,2048]{1,0:T(8,128)(2,1)}, bf16[256,2048]{1,0:T(8,128)(2,1)S(1)}, u32[]{:S(2)}) copy-start(bf16[256,2048]{1,0:T(8,128)(2,1)S(1)} %get-tuple-element.31) | copy-start | bytes 3145732
  279.1 430.8 %copy-start.30 = (f32[256]{0:T(256)}, f32[256]{0:T(256)S(1)}, u32[]{:S(2)}) copy-start(f32[256]{0:T(256)S(1)} %fusion.85) | copy-start | bytes 3076
  356.8 297.5 %copy-start.16 = (bf16[256,2048]{1,0:T(8,128)(2,1)S(1)}, bf16[256,2048]{1,0:T(8,128)(2,1)}, u32[]{:S(2)}) copy-start(bf16[256,2048]{1,0:T(8,128)(2,1)} %param.14) | copy-start | bytes 3145732
  734.1 40.3 %copy-start.24 = (bf16[8,4,8,8,256]{4,3,0,2,1:T(8,128)(2,1)}, bf16[8,4,8,8,256]{4,3,0,2,1:T(8,128)(2,1)S(1)}, u32[]{:S(2)}) copy-start(bf16[8,4,8,8,256]{4,3,0,2,1:T(8,128)(2,1)S(1)} %copy.71) | copy-start | bytes 3145732
  774.4 44.1 %copy-start.19 = (bf16[8,4,8,8,256]{4,3,0,2,1:T(8,128)(2,1)S(1)}, bf16[8,4,8,8,256]{4,3,0,2,1:T(8,128)(2,1)}, u32[]{:S(2)}) copy-start(bf16[8,4,8,8,256]{4,3,0,2,1:T(8,128)(2,1)} %copy-done.18) | copy-start | bytes 3145732
  848.2 251.1 %reduce-scatter.12.cloned.1.call-start = ((), (), s32[]{:S(2)}) async-start(), calls=%async_computation.24 | async-start | bytes 4718592 | tf_op jit(solution)/shard_map/reduce_scatter | solution.py:127
  891.8 207.5 %reduce-scatter.14.cloned.1.call-start = ((), (), s32[]{:S(2)}) async-start(), calls=%async_computation.25 | async-start | bytes 18874368 | tf_op jit(solution)/shard_map/reduce_scatter | solution.py:127
  900.0 266.0 %reduce-scatter.8.cloned.1.call-start = ((), (), s32[]{:S(2)}) async-start(), calls=%async_computation.22 | async-start | bytes 18874368 | tf_op jit(solution)/shard_map/reduce_scatter | solution.py:127
  959.3 585.4 %reduce-scatter.16.cloned.1.call-start = ((), (), s32[]{:S(2)}) async-start(), calls=%async_computation.26 | async-start | bytes 75497472 | tf_op jit(solution)/shard_map/reduce_scatter | solution.py:127
  989.1 934.3 %reduce-scatter.18.cloned.1.call-start = ((), (), s32[]{:S(2)}) async-start(), calls=%async_computation.27 | async-start | bytes 75497472 | tf_op jit(solution)/shard_map/reduce_scatter | solution.py:127
  1016.6 1285.5 %reduce-scatter.20.cloned.1.call-start = ((), (), s32[]{:S(2)}) async-start(), calls=%async_computation.28 | async-start | bytes 75497472 | tf_op jit(solution)/shard_map/reduce_scatter | solution.py:127
  1072.2 25.3 %copy-start.44 = (f32[256]{0:T(256)S(1)}, f32[256]{0:T(256)}, u32[]{:S(2)}) copy-start(f32[256]{0:T(256)} %copy-done.43) | copy-start | bytes 3076
  1072.2 25.3 %copy-start.11 = (bf16[256,2048]{1,0:T(8,128)(2,1)S(1)}, bf16[256,2048]{1,0:T(8,128)(2,1)}, u32[]{:S(2)}) copy-start(bf16[256,2048]{1,0:T(8,128)(2,1)} %copy-done.9) | copy-start | bytes 3145732
  (37 other events, 232.6 us)
Sparse Core Ops, SparseCore 0:
  9.8 25.1 all-gather.9
  36.8 24.1 all-gather.11
  62.8 49.9 all-gather.13
  114.5 57.6 all-gather.15
  173.9 166.4 all-gather.19
  342.0 155.1 all-gather.17
  499.1 155.2 all-gather.21
  848.3 42.7 reduce-scatter.9
  894.9 48.1 reduce-scatter.11
  947.0 107.2 reduce-scatter.13
  1058.4 107.5 reduce-scatter.7
  1169.9 374.7 reduce-scatter.15
  1548.7 374.6 reduce-scatter.17
  1927.3 374.7 reduce-scatter.19
where the time goes:
time: 2310 us
  waiting for transfers between devices  1650 us (71%)
  matrix products  395 us (17%)
  blocking collectives  125 us (5%)
  other arithmetic  81.2 us (4%)
  local copies, waits for them, and re-layouts  31.8 us (1%)
    reduce_scatter x7, waiting for transfers between devices, layer_step(): scatter_rows(grad_part)  1200 us
    all_gather x7, waiting for transfers between devices, layer_step(): gather_rows(shard_w)  420 us
    another operation x5, other arithmetic  46.2 us
  transfers between devices with their start and end apart: 18, of which 12 were waited for; matrix products, arithmetic and copies ran while one was open for 15% of the time, Pallas kernels for 0%

commit v1 on v0

v1 whole, which is shorter than its diff:
```python
import functools
import jax
import jax.numpy as jnp
from jax import lax
from jax.experimental import pallas as pl
from jax.experimental.pallas import tpu as pltpu
from jax.sharding import PartitionSpec as P

ROPE_BASE = 10000.0
NORM_EPS = 1e-5
NEG_LARGE = -1e30
F32 = jnp.float32
BF16 = jnp.bfloat16
BLK = 256


def dot(lhs, rhs, lhs_dim, rhs_dim):
    return lax.dot_general(lhs, rhs, (((lhs_dim,), (rhs_dim,)), ((), ())), preferred_element_type=F32)


def norm_forward(hidden, gain_vec):
    inv_rms = lax.rsqrt(jnp.mean(hidden * hidden, axis=-1, keepdims=True) + NORM_EPS)
    return hidden * inv_rms * gain_vec


def rope_tables(positions, head_dim):
    half_dim = head_dim // 2
    inv_freq = 1.0 / (ROPE_BASE ** (jnp.arange(half_dim, dtype=F32) * (2.0 / head_dim)))
    angles = positions.astype(F32)[:, None] * inv_freq[None, :]
    return jnp.cos(angles)[:, None, :], jnp.sin(angles)[:, None, :]


def rotate(values_in, cos_tab, sin_tab):
    half_dim = values_in.shape[-1] // 2
    first_half = values_in[..., :half_dim].astype(F32)
    second_half = values_in[..., half_dim:].astype(F32)
    return jnp.concatenate([first_half * cos_tab - second_half * sin_tab, second_half * cos_tab + first_half * sin_tab], axis=-1)


def probs_transposed(k_rows, q_blk, start):
    scores = dot(k_rows, q_blk, 1, 1)
    rows = lax.broadcasted_iota(jnp.int32, (BLK, BLK), 0)
    cols = lax.broadcasted_iota(jnp.int32, (BLK, BLK), 1)
    tail = jnp.where(rows <= cols, scores[start:], NEG_LARGE)
    scores = jnp.concatenate([scores[:start], tail], axis=0) if start else tail
    top = jnp.max(scores, axis=0, keepdims=True)
    weights = jnp.exp((scores - top) * (q_blk.shape[1] ** -0.5))
    return weights * (1.0 / jnp.sum(weights, axis=0, keepdims=True))


def attention_fwd_kernel(q_ref, k_ref, v_ref, o_ref):
    seq_len = k_ref.shape[0]
    for start in range(0, seq_len, BLK):
        keys = pl.ds(0, start + BLK)
        probs = probs_transposed(k_ref[keys, :], q_ref[0, pl.ds(start, BLK), :], start)
        o_ref[0, pl.ds(start, BLK), :] = dot(probs.astype(BF16), v_ref[keys, :], 0, 0).astype(BF16)


def attention_bwd_kernel(q_ref, k_ref, v_ref, do_ref, dq_ref, dk_ref, dv_ref, dk_acc, dv_acc):
    seq_len, head_dim = k_ref.shape

    @pl.when(pl.program_id(0) == 0)
    def _():
        dk_acc[...] = jnp.zeros_like(dk_acc)
        dv_acc[...] = jnp.zeros_like(dv_acc)

    for start in range(0, seq_len, BLK):
        keys = pl.ds(0, start + BLK)
        rows = pl.ds(start, BLK)
        q_blk, do_blk = q_ref[0, rows, :], do_ref[0, rows, :]
        probs = probs_transposed(k_ref[keys, :], q_blk, start)
        d_probs = dot(v_ref[keys, :], do_blk, 1, 1).astype(BF16).astype(F32)
        row_dot = jnp.sum(d_probs * probs, axis=0, keepdims=True)
        d_scores = (probs * (d_probs - row_dot) * (head_dim ** -0.5)).astype(BF16)
        dq_ref[0, rows, :] = dot(d_scores, k_ref[keys, :], 0, 0).astype(BF16)
        dk_acc[keys, :] += dot(d_scores, q_blk, 1, 0)
        dv_acc[keys, :] += dot(probs.astype(BF16), do_blk, 1, 0)

    @pl.when(pl.program_id(0) == pl.num_programs(0) - 1)
    def _():
        dk_ref[...] = dk_acc[...].astype(BF16)
        dv_ref[...] = dv_acc[...].astype(BF16)


def head_spec(seq_len, head_dim):
    return pl.BlockSpec((1, seq_len, head_dim), lambda h: (h, 0, 0))


def full_spec(seq_len, head_dim):
    return pl.BlockSpec((seq_len, head_dim), lambda h: (0, 0))


def attention_forward(q_heads, keys, values):
    heads, seq_len, head_dim = q_heads.shape
    hs, fs = head_spec(seq_len, head_dim), full_spec(seq_len, head_dim)
    flops = 4 * heads * seq_len * seq_len * head_dim
    return pl.pallas_call(
        attention_fwd_kernel, grid=(heads,), in_specs=[hs, fs, fs], out_specs=hs,
        out_shape=jax.ShapeDtypeStruct(q_heads.shape, BF16), name='attn_fwd',
        cost_estimate=pl.CostEstimate(flops=flops, bytes_accessed=8 * heads * seq_len * head_dim, transcendentals=heads * seq_len * seq_len // 2),
    )(q_heads, keys, values)


def attention_backward(q_heads, keys, values, d_attn):
    heads, seq_len, head_dim = q_heads.shape
    hs, fs = head_spec(seq_len, head_dim), full_spec(seq_len, head_dim)
    flops = 10 * heads * seq_len * seq_len * head_dim
    kv_shape = jax.ShapeDtypeStruct(keys.shape, BF16)
    return pl.pallas_call(
        attention_bwd_kernel, grid=(heads,), in_specs=[hs, fs, fs, hs], out_specs=[hs, fs, fs],
        out_shape=[jax.ShapeDtypeStruct(q_heads.shape, BF16), kv_shape, kv_shape], name='attn_bwd',
        scratch_shapes=[pltpu.VMEM((seq_len, head_dim), F32), pltpu.VMEM((seq_len, head_dim), F32)],
        cost_estimate=pl.CostEstimate(flops=flops, bytes_accessed=8 * heads * seq_len * head_dim, transcendentals=heads * seq_len * seq_len // 2),
    )(q_heads, keys, values, d_attn)


def solution(mesh):
    n_dev = mesh.shape['sp']
    gather_rows = functools.partial(lax.all_gather, axis_name='sp', axis=0, tiled=True)
    scatter_rows = functools.partial(lax.psum_scatter, axis_name='sp', scatter_dimension=0, tiled=True)
    a2a = functools.partial(lax.all_to_all, axis_name='sp', tiled=True)

    def layer_step(x_in, positions, d_out, norm1_gain, norm2_gain, w_q, w_k, w_v, w_o, w_gate, w_up, w_down):
        tokens, model = x_in.shape
        seq_len = tokens * n_dev
        head_dim = w_q.shape[2]
        heads = w_q.shape[1] // n_dev
        rows_own = w_q.shape[0]
        gains = gather_rows(jnp.stack([norm1_gain, norm2_gain], axis=1))
        g1_full, g2_full = gains[:, 0].astype(F32), gains[:, 1].astype(F32)
        pos_all = gather_rows(positions)
        cos_tab, sin_tab = rope_tables(pos_all, head_dim)
        x_all = gather_rows(x_in)
        wo_all = gather_rows(w_o.reshape(-1, model))
        dout_all = gather_rows(d_out)
        to_cols = lambda w: w.transpose(1, 2, 0).reshape(n_dev, -1, rows_own)
        qkv_rows = jnp.concatenate([to_cols(w_q), to_cols(w_k), to_cols(w_v)], axis=1)
        qkv_w = a2a(qkv_rows, split_axis=0, concat_axis=2)[0]
        w13 = jnp.stack([w_gate, w_up])
        w13 = a2a(w13, split_axis=2, concat_axis=1)
        w1, w3 = w13[0], w13[1]

        normed = norm_forward(x_all.astype(F32), g1_full).astype(BF16)
        qkv = dot(normed, qkv_w, 1, 1).astype(BF16)
        split_q, split_k = heads * head_dim, (heads + 1) * head_dim
        q_rot = rotate(qkv[:, :split_q].reshape(seq_len, heads, head_dim), cos_tab, sin_tab).astype(BF16).transpose(1, 0, 2)
        k_rot = rotate(qkv[:, split_q:split_k][:, None, :], cos_tab, sin_tab).astype(BF16)[:, 0]
        v_lin = qkv[:, split_k:]
        o_heads = attention_forward(q_rot, k_rot, v_lin)
        o_cols = o_heads.transpose(1, 0, 2).reshape(seq_len, heads * head_dim)
        o_tok = a2a(o_cols, split_axis=0, concat_axis=1)
        hidden = (x_in.astype(F32) + dot(o_tok, wo_all, 1, 0)).astype(BF16)
        hidden_f32 = hidden.astype(F32)
        mlp_pre, norm2_pull = jax.vjp(norm_forward, hidden_f32, g2_full)
        mlp_in = gather_rows(mlp_pre.astype(BF16))
        gate_act = dot(mlp_in, w1, 1, 0).astype(BF16)
        up_act = dot(mlp_in, w3, 1, 0).astype(BF16)
        glu_pre, glu_pull = jax.vjp(lambda g, u: jax.nn.silu(g) * u, gate_act.astype(F32), up_act.astype(F32))
        glu_out = glu_pre.astype(BF16)
        y_out = (hidden_f32 + scatter_rows(dot(glu_out, w_down, 1, 0))).astype(BF16)

        d_down = dot(glu_out, dout_all, 0, 0)
        d_glu = dot(dout_all, w_down, 1, 1).astype(BF16)
        d_gate_f, d_up_f = glu_pull(d_glu.astype(F32))
        d_gate_act, d_up_act = d_gate_f.astype(BF16), d_up_f.astype(BF16)
        d_w13 = jnp.stack([dot(mlp_in, d_gate_act, 0, 0), dot(mlp_in, d_up_act, 0, 0)])
        d_w13 = a2a(d_w13, split_axis=1, concat_axis=2)
        d_mlp = scatter_rows(dot(d_gate_act, w1, 1, 1) + dot(d_up_act, w3, 1, 1)).astype(BF16)
        d_hidden_norm, d_g2 = norm2_pull(d_mlp.astype(F32))
        d_hidden = (d_out.astype(F32) + d_hidden_norm).astype(BF16)
        dh_all = gather_rows(d_hidden)
        wo_own = w_o.reshape(-1, model)
        d_wo = dot(o_cols, dh_all, 0, 0).reshape(w_o.shape)
        d_attn = dot(dh_all, wo_own, 1, 1).astype(BF16).reshape(seq_len, heads, head_dim).transpose(1, 0, 2)
        d_q_rot, d_k_rot, d_v = attention_backward(q_rot, k_rot, v_lin, d_attn)
        d_q = rotate(d_q_rot.transpose(1, 0, 2), cos_tab, -sin_tab).astype(BF16).reshape(seq_len, -1)
        d_k = rotate(d_k_rot[:, None, :], cos_tab, -sin_tab).astype(BF16)[:, 0]
        d_qkv = jnp.concatenate([d_q, d_k, d_v], axis=1)
        d_qkv_all = gather_rows(d_qkv.T)
        normed_own = a2a(norm_forward(x_in.astype(F32), g1_full).astype(BF16), split_axis=1, concat_axis=0)
        w_own = jnp.concatenate([to_cols(w_q), to_cols(w_k), to_cols(w_v)], axis=1).reshape(-1, rows_own)
        d_w_own = dot(d_qkv_all, normed_own, 1, 0).reshape(n_dev, -1, rows_own)
        from_cols = lambda d, w: d.reshape(w.shape[1], w.shape[2], rows_own).transpose(2, 0, 1)
        d_wq = from_cols(d_w_own[:, :split_q], w_q)
        d_wk = from_cols(d_w_own[:, split_q:split_k], w_k)
        d_wv = from_cols(d_w_own[:, split_k:], w_v)
        d_normed = a2a(dot(d_qkv_all, w_own, 0, 0).astype(BF16), split_axis=0, concat_axis=1)
        _, norm1_pull = jax.vjp(norm_forward, x_in.astype(F32), g1_full)
        d_x_norm, d_g1 = norm1_pull(d_normed.astype(F32))
        d_x = (d_hidden.astype(F32) + d_x_norm).astype(BF16)
        d_gains = scatter_rows(jnp.stack([d_g1, d_g2], axis=1))
        return (y_out, d_x, d_gains[:, 0], d_gains[:, 1], d_wq, d_wk, d_wv, d_wo, d_w13[0], d_w13[1], d_down)

    all_rows = P('sp')
    return jax.shard_map(layer_step, mesh=mesh, in_specs=(all_rows,) * 12, out_specs=(all_rows,) * 11, check_vma=False)
```

time: 2310 us -> 1140 us (0.49)
  waiting for transfers between devices: 1650 us -> 453 us
  matrix products: 395 us -> 180 us
  local copies, waits for them, and re-layouts: 31.8 us -> 159 us
  Pallas kernels: 0 us -> 69.3 us
  blocking collectives: 125 us -> 173 us
    reduce_scatter x7 -> x2, waiting for transfers between devices: 1200 us -> 197 us  [the longest x1 107 us: layer_step(): y_out = (hidden_f32 + scatter_rows(dot(glu_out, w_down, 1, 0))).astype(BF16)]
    all_gather x7 -> x6, waiting for transfers between devices: 420 us -> 53.8 us  [the longest x1 48.5 us: layer_step(): dh_all = gather_rows(d_hidden)]
    dot_general x21 -> x15, matrix products: 371 us -> 180 us  [dot(): lax.dot_general(lhs, rhs, (((lhs_dim,), (rhs_dim,)), ((), ())), preferred...]
    all_to_all x4 -> x5, waiting for transfers between devices: 22.3 us -> 181 us  [the longest x1 158 us: layer_step(): d_w13 = a2a(d_w13, split_axis=1, concat_axis=2)]
    pallas_call x0 -> x2, Pallas kernels: none -> 69.3 us  [the longest x1 48.2 us: attention_backward(): pl.pallas_call(attention_bwd_kernel, grid=(heads,), in_specs=[hs, fs, fs,...]
    all_to_all x4 -> x1, blocking collectives: 57.7 us -> 126 us  [layer_step(): w13 = a2a(w13, split_axis=2, concat_axis=1)]
    slice x0 -> x11, local copies, waits for them, and re-layouts: none -> 56.6 us  [the longest x2 24.1 us: layer_step(): d_w13[1]]
    another operation x4, local copies, waits for them, and re-layouts: 0.49 us -> 46.1 us  [the longest x1 25.1 us: layer_step(): jnp.stack([dot(mlp_in, d_gate_act, 0, 0), dot(mlp_in, d_up_act, 0, 0)])]
  transfers between devices with their start and end apart: 18 -> 14, of which waited for: 12 -> 7; matrix products, arithmetic and copies ran while one was open for 15% -> 26% of each run, Pallas kernels for 0% -> 2%
where the time goes in v1:
time: 1140 us; the launch traced here: 1130 us
  waiting for transfers between devices  453 us (40%)
  matrix products  180 us (16%)
  blocking collectives  173 us (15%)
  local copies, waits for them, and re-layouts  159 us (14%)
  Pallas kernels  69.3 us (6%)
  other arithmetic  65 us (6%)
  starting transfers between devices  17.1 us (2%)
  between operations  14.9 us (1%)
    dot_general x15, matrix products, dot(): lax.dot_general(lhs, rhs, (((lhs_dim,), (rhs_dim,)), ((), ())), preferred...  180 us
    all_to_all x1, waiting for transfers between devices, layer_step(): d_w13 = a2a(d_w13, split_axis=1, concat_axis=2)  158 us
    all_to_all x1, blocking collectives, layer_step(): w13 = a2a(w13, split_axis=2, concat_axis=1)  126 us
    reduce_scatter x1, waiting for transfers between devices, layer_step(): y_out = (hidden_f32 + scatter_rows(dot(glu_out, w_down, 1, 0))).astype(BF16)  107 us
    reduce_scatter x1, waiting for transfers between devices, layer_step(): scatter_rows(dot(d_gate_act, w1, 1, 1) + dot(d_up_act, w3, 1, 1))  90.2 us
    all_gather x1, waiting for transfers between devices, layer_step(): dh_all = gather_rows(d_hidden)  48.5 us
    pallas_call x1, Pallas kernels, attention_backward(): pl.pallas_call(attention_bwd_kernel, grid=(heads,), in_specs=[hs, fs, fs,...  48.2 us
    all_gather x1, blocking collectives, layer_step(): pos_all = gather_rows(positions)  36.5 us
  transfers between devices with their start and end apart: 14, of which 7 were waited for; matrix products, arithmetic and copies ran while one was open for 26% of the time, Pallas kernels for 2%

profile of v1, /device:TPU:0, one launch (start us, length us, event | category | flops | bytes accessed | tf_op | source)
XLA Modules:
  0.0 1131.0 jit_solution(5962261551084668313)
XLA Ops:
  16.4 36.5 %all-gather = s32[8,1,256]{2,1,0:T(1,128)S(1)} all-gather(s32[1,1,256]{2,1,0:T(1,128)S(1)} %bitcast.168), channel_id=1, replica_groups=mesh['sp'=8] {'sp'}, dimensions={0}, use_global_device_ids=true | all-gather | bytes 9216 | tf_op jit(solution)/shard_map/all_gather | solution.py:131
  53.0 10.9 all_gather.25
  109.4 21.1 %attn_fwd.1 = bf16[4,2048,64]{2,1,0:T(8,128)(2,1)} custom-call(bf16[4,2048,64]{2,1,0:T(8,128)(2,1)} %maximum_bitcast_fusion.q_ref, bf16[2048,64]{1,0:T(8,128)(2,1)} %pad_maximum_fusion.4.k_ref, bf16[2048,64]{1,0:T(8,128)(2,1)} %get-tuple-element.31.v_ref), custom_call_target="tpu_custom_call" | custom-call | flops 4294967296 | bytes 4194304 | tf_op jit(solution)/shard_map/attn_fwd/pallas_call | solution.py:97
  136.4 23.1 %all-to-all-done.1 = bf16[8,256,256]{1,2,0:T(8,128)(2,1)S(1)} async-done(((bf16[8,256,256]{1,2,0:T(8,128)(2,1)}), bf16[8,256,256]{1,2,0:T(8,128)(2,1)S(1)}, u32[]{:S(2)}, u32[]{:S(2)}) %all-to-all-start.1) | async-done | bytes 1048608 | tf_op jit(solution)/shard_map/all_to_all | solution.py:151
  167.7 7.6 pad_maximum_fusion.1
  175.3 21.0 %copy.125 = bf16[2,256,8192]{1,0,2:T(2,128)(2,1)} copy(bf16[2,256,8192]{2,1,0:T(8,128)(2,1)} %pad_maximum_fusion.1) | data formatting | bytes 16777216 | tf_op jit(solution)/shard_map/stack | solution.py:139
  196.4 125.9 %all_to_all.96 = bf16[2,256,8192]{1,0,2:T(2,128)(2,1)} all-to-all(bf16[2,256,8192]{1,0,2:T(2,128)(2,1)} %copy.125), channel_id=1, replica_groups=mesh['sp'=8] {'sp'}, dimensions={2} | all-to-all | bytes 16777216 | tf_op jit(solution)/shard_map/all_to_all | solution.py:140
  322.3 7.9 copy.126
  348.8 14.0 %convolution_convert_fusion = bf16[2048,1024]{1,0:T(8,128)(2,1)} fusion(bf16[2048,2048]{1,0:T(8,128)(2,1)} %all-gather.14.cloned.1.call-done, bf16[1024,2048]{1,0:T(8,128)(2,1)} %param.23), kind=kOutput, calls=%fused_computation.54 | convolution fusion | flops 8592031744 | bytes 16777216 | tf_op jit(solution)/shard_map/dot_general | solution.py:18
  362.9 12.6 %convolution_convert_fusion.2 = bf16[2048,1024]{1,0:T(8,128)(2,1)S(1)} fusion(bf16[2048,2048]{1,0:T(8,128)(2,1)} %all-gather.12.cloned.1.call-done, bf16[2048,1024]{1,0:T(8,128)(2,1)} %bitcast.134), kind=kOutput, calls=%fused_computation.56 | convolution fusion | flops 8592031744 | bytes 16777216 | tf_op jit(solution)/shard_map/dot_general | solution.py:18
  375.5 10.6 convolution_convert_fusion.1
  386.1 16.1 %fusion.78 = f32[2048,2048]{1,0:T(8,128)} fusion(bf16[2048,1024]{1,0:T(8,128)(2,1)S(1)} %bitcast.135, bf16[2048,1024]{1,0:T(8,128)(2,1)S(1)} %convolution_convert_fusion.2, bf16[2048,1024]{1,0:T(8,128)(2,1)} %convolution_convert_fusion.1, bf16[2048,1024]{1,0:T(8,128)(2,1)S(1)} %copy-done.36), kind=kOutput, calls=%fused_computation.134 | convolution fusion | flops 8619294720 | bytes 33554432 | tf_op jit(solution)/shard_map/dot_general | solution.py:18
  402.2 20.7 %convolution_add_fusion = f32[2048,2048]{1,0:T(8,128)} fusion(f32[2048,2048]{1,0:T(8,128)} %fusion.78, bf16[2048,1024]{1,0:T(8,128)(2,1)} %bitcast.136, bf16[2048,1024]{1,0:T(8,128)(2,1)} %convolution_convert_fusion, bf16[2048,1024]{1,0:T(8,128)(2,1)} %copy-done.34), kind=kOutput, calls=%fused_computation.27 | convolution fusion | flops 8610906112 | bytes 46137344 | tf_op jit(solution)/shard_map/dot_general | solution.py:18
  422.9 16.4 %fusion.75 = f32[2048,2048]{1,0:T(8,128)} fusion(bf16[1024,2048]{1,0:T(8,128)(2,1)} %param.23, bf16[2048,1024]{1,0:T(8,128)(2,1)} %convolution_convert_fusion.1, bf16[2048,1024]{1,0:T(8,128)(2,1)} %copy-done.34), kind=kOutput, calls=%fused_computation.133 | convolution fusion | flops 8606711808 | bytes 29360128 | tf_op jit(solution)/shard_map/dot_general | solution.py:18
  439.4 90.2 %reduce-scatter.8.cloned.1.call-done = f32[256,2048]{1,0:T(8,128)} async-done(((f32[2048,2048]{1,0:T(8,128)}), f32[256,2048]{1,0:T(8,128)}) %reduce-scatter.8.cloned.1.call-update) | async-done | bytes 2097168 | tf_op jit(solution)/shard_map/reduce_scatter | solution.py:168
  532.6 107.3 %reduce-scatter.6.cloned.1.call-done = f32[256,2048]{1,0:T(8,128)} async-done(((f32[2048,2048]{1,0:T(8,128)}), f32[256,2048]{1,0:T(8,128)}) %reduce-scatter.6.cloned.1.call-update) | async-done | bytes 2097168 | tf_op jit(solution)/shard_map/reduce_scatter | solution.py:160
  644.1 48.5 %all-gather.16.cloned.1.call-done = bf16[2048,2048]{1,0:T(8,128)(2,1)} async-done(((bf16[256,2048]{1,0:T(8,128)(2,1)}), bf16[2048,2048]{1,0:T(8,128)(2,1)}) %all-gather.16.cloned.1.call-update) | async-done | bytes 8388624 | tf_op jit(solution)/shard_map/all_gather | solution.py:171
  700.7 48.2 %attn_bwd.1 = (bf16[4,2048,64]{2,1,0:T(8,128)(2,1)}, bf16[2048,64]{1,0:T(8,128)(2,1)}, bf16[2048,64]{1,0:T(8,128)(2,1)}) custom-call(bf16[4,2048,64]{2,1,0:T(8,128)(2,1)} %maximum_bitcast_fusion.q_ref, bf16[2048,64]{1,0:T(8,128)(2,1)} %pad_maximum_fusion.4.k_ref, bf16[2048,64]{1,0:T(8,128)(2,1)} %get-tuple-element.31.v_ref, bf16[4,2048,64]{2,1,0:T(8,128)(2,1)} %bitcast.144), custom_call_target="tpu_custom_call" | custom-call | flops 10737418240 | bytes 4194304 | tf_op jit(solution)/shard_map/attn_bwd/pallas_call | solution.py:109
  750.3 7.4 fusion.67
  767.8 17.6 %convolution_bitcast_fusion.1 = f32[1,2048,1024]{2,1,0:T(8,128)} fusion(bf16[2048,2048]{1,0:T(8,128)(2,1)} %all-gather.12.cloned.1.call-done, bf16[2048,1024]{1,0:T(8,128)(2,1)} %copy-done.34, bf16[2048,1024]{1,0:T(8,128)(2,1)} %convolution_convert_fusion.1, bf16[2048,1024]{1,0:T(8,128)(2,1)} %convolution_convert_fusion), kind=kOutput, calls=%fused_computation.35 | convolution fusion | flops 8619294720 | bytes 29360128 | tf_op jit(solution)/shard_map/dot_general | solution.py:18
  785.4 14.2 %convolution_bitcast_fusion = f32[1,2048,1024]{2,1,0:T(8,128)} fusion(bf16[2048,2048]{1,0:T(8,128)(2,1)} %all-gather.12.cloned.1.call-done, bf16[2048,1024]{1,0:T(8,128)(2,1)S(1)} %copy-done.37, bf16[2048,1024]{1,0:T(8,128)(2,1)S(1)} %copy-done.35), kind=kOutput, calls=%fused_computation.34 | convolution fusion | flops 8606711808 | bytes 25165824 | tf_op jit(solution)/shard_map/dot_general | solution.py:18
  799.6 6.6 pad_maximum_fusion
  806.2 25.1 %copy.137 = f32[2,2048,1024]{2,0,1:T(2,128)} copy(f32[2,2048,1024]{2,1,0:T(8,128)S(1)} %pad_maximum_fusion) | data formatting | bytes 33554432 | tf_op jit(solution)/shard_map/stack | solution.py:166
  836.7 16.2 %fusion.73 = f32[1024,2048]{1,0:T(8,128)} fusion(bf16[2048,2048]{1,0:T(8,128)(2,1)} %all-gather.14.cloned.1.call-done, bf16[2048,1024]{1,0:T(8,128)(2,1)} %convolution_convert_fusion.1, bf16[2048,1024]{1,0:T(8,128)(2,1)} %copy-done.34), kind=kOutput, calls=%fused_computation.132 | convolution fusion | flops 8606711808 | bytes 25165824 | tf_op jit(solution)/shard_map/dot_general | solution.py:18
  852.9 9.7 convolution_convert_fusion.3
  862.5 157.8 %all-to-all-done.5 = f32[2,2048,1024]{2,0,1:T(2,128)} async-done(((f32[2,2048,1024]{2,0,1:T(2,128)}), f32[2,2048,1024]{2,0,1:T(2,128)}, u32[]{:S(2)}, u32[]{:S(2)}) %all-to-all-start.5) | async-done | bytes 16777248 | tf_op jit(solution)/shard_map/all_to_all | solution.py:167
  1022.7 19.3 %fusion.80 = (f32[1,256,8,1024]{3,0,1,2:T(1,128)S(1)}, f32[1,256,8,1024]{3,0,1,2:T(1,128)}) fusion(f32[2,256,8,1024]{3,0,1,2:T(2,128)} %bitcast.57), kind=kLoop, calls=%fused_computation.135 | loop fusion | bytes 33554432 | tf_op jit(solution)/shard_map/slice | solution.py:192
  1041.9 8.2 copy.138
  1050.2 11.2 copy.149
  1066.2 11.2 copy.150
  1087.1 7.0 fusion.13
  1094.2 18.4 %reduce-scatter.10.cloned.1.call-done = f32[256,2]{1,0:T(8,128)} async-done(((f32[2048,2]{1,0:T(8,128)}), f32[256,2]{1,0:T(8,128)}) %reduce-scatter.10.cloned.1.call-update) | async-done | bytes 2064
  (167 shorter events, 147.8 us)
Async XLA Ops:
  7.2 69.2 %all-gather.8.cloned.1.call-start = ((), (), s32[]{:S(2)}) async-start(), calls=%async_computation.9 | async-start | bytes 9437184 | tf_op jit(solution)/shard_map/all_gather | solution.py:133
  7.9 128.5 %all-gather.10.cloned.1.call-start = ((), (), s32[]{:S(2)}) async-start(), calls=%async_computation.10 | async-start | bytes 9437184 | tf_op jit(solution)/shard_map/all_gather | solution.py:134
  8.7 340.2 %all-gather.14.cloned.1.call-start = ((), (), s32[]{:S(2)}) async-start(), calls=%async_computation.13 | async-start | bytes 9437184 | tf_op jit(solution)/shard_map/all_gather | solution.py:135
  12.1 57.4 %all-to-all-start = ((bf16[8,384,256]{2,1,0:T(8,128)(2,1)}), bf16[8,384,256]{2,1,0:T(8,128)(2,1)S(1)}, u32[]{:S(2)}, u32[]{:S(2)}) async-start(bf16[8,384,256]{2,1,0:T(8,128)(2,1)} %pad_maximum_fusion.3), calls=%async_computation | async-start | bytes 3145728 | tf_op jit(solution)/shard_map/all_to_all | solution.py:138
  52.9 46.6 %copy-start.17 = (f32[8,1,256]{2,1,0:T(1,128)}, f32[8,1,256]{2,1,0:T(1,128)S(1)}, u32[]{:S(2)}) copy-start(f32[8,1,256]{2,1,0:T(1,128)S(1)} %convert_element_type.197) | copy-start | bytes 24580
  63.8 35.6 %copy-start.28 = (f32[32]{0:T(128)}, f32[32]{0:T(128)S(1)}, u32[]{:S(2)}) copy-start(f32[32]{0:T(128)S(1)} %negate_power_fusion) | copy-start | bytes 388
  63.9 17.7 %copy-start.21 = (f32[2048,1]{0,1:T(1,128)}, f32[2048,1]{0,1:T(1,128)S(1)}, u32[]{:S(2)}) copy-start(f32[2048,1]{0,1:T(1,128)S(1)} %get-tuple-element.49) | copy-start | bytes 24580
  63.9 101.5 %copy-start.19 = (f32[2048,1]{0,1:T(1,128)}, f32[2048,1]{0,1:T(1,128)S(1)}, u32[]{:S(2)}) copy-start(f32[2048,1]{0,1:T(1,128)S(1)} %get-tuple-element.48) | copy-start | bytes 24580
  69.5 36.2 %copy-start.5 = (f32[2048,32]{1,0:T(8,128)}, f32[2048,32]{1,0:T(8,128)S(1)}, u32[]{:S(2)}) copy-start(f32[2048,32]{1,0:T(8,128)S(1)} %get-tuple-element.47) | copy-start | bytes 786436
  130.5 29.0 %copy-start = (bf16[256,2048]{1,0:T(8,128)(2,1)S(1)}, bf16[256,2048]{1,0:T(8,128)(2,1)}, u32[]{:S(2)}) copy-start(bf16[256,2048]{1,0:T(8,128)(2,1)} %param.12) | copy-start | bytes 3145732
  134.0 25.5 %all-to-all-start.1 = ((bf16[8,256,256]{1,2,0:T(8,128)(2,1)}), bf16[8,256,256]{1,2,0:T(8,128)(2,1)S(1)}, u32[]{:S(2)}, u32[]{:S(2)}) async-start(bf16[8,256,256]{1,2,0:T(8,128)(2,1)} %copy.124), calls=%async_computation.1 | async-start | bytes 2097152 | tf_op jit(solution)/shard_map/all_to_all | solution.py:151
  136.3 226.5 %all-gather.12.cloned.1.call-start = ((), (), s32[]{:S(2)}) async-start(), calls=%async_computation.11 | async-start | bytes 9437184 | tf_op jit(solution)/shard_map/all_gather | solution.py:155
  167.7 361.9 %reduce-scatter.8.cloned.1.call-start = ((), (), s32[]{:S(2)}) async-start(), calls=%async_computation.14 | async-start | bytes 18874368 | tf_op jit(solution)/shard_map/reduce_scatter | solution.py:168
  362.9 12.6 %copy-start.15 = (bf16[1,8,256,1024]{3,2,1,0:T(8,128)(2,1)S(1)}, bf16[1,8,256,1024]{3,2,1,0:T(8,128)(2,1)}, u32[]{:S(2)}) copy-start(bf16[1,8,256,1024]{3,2,1,0:T(8,128)(2,1)} %copy.128) | copy-start | bytes 12582916
  362.9 12.6 %copy-start.31 = (bf16[2048,2048]{1,0:T(8,128)(2,1)S(1)}, bf16[2048,2048]{1,0:T(8,128)(2,1)}, u32[]{:S(2)}) copy-start(bf16[2048,2048]{1,0:T(8,128)(2,1)} %all-gather.12.cloned.1.call-done) | copy-start | bytes 25165828
  422.9 217.0 %reduce-scatter.6.cloned.1.call-start = ((), (), s32[]{:S(2)}) async-start(), calls=%async_computation.12 | async-start | bytes 18874368 | tf_op jit(solution)/shard_map/reduce_scatter | solution.py:160
  439.3 90.3 %copy-start.4 = (bf16[256,2048]{1,0:T(8,128)(2,1)S(1)}, bf16[256,2048]{1,0:T(8,128)(2,1)}, u32[]{:S(2)}) copy-start(bf16[256,2048]{1,0:T(8,128)(2,1)} %copy-done.3) | copy-start | bytes 3145732
  439.3 90.3 %copy-start.20 = (f32[2048,1]{0,1:T(1,128)S(1)}, f32[2048,1]{0,1:T(1,128)}, u32[]{:S(2)}) copy-start(f32[2048,1]{0,1:T(1,128)} %copy-done.19) | copy-start | bytes 24580
  439.3 90.3 %copy-start.25 = (f32[256]{0:T(256)S(1)}, f32[256]{0:T(256)}, u32[]{:S(2)}) copy-start(f32[256]{0:T(256)} %copy-done.24) | copy-start | bytes 3076
  439.3 93.3 %copy-start.27 = (f32[256]{0:T(256)S(1)}, f32[256]{0:T(256)}, u32[]{:S(2)}) copy-start(f32[256]{0:T(256)} %copy-done.26) | copy-start | bytes 3076
  439.3 253.2 %all-gather.16.cloned.1.call-start = ((), (), s32[]{:S(2)}) async-start(), calls=%async_computation.15 | async-start | bytes 9437184 | tf_op jit(solution)/shard_map/all_gather | solution.py:171
  529.6 110.3 %copy-start.10 = (f32[256,2048]{1,0:T(8,128)S(1)}, f32[256,2048]{1,0:T(8,128)}, u32[]{:S(2)}) copy-start(f32[256,2048]{1,0:T(8,128)} %reduce-scatter.8.cloned.1.call-done) | copy-start | bytes 6291460
  644.0 208.9 %all-gather.18.cloned.1.call-start = ((), (), s32[]{:S(2)}) async-start(), calls=%async_computation.16 | async-start | bytes 14155776 | tf_op jit(solution)/shard_map/all_gather | solution.py:179
  700.7 49.6 %copy-start.18 = (f32[8,1,256]{2,1,0:T(1,128)S(1)}, f32[8,1,256]{2,1,0:T(1,128)}, u32[]{:S(2)}) copy-start(f32[8,1,256]{2,1,0:T(1,128)} %copy-done.17) | copy-start | bytes 24580
  700.7 49.6 %copy-start.29 = (f32[32]{0:T(128)S(1)}, f32[32]{0:T(128)}, u32[]{:S(2)}) copy-start(f32[32]{0:T(128)} %copy-done.28) | copy-start | bytes 388
  748.8 12.0 %copy-start.6 = (f32[2048,32]{1,0:T(8,128)S(1)}, f32[2048,32]{1,0:T(8,128)}, u32[]{:S(2)}) copy-start(f32[2048,32]{1,0:T(8,128)} %copy-done.5) | copy-start | bytes 786436
  767.8 17.6 %copy-start.35 = (bf16[2048,1024]{1,0:T(8,128)(2,1)S(1)}, bf16[2048,1024]{1,0:T(8,128)(2,1)}, u32[]{:S(2)}) copy-start(bf16[2048,1024]{1,0:T(8,128)(2,1)} %copy-done.34) | copy-start | bytes 12582916
  767.8 17.6 %copy-start.37 = (bf16[2048,1024]{1,0:T(8,128)(2,1)S(1)}, bf16[2048,1024]{1,0:T(8,128)(2,1)}, u32[]{:S(2)}) copy-start(bf16[2048,1024]{1,0:T(8,128)(2,1)} %convolution_convert_fusion) | copy-start | bytes 12582916
  831.3 189.0 %all-to-all-start.5 = ((f32[2,2048,1024]{2,0,1:T(2,128)}), f32[2,2048,1024]{2,0,1:T(2,128)}, u32[]{:S(2)}, u32[]{:S(2)}) async-start(f32[2,2048,1024]{2,0,1:T(2,128)} %copy.137), calls=%async_computation.7 | async-start | bytes 33554432 | tf_op jit(solution)/shard_map/all_to_all | solution.py:167
  1020.3 57.1 %all-to-all-start.3 = ((bf16[8,256,256]{2,1,0:T(8,128)(2,1)}), bf16[8,256,256]{2,1,0:T(8,128)(2,1)S(1)}, u32[]{:S(2)}, u32[]{:S(2)}) async-start(bf16[8,256,256]{2,1,0:T(8,128)(2,1)} %bitcast.36), calls=%async_computation.5 | async-start | bytes 2097152 | tf_op jit(solution)/shard_map/all_to_all | solution.py:187
  1022.6 90.0 %reduce-scatter.10.cloned.1.call-start = ((), (), s32[]{:S(2)}) async-start(), calls=%async_computation.17 | async-start | bytes 1179648
  1084.3 30.6 %all-to-all-start.4 = ((bf16[256,8,256]{2,0,1:T(8,128)(2,1)}), bf16[256,8,256]{2,0,1:T(8,128)(2,1)S(1)}, u32[]{:S(2)}, u32[]{:S(2)}) async-start(bf16[256,8,256]{2,0,1:T(8,128)(2,1)} %bitcast.121), calls=%async_computation.6 | async-start | bytes 2097152 | tf_op jit(solution)/shard_map/all_to_all | solution.py:180
  (20 other events, 122.6 us)
Sparse Core Ops, SparseCore 0:
  9.8 66.5 all-gather.7
  78.2 48.3 all-gather.9
  128.4 59.5 all-gather.13
  190.3 106.5 all-gather.11
  423.0 106.5 reduce-scatter.7
  532.9 106.9 reduce-scatter.5
  644.1 48.3 all-gather.15
  767.9 66.2 all-gather.17
  1083.3 29.2 reduce-scatter.9

commit v2 on v1

--- a/solution.py
+++ b/solution.py
@@ -112,6 +112,230 @@
         scratch_shapes=[pltpu.VMEM((seq_len, head_dim), F32), pltpu.VMEM((seq_len, head_dim), F32)],
         cost_estimate=pl.CostEstimate(flops=flops, bytes_accessed=8 * heads * seq_len * head_dim, transcendentals=heads * seq_len * seq_len // 2),
     )(q_heads, keys, values, d_attn)
+
+
+MESH = pl.DeviceIdType.MESH
+
+
+def place(axis):
+    me = lax.axis_index(axis)
+    core = lax.rem(me, 2)
+    col = lax.rem(lax.div(me, 2), 2)
+    row = lax.div(me, 4)
+
+    def other(flip_core, flip_col, flip_row):
+        pick = lambda v, f: 1 - v if f else v
+        return pick(row, flip_row) * 4 + pick(col, flip_col) * 2 + pick(core, flip_core)
+
+    nbr_x, nbr_y = other(0, 1, 0), other(0, 0, 1)
+    first = nbr_x * (1 - core) + nbr_y * core
+    second = nbr_y * (1 - core) + nbr_x * core
+    return me, other, first, second
+
+
+def greet(other):
+    barrier = pltpu.get_barrier_semaphore()
+    for r in range(1, 8):
+        pl.semaphore_signal(barrier, inc=1, device_id=(other(r & 1, (r >> 1) & 1, r >> 2),), device_id_type=MESH)
+    pl.semaphore_wait(barrier, 7)
+
+
+class Gather:
+    def __init__(self, slot, send_sem, recv_sem, where, own=None):
+        me, other, first, second = where
+        partner, diag = other(1, 0, 0), other(0, 1, 1)
+        own = slot(me) if own is None else own
+        self.copies = []
+        plan = [(own, me, first), (own, me, second), (own, me, partner), (slot(first), first, second),
+                (slot(first), first, partner), (slot(second), second, partner), (slot(diag), diag, partner)]
+        for i, (src, what, dest) in enumerate(plan):
+            self.copies.append(pltpu.make_async_remote_copy(
+                src_ref=src, dst_ref=slot(what), send_sem=send_sem.at[i], recv_sem=recv_sem.at[i],
+                device_id=(dest,), device_id_type=MESH))
+
+    def start(self):
+        for i in range(3):
+            self.copies[i].start()
+
+    def got_first(self):
+        self.copies[0].wait_recv()
+        self.copies[3].start()
+        self.copies[4].start()
+
+    def got_second(self):
+        self.copies[1].wait_recv()
+        self.copies[5].start()
+
+    def got_diag(self):
+        self.copies[3].wait_recv()
+        self.copies[6].start()
+
+    def got_partner(self, i):
+        self.copies[(2, 4, 5, 6)[i]].wait_recv()
+
+    def drain(self):
+        for copy in self.copies:
+            copy.wait_send()
+
+
+def turn_halves(values, cos_blk, sin_blk):
+    width = values.shape[1]
+    lanes = lax.broadcasted_iota(jnp.int32, values.shape, 1)
+    partner = jnp.where(lax.rem(lanes, 64) < 32, pltpu.roll(values, width - 32, 1), pltpu.roll(values, 32, 1))
+    return values * cos_blk + partner * sin_blk
+
+
+def norm_backward(hidden, gain, d_out):
+    inv = lax.rsqrt(jnp.mean(hidden * hidden, axis=-1, keepdims=True) + NORM_EPS)
+    d_scaled = d_out * gain
+    d_hidden = d_scaled * inv - hidden * (inv * inv * inv * jnp.mean(d_scaled * hidden, axis=-1, keepdims=True))
+    return d_hidden, jnp.sum(d_out * (hidden * inv), axis=0, keepdims=True)
+
+
+def attn_bwd_comm_kernel(axis, heads, dh_ref, wo_ref, ot_ref, q_ref, k_ref, v_ref, cos_ref, sin_ref, cosk_ref, sink_ref,
+                         dw1_ref, dw3_ref, wown_ref, ut_ref, x_ref, g1_ref,
+                         dwo_ref, dwq_ref, dwk_ref, dwv_ref, out1_ref, out3_ref, dx_ref, dg1_ref,
+                         slots, do_scr, dk_acc, dv_acc, du_acc, du_scr, du_recv, stage,
+                         bulk_send, bulk_recv, gat_send, gat_recv, du_send, du_rsem, loc_sem):
+    where = place(axis)
+    me, other, first, second = where
+    greet(other)
+    seq_len, head_dim = k_ref.shape
+    rows_own, hid = stage.shape[1], stage.shape[2]
+    tokens = x_ref.shape[0]
+    qw = heads * head_dim
+
+    rows_of = lambda d: pl.ds(pl.multiple_of(d * rows_own, rows_own), rows_own)
+    hid_of = lambda d: pl.ds(pl.multiple_of(d * hid, hid), hid)
+    bulk = []
+    for n, r in enumerate((2, 4, 6, 3, 5, 7, 1)):
+        dest = other(r & 1, (r >> 1) & 1, r >> 2)
+        for i, (src, dst) in enumerate(((dw1_ref, out1_ref), (dw3_ref, out3_ref))):
+            bulk.append(pltpu.make_async_remote_copy(
+                src_ref=src.at[rows_of(dest), :], dst_ref=dst.at[:, hid_of(me)], send_sem=bulk_send.at[2 * n + i],
+                recv_sem=bulk_recv.at[2 * n + i], device_id=(dest,), device_id_type=MESH))
+            bulk[-1].start()
+    for i, src in enumerate((dw1_ref, dw3_ref)):
+        pltpu.make_async_copy(src.at[rows_of(me), :], stage.at[i], loc_sem.at[i]).start()
+
+    for start in range(0, seq_len, BLK):
+        rows = pl.ds(start, BLK)
+        do_blk = dot(dh_ref[rows, :], wo_ref[...], 1, 1).astype(BF16)
+        for h in range(heads):
+            do_scr[h, rows, :] = do_blk[:, h * head_dim:(h + 1) * head_dim]
+    for start in range(0, dwo_ref.shape[1], 512):
+        cols = pl.ds(start, 512)
+        dwo_ref[:, cols] = dot(ot_ref[...], dh_ref[:, cols], 1, 0)
+
+    for i, (src, dst) in enumerate(((dw1_ref, out1_ref), (dw3_ref, out3_ref))):
+        pltpu.make_async_copy(src.at[rows_of(me), :], stage.at[i], loc_sem.at[i]).wait()
+        pltpu.make_async_copy(stage.at[i], dst.at[:, hid_of(me)], loc_sem.at[2 + i]).start()
+
+    dk_acc[...] = jnp.zeros_like(dk_acc)
+    dv_acc[...] = jnp.zeros_like(dv_acc)
+    mine = slots.at[me]
+    for h in range(heads):
+        def one_block(start):
+            keys = pl.ds(0, start + BLK)
+            rows = pl.ds(start, BLK)
+            q_blk, do_blk = q_ref[h, rows, :], do_scr[h, rows, :]
+            probs = probs_transposed(k_ref[keys, :], q_blk, start)
+            d_probs = dot(v_ref[keys, :], do_blk, 1, 1).astype(BF16).astype(F32)
+            row_dot = jnp.sum(d_probs * probs, axis=0, keepdims=True)
+            d_scores = (probs * (d_probs - row_dot) * (head_dim ** -0.5)).astype(BF16)
+            mine[rows, h * head_dim:(h + 1) * head_dim] = dot(d_scores, k_ref[keys, :], 0, 0).astype(BF16)
+            dk_acc[keys, :] += dot(d_scores, q_blk, 1, 0)
+            dv_acc[keys, :] += dot(probs.astype(BF16), do_blk, 1, 0)
+        for start in range(0, seq_len, BLK):
+            one_block(start)
+    mine[:, qw:qw + head_dim] = dk_acc[...].astype(BF16)
+    mine[:, qw + head_dim:] = dv_acc[...].astype(BF16)
+    for start in range(0, seq_len, BLK):
+        rows = pl.ds(start, BLK)
+        for h in range(0, qw, 128):
+            cols = pl.ds(h, 128)
+            mine[rows, cols] = turn_halves(mine[rows, cols].astype(F32), cos_ref[rows, :], -sin_ref[rows, :]).astype(BF16)
+        cols = pl.ds(qw, 128)
+        mine[rows, cols] = turn_halves(mine[rows, cols].astype(F32), cosk_ref[rows, :], -sink_ref[rows, :]).astype(BF16)
+
+    gather = Gather(lambda d: slots.at[d], gat_send, gat_recv, where)
+    gather.start()
+    du_acc[...] = jnp.zeros_like(du_acc)
+
+    def use(d):
+        kv_rows = pl.ds(pl.multiple_of(d * head_dim, head_dim), head_dim)
+        w_rows = pl.ds(pl.multiple_of(d * 384, 384), 384)
+        for start in range(0, seq_len, 512):
+            rows = pl.ds(start, 512)
+            du_acc[rows, :] += dot(slots[d, rows, :], wown_ref[w_rows, :], 1, 0)
+        d_w = dot(ut_ref[...], slots[d], 1, 0).T
+        dwq_ref[pl.ds(pl.multiple_of(d * qw, qw), qw), :] = d_w[:qw]
+        dwk_ref[kv_rows, :] = d_w[qw:qw + head_dim]
+        dwv_ref[kv_rows, :] = d_w[qw + head_dim:]
+
+    partner = other(1, 0, 0)
+    use(me)
+    gather.got_first()
+    gather.got_second()
+    use(first)
+    use(second)
+    gather.got_partner(0)
+    use(partner)
+    gather.got_diag()
+    use(other(0, 1, 1))
+    gather.got_partner(1)
+    gather.got_partner(2)
+    use(other(1, 1, 0))
+    use(other(1, 0, 1))
+    gather.got_partner(3)
+    use(other(1, 1, 1))
+    du_scr[...] = du_acc[...].astype(BF16)
+
+    tok_of = lambda d: pl.ds(pl.multiple_of(d * tokens, tokens), tokens)
+    sends = []
+    for n, r in enumerate((6, 7, 2, 4, 3, 5, 1)):
+        dest = other(r & 1, (r >> 1) & 1, r >> 2)
+        sends.append(pltpu.make_async_remote_copy(
+            src_ref=du_scr.at[tok_of(dest), :], dst_ref=du_recv.at[:, rows_of(me)], send_sem=du_send.at[n],
+            recv_sem=du_rsem.at[n], device_id=(dest,), device_id_type=MESH))
+        sends[-1].start()
+    du_recv[:, rows_of(me)] = du_scr[tok_of(me), :]
+    for copy in sends:
+        copy.wait_recv()
+    d_norm, d_gain = norm_backward(x_ref[...].astype(F32), g1_ref[...], du_recv[...].astype(F32))
+    dx_ref[...] = (dh_ref[tok_of(me), :].astype(F32) + d_norm).astype(BF16)
+    dg1_ref[...] = d_gain
+    for copy in sends:
+        copy.wait_send()
+    gather.drain()
+    for copy in bulk:
+        copy.wait()
+    for i, dst in enumerate((out1_ref, out3_ref)):
+        pltpu.make_async_copy(stage.at[i], dst.at[:, hid_of(me)], loc_sem.at[2 + i]).wait()
+
+
+def attention_backward_step(heads, dh_all, wo_own, o_t, q_rot, k_rot, v_lin, tables, d_w1, d_w3, w_own, u_t, x_in, g1):
+    seq_len, model = dh_all.shape
+    head_dim = k_rot.shape[1]
+    tokens = x_in.shape[0]
+    rows_own, hid = model // 8, d_w1.shape[1]
+    shape = jax.ShapeDtypeStruct
+    vmem, hbm = pl.BlockSpec(memory_space=pltpu.VMEM), pl.BlockSpec(memory_space=pl.ANY)
+    dma = pltpu.SemaphoreType.DMA
+    return pl.pallas_call(
+        functools.partial(attn_bwd_comm_kernel, 'sp', heads), name='attn_bwd_comm',
+        in_specs=[vmem] * 10 + [hbm] * 2 + [vmem] * 4,
+        out_specs=[vmem] * 4 + [hbm] * 2 + [vmem] * 2,
+        out_shape=[shape(wo_own.shape, F32), shape((8 * heads * head_dim, rows_own), F32), shape((8 * head_dim, rows_own), F32),
+                   shape((8 * head_dim, rows_own), F32), shape((rows_own, 8 * hid), F32), shape((rows_own, 8 * hid), F32),
+                   shape(x_in.shape, BF16), shape((1, model), F32)],
+        scratch_shapes=[pltpu.VMEM((8, seq_len, 384), BF16), pltpu.VMEM((heads, seq_len, head_dim), BF16),
+                        pltpu.VMEM((seq_len, head_dim), F32), pltpu.VMEM((seq_len, head_dim), F32),
+                        pltpu.VMEM((seq_len, rows_own), F32), pltpu.VMEM((seq_len, rows_own), BF16),
+                        pltpu.VMEM((tokens, model), BF16), pltpu.VMEM((2, rows_own, hid), F32),
+                        dma((14,)), dma((14,)), dma((7,)), dma((7,)), dma((7,)), dma((7,)), dma((4,))],
+        compiler_params=pltpu.CompilerParams(collective_id=2, has_side_effects=True, vmem_limit_bytes=63 * 1024 * 1024),
+    )(dh_all, wo_own, o_t, q_rot, k_rot, v_lin, *tables, d_w1, d_w3, w_own, u_t, x_in, g1)
 
 
 def solution(mesh):
@@ -163,33 +387,25 @@
         d_glu = dot(dout_all, w_down, 1, 1).astype(BF16)
         d_gate_f, d_up_f = glu_pull(d_glu.astype(F32))
         d_gate_act, d_up_act = d_gate_f.astype(BF16), d_up_f.astype(BF16)
-        d_w13 = jnp.stack([dot(mlp_in, d_gate_act, 0, 0), dot(mlp_in, d_up_act, 0, 0)])
-        d_w13 = a2a(d_w13, split_axis=1, concat_axis=2)
+        d_w1s, d_w3s = dot(mlp_in, d_gate_act, 0, 0), dot(mlp_in, d_up_act, 0, 0)
         d_mlp = scatter_rows(dot(d_gate_act, w1, 1, 1) + dot(d_up_act, w3, 1, 1)).astype(BF16)
         d_hidden_norm, d_g2 = norm2_pull(d_mlp.astype(F32))
         d_hidden = (d_out.astype(F32) + d_hidden_norm).astype(BF16)
         dh_all = gather_rows(d_hidden)
-        wo_own = w_o.reshape(-1, model)
-        d_wo = dot(o_cols, dh_all, 0, 0).reshape(w_o.shape)
-        d_attn = dot(dh_all, wo_own, 1, 1).astype(BF16).reshape(seq_len, heads, head_dim).transpose(1, 0, 2)
-        d_q_rot, d_k_rot, d_v = attention_backward(q_rot, k_rot, v_lin, d_attn)
-        d_q = rotate(d_q_rot.transpose(1, 0, 2), cos_tab, -sin_tab).astype(BF16).reshape(seq_len, -1)
-        d_k = rotate(d_k_rot[:, None, :], cos_tab, -sin_tab).astype(BF16)[:, 0]
-        d_qkv = jnp.concatenate([d_q, d_k, d_v], axis=1)
-        d_qkv_all = gather_rows(d_qkv.T)
         normed_own = a2a(norm_forward(x_in.astype(F32), g1_full).astype(BF16), split_axis=1, concat_axis=0)
-        w_own = jnp.concatenate([to_cols(w_q), to_cols(w_k), to_cols(w_v)], axis=1).reshape(-1, rows_own)
-        d_w_own = dot(d_qkv_all, normed_own, 1, 0).reshape(n_dev, -1, rows_own)
+        w_own = qkv_rows.reshape(-1, rows_own)
+        cos2, sin2 = cos_tab[:, 0], sin_tab[:, 0]
+        cos_lanes = jnp.concatenate([cos2] * 4, axis=1)
+        sin_lanes = jnp.concatenate([-sin2, sin2] * 2, axis=1)
+        cosk = jnp.concatenate([cos2, cos2, jnp.ones_like(cos2), jnp.ones_like(cos2)], axis=1)
+        sink = jnp.concatenate([-sin2, sin2, jnp.zeros_like(cos2), jnp.zeros_like(cos2)], axis=1)
+        d_wo, d_wq_t, d_wk_t, d_wv_t, d_w1, d_w3, d_x, d_g1 = attention_backward_step(
+            heads, dh_all, w_o.reshape(-1, model), o_cols.T, q_rot, k_rot, v_lin, (cos_lanes, sin_lanes, cosk, sink),
+            d_w1s, d_w3s, w_own, normed_own.T, x_in, g1_full[None])
         from_cols = lambda d, w: d.reshape(w.shape[1], w.shape[2], rows_own).transpose(2, 0, 1)
-        d_wq = from_cols(d_w_own[:, :split_q], w_q)
-        d_wk = from_cols(d_w_own[:, split_q:split_k], w_k)
-        d_wv = from_cols(d_w_own[:, split_k:], w_v)
-        d_normed = a2a(dot(d_qkv_all, w_own, 0, 0).astype(BF16), split_axis=0, concat_axis=1)
-        _, norm1_pull = jax.vjp(norm_forward, x_in.astype(F32), g1_full)
-        d_x_norm, d_g1 = norm1_pull(d_normed.astype(F32))
-        d_x = (d_hidden.astype(F32) + d_x_norm).astype(BF16)
-        d_gains = scatter_rows(jnp.stack([d_g1, d_g2], axis=1))
-        return (y_out, d_x, d_gains[:, 0], d_gains[:, 1], d_wq, d_wk, d_wv, d_wo, d_w13[0], d_w13[1], d_down)
+        d_gains = scatter_rows(jnp.stack([d_g1[0], d_g2], axis=1))
+        return (y_out, d_x, d_gains[:, 0], d_gains[:, 1], from_cols(d_wq_t, w_q), from_cols(d_wk_t, w_k), from_cols(d_wv_t, w_v),
+                d_wo.reshape(w_o.shape), d_w1, d_w3, d_down)
 
     all_rows = P('sp')
     return jax.shard_map(layer_step, mesh=mesh, in_specs=(all_rows,) * 12, out_specs=(all_rows,) * 11, check_vma=False)

time: 1140 us -> 1040 us (0.912)
  Pallas kernels: 69.3 us -> 287 us
  waiting for transfers between devices: 453 us -> 254 us
  local copies, waits for them, and re-layouts: 159 us -> 90.6 us
  matrix products: 180 us -> 148 us
  other arithmetic: 65 us -> 50.5 us
    pallas_call x1, Pallas kernels: 48.2 us -> 266 us  [attention_backward_step(): pl.pallas_call(functools.partial(attn_bwd_comm_kernel, 'sp', heads), name...]
    all_to_all x2 -> x0, waiting for transfers between devices: 158 us -> none  [the longest x1 158 us: layer_step(): d_w13 = a2a(d_w13, split_axis=1, concat_axis=2)]
    all_gather x1, waiting for transfers between devices: 48.5 us -> 0.02 us  [layer_step(): dh_all = gather_rows(d_hidden)]
    slice x4 -> x0, local copies, waits for them, and re-layouts: 33.8 us -> none  [the longest x2 24.1 us: layer_step(): d_w13[1]]
    dot_general x15 -> x11, matrix products: 180 us -> 148 us  [dot(): lax.dot_general(lhs, rhs, (((lhs_dim,), (rhs_dim,)), ((), ())), preferred...]
    another operation x1 -> x0, local copies, waits for them, and re-layouts: 25.1 us -> none  [layer_step(): jnp.stack([dot(mlp_in, d_gate_act, 0, 0), dot(mlp_in, d_up_act, 0, 0)])]
    all_to_all x1, waiting for transfers between devices: 0.01 us -> 19.6 us  [layer_step(): a2a(norm_forward(x_in.astype(F32), g1_full).astype(BF16), split_axis=1, c...]
    unnamed x83 -> x86, local copies, waits for them, and re-layouts: 30.2 us -> 25.4 us
  transfers between devices with their start and end apart: 14 -> 11, of which waited for: 7 -> 6; matrix products, arithmetic and copies ran while one was open for 26% -> 19% of each run, Pallas kernels for 2% -> 2%
where the time goes in v2:
time: 1040 us; the launch traced here: 1030 us
  Pallas kernels  287 us (28%)
  waiting for transfers between devices  254 us (24%)
  blocking collectives  173 us (17%)
  matrix products  148 us (14%)
  local copies, waits for them, and re-layouts  90.6 us (9%)
  other arithmetic  50.5 us (5%)
  between operations  15 us (1%)
    pallas_call x1, Pallas kernels, attention_backward_step(): pl.pallas_call(functools.partial(attn_bwd_comm_kernel, 'sp', heads), name...  266 us
    dot_general x11, matrix products, dot(): lax.dot_general(lhs, rhs, (((lhs_dim,), (rhs_dim,)), ((), ())), preferred...  148 us
    all_to_all x1, blocking collectives, layer_step(): w13 = a2a(w13, split_axis=2, concat_axis=1)  126 us
    reduce_scatter x1, waiting for transfers between devices, layer_step(): y_out = (hidden_f32 + scatter_rows(dot(glu_out, w_down, 1, 0))).astype(BF16)  108 us
    reduce_scatter x1, waiting for transfers between devices, layer_step(): scatter_rows(dot(d_gate_act, w1, 1, 1) + dot(d_up_act, w3, 1, 1))  89.8 us
    all_gather x1, blocking collectives, layer_step(): pos_all = gather_rows(positions)  36.5 us
    unnamed x86, local copies, waits for them, and re-layouts  25.4 us
    pallas_call x1, Pallas kernels, attention_forward(): pl.pallas_call(attention_fwd_kernel, grid=(heads,), in_specs=[hs, fs, fs]...  21.1 us
  transfers between devices with their start and end apart: 11, of which 6 were waited for; matrix products, arithmetic and copies ran while one was open for 19% of the time, Pallas kernels for 2%

profile of v2, /device:TPU:0, one launch (start us, length us, event | category | flops | bytes accessed | tf_op | source)
XLA Modules:
  0.0 1028.3 jit_solution(1831222993721723307)
XLA Ops:
  16.4 36.5 %all-gather = s32[8,1,256]{2,1,0:T(1,128)S(1)} all-gather(s32[1,1,256]{2,1,0:T(1,128)S(1)} %bitcast.122), channel_id=1, replica_groups=mesh['sp'=8] {'sp'}, dimensions={0}, use_global_device_ids=true | all-gather | bytes 9216 | tf_op jit(solution)/shard_map/all_gather | solution.py:355
  52.9 10.9 %all_gather.22 = bf16[2048,2]{0,1:T(2,128)(2,1)S(1)} all-gather(bf16[256,2]{0,1:T(2,128)(2,1)S(1)} %pad_maximum_fusion.8), channel_id=1, replica_groups=mesh['sp'=8] {'sp'}, dimensions={0}, use_global_device_ids=true | all-gather | bytes 9216 | tf_op jit(solution)/shard_map/all_gather | solution.py:353
  64.4 5.3 fusion.47
  76.4 5.2 fusion
  82.1 6.2 fusion.19
  100.8 5.1 fusion.46
  112.3 21.1 %attn_fwd.1 = bf16[4,2048,64]{2,1,0:T(8,128)(2,1)} custom-call(bf16[4,2048,64]{2,1,0:T(8,128)(2,1)} %maximum_bitcast_fusion.q_ref, bf16[2048,64]{1,0:T(8,128)(2,1)} %pad_maximum_fusion.6.k_ref, bf16[2048,64]{1,0:T(8,128)(2,1)} %get-tuple-element.35.v_ref), custom_call_target="tpu_custom_call" | custom-call | flops 4294967296 | bytes 4194304 | tf_op jit(solution)/shard_map/attn_fwd/pallas_call | solution.py:97
  139.3 20.2 %all-to-all-done.1 = bf16[8,256,256]{1,2,0:T(8,128)(2,1)S(1)} async-done(((bf16[8,256,256]{1,2,0:T(8,128)(2,1)}), bf16[8,256,256]{1,2,0:T(8,128)(2,1)S(1)}, u32[]{:S(2)}, u32[]{:S(2)}) %all-to-all-start.1) | async-done | bytes 1048608 | tf_op jit(solution)/shard_map/all_to_all | solution.py:375
  159.5 5.9 fusion.32
  167.8 7.6 pad_maximum_fusion
  175.5 21.0 %copy.89 = bf16[2,256,8192]{1,0,2:T(2,128)(2,1)} copy(bf16[2,256,8192]{2,1,0:T(8,128)(2,1)} %pad_maximum_fusion) | data formatting | bytes 16777216 | tf_op jit(solution)/shard_map/stack | solution.py:363
  196.5 125.7 %all_to_all.68 = bf16[2,256,8192]{1,0,2:T(2,128)(2,1)} all-to-all(bf16[2,256,8192]{1,0,2:T(2,128)(2,1)} %copy.89), channel_id=1, replica_groups=mesh['sp'=8] {'sp'}, dimensions={2} | all-to-all | bytes 16777216 | tf_op jit(solution)/shard_map/all_to_all | solution.py:364
  322.2 7.9 copy.90
  330.1 5.8 fusion.57
  335.9 6.4 copy.92
  342.3 6.4 copy.91
  348.8 13.9 %convolution_convert_fusion = bf16[2048,1024]{1,0:T(8,128)(2,1)} fusion(bf16[2048,2048]{1,0:T(8,128)(2,1)} %all-gather.13.cloned.1.call-done, bf16[1024,2048]{1,0:T(8,128)(2,1)} %param.23), kind=kOutput, calls=%fused_computation.36 | convolution fusion | flops 8592031744 | bytes 16777216 | tf_op jit(solution)/shard_map/dot_general | solution.py:18
  362.7 13.9 %convolution_convert_fusion.1 = bf16[2048,1024]{1,0:T(8,128)(2,1)} fusion(bf16[2048,2048]{1,0:T(8,128)(2,1)} %all-gather.11.cloned.1.call-done, bf16[2048,1024]{1,0:T(8,128)(2,1)} %bitcast.89), kind=kOutput, calls=%fused_computation.37 | convolution fusion | flops 8592031744 | bytes 16777216 | tf_op jit(solution)/shard_map/dot_general | solution.py:18
  376.6 14.6 %fusion.10 = (bf16[2048,1024]{1,0:T(8,128)(2,1)S(1)}, bf16[2048,1024]{1,0:T(8,128)(2,1)}) fusion(bf16[2048,1024]{1,0:T(8,128)(2,1)} %convolution_convert_fusion.1, bf16[2048,1024]{1,0:T(8,128)(2,1)S(1)} %copy-done.32, bf16[2048,2048]{1,0:T(8,128)(2,1)S(1)} %copy-done.28, bf16[2048,1024]{1,0:T(8,128)(2,1)S(1)} %bitcast.91), kind=kOutput, calls=%fused_computation.19 | convolution fusion | flops 8621391872 | bytes 29360128 | tf_op jit(solution)/shard_map/dot_general | solution.py:18
  391.2 11.9 %fusion.60 = f32[2048,2048]{1,0:T(8,128)} fusion(bf16[2048,1024]{1,0:T(8,128)(2,1)S(1)} %get-tuple-element.55, bf16[2048,1024]{1,0:T(8,128)(2,1)S(1)} %bitcast.92), kind=kOutput, calls=%fused_computation.102 | convolution fusion | flops 8589934592 | bytes 25165824 | tf_op jit(solution)/shard_map/dot_general | solution.py:18
  403.1 20.5 %convolution_add_fusion = f32[2048,2048]{1,0:T(8,128)} fusion(f32[2048,2048]{1,0:T(8,128)} %fusion.60, bf16[2048,1024]{1,0:T(8,128)(2,1)} %bitcast.90, bf16[2048,1024]{1,0:T(8,128)(2,1)} %convolution_convert_fusion, bf16[2048,1024]{1,0:T(8,128)(2,1)} %get-tuple-element.56), kind=kOutput, calls=%fused_computation.24 | convolution fusion | flops 8610906112 | bytes 46137344 | tf_op jit(solution)/shard_map/dot_general | solution.py:18
  423.7 16.4 %fusion.55 = f32[2048,2048]{1,0:T(8,128)} fusion(bf16[1024,2048]{1,0:T(8,128)(2,1)} %param.23, bf16[2048,1024]{1,0:T(8,128)(2,1)} %convolution_convert_fusion.1, bf16[2048,1024]{1,0:T(8,128)(2,1)} %get-tuple-element.56), kind=kOutput, calls=%fused_computation.98 | convolution fusion | flops 8606711808 | bytes 29360128 | tf_op jit(solution)/shard_map/dot_general | solution.py:18
  440.6 89.8 %reduce-scatter.8.cloned.1.call-done = f32[256,2048]{1,0:T(8,128)} async-done(((f32[2048,2048]{1,0:T(8,128)}), f32[256,2048]{1,0:T(8,128)}) %reduce-scatter.8.cloned.1.call-update) | async-done | bytes 2097168 | tf_op jit(solution)/shard_map/reduce_scatter | solution.py:391
  532.7 108.0 %reduce-scatter.6.cloned.1.call-done = f32[256,2048]{1,0:T(8,128)} async-done(((f32[2048,2048]{1,0:T(8,128)}), f32[256,2048]{1,0:T(8,128)}) %reduce-scatter.6.cloned.1.call-update) | async-done | bytes 2097168 | tf_op jit(solution)/shard_map/reduce_scatter | solution.py:384
  651.5 5.1 fusion.43
  656.6 19.6 %all-to-all-done.3 = bf16[256,8,256]{0,2,1:T(8,128)(2,1)S(1)} async-done(((bf16[256,8,256]{0,2,1:T(8,128)(2,1)}), bf16[256,8,256]{0,2,1:T(8,128)(2,1)S(1)}, u32[]{:S(2)}, u32[]{:S(2)}) %all-to-all-start.3) | async-done | bytes 1048608 | tf_op jit(solution)/shard_map/all_to_all | solution.py:395
  677.4 14.8 %fusion.61.dw1_ref = f32[2048,1024]{1,0:T(8,128)} fusion(bf16[2048,2048]{1,0:T(8,128)(2,1)} %all-gather.11.cloned.1.call-done, bf16[2048,1024]{1,0:T(8,128)(2,1)} %copy-done.34), kind=kOutput, calls=%fused_computation.103 | convolution fusion | flops 8589934592 | bytes 20971520 | tf_op jit(solution)/shard_map/dot_general | solution.py:18
  692.2 13.8 %fusion.50.dw3_ref = f32[2048,1024]{1,0:T(8,128)} fusion(bf16[2048,2048]{1,0:T(8,128)(2,1)} %all-gather.11.cloned.1.call-done, bf16[2048,1024]{1,0:T(8,128)(2,1)S(1)} %copy-done.33, bf16[2048,1024]{1,0:T(8,128)(2,1)S(1)} %copy-done.31), kind=kOutput, calls=%fused_computation.96 | convolution fusion | flops 8606711808 | bytes 25165824 | tf_op jit(solution)/shard_map/dot_general | solution.py:18
  706.0 265.8 %attn_bwd_comm.1 = (f32[256,2048]{1,0:T(8,128)}, f32[2048,256]{1,0:T(8,128)}, f32[512,256]{1,0:T(8,128)}, f32[512,256]{1,0:T(8,128)}, f32[256,8192]{1,0:T(8,128)...) custom-call(bf16[2048,2048]{1,0:T(8,128)(2,1)} %all-gather.15.cloned.1.call-done.dh_ref, ...), custom_call_target="tpu_custom_call" | custom-call | tf_op jit(solution)/shard_map/attn_bwd_comm/pallas_call | solution.py:325
  974.0 16.5 %fusion.53 = f32[1024,2048]{1,0:T(8,128)} fusion(bf16[2048,2048]{1,0:T(8,128)(2,1)} %all-gather.13.cloned.1.call-done, bf16[2048,1024]{1,0:T(8,128)(2,1)} %convolution_convert_fusion.1, bf16[2048,1024]{1,0:T(8,128)(2,1)} %get-tuple-element.56), kind=kOutput, calls=%fused_computation.97 | convolution fusion | flops 8606711808 | bytes 25165824 | tf_op jit(solution)/shard_map/dot_general | solution.py:18
  990.5 11.2 %reduce-scatter.10.cloned.1.call-done = f32[256,2]{1,0:T(8,128)} async-done(((f32[2048,2]{1,0:T(8,128)}), f32[256,2]{1,0:T(8,128)}) %reduce-scatter.10.cloned.1.call-update) | async-done | bytes 2064
  1009.3 8.4 copy.117
  (146 shorter events, 71.8 us)
Async XLA Ops:
  7.2 69.2 %all-gather.7.cloned.1.call-start = ((), (), s32[]{:S(2)}) async-start(), calls=%async_computation.7 | async-start | bytes 9437184 | tf_op jit(solution)/shard_map/all_gather | solution.py:357
  7.9 131.4 %all-gather.9.cloned.1.call-start = ((), (), s32[]{:S(2)}) async-start(), calls=%async_computation.8 | async-start | bytes 9437184 | tf_op jit(solution)/shard_map/all_gather | solution.py:358
  8.7 340.1 %all-gather.13.cloned.1.call-start = ((), (), s32[]{:S(2)}) async-start(), calls=%async_computation.11 | async-start | bytes 9437184 | tf_op jit(solution)/shard_map/all_gather | solution.py:359
  12.1 57.7 %all-to-all-start = ((bf16[8,384,256]{2,1,0:T(8,128)(2,1)}), bf16[8,384,256]{2,1,0:T(8,128)(2,1)}, u32[]{:S(2)}, u32[]{:S(2)}) async-start(bf16[8,384,256]{2,1,0:T(8,128)(2,1)} %pad_maximum_fusion.1), calls=%async_computation | async-start | bytes 3145728 | tf_op jit(solution)/shard_map/all_to_all | solution.py:362
  64.4 17.2 %copy-start.21 = (f32[2048,1]{0,1:T(1,128)}, f32[2048,1]{0,1:T(1,128)S(1)}, u32[]{:S(2)}) copy-start(f32[2048,1]{0,1:T(1,128)S(1)} %get-tuple-element.52) | copy-start | bytes 24580
  64.4 101.5 %copy-start.19 = (f32[2048,1]{0,1:T(1,128)}, f32[2048,1]{0,1:T(1,128)S(1)}, u32[]{:S(2)}) copy-start(f32[2048,1]{0,1:T(1,128)S(1)} %get-tuple-element.51) | copy-start | bytes 24580
  69.8 37.3 %copy-start.5 = (f32[2048,32]{1,0:T(8,128)}, f32[2048,32]{1,0:T(8,128)S(1)}, u32[]{:S(2)}) copy-start(f32[2048,32]{1,0:T(8,128)S(1)} %get-tuple-element.48) | copy-start | bytes 786436
  69.8 37.3 %copy-start.7 = (f32[2048,32]{1,0:T(8,128)}, f32[2048,32]{1,0:T(8,128)S(1)}, u32[]{:S(2)}) copy-start(f32[2048,32]{1,0:T(8,128)S(1)} %get-tuple-element.49) | copy-start | bytes 786436
  133.4 26.0 %copy-start = (bf16[256,2048]{1,0:T(8,128)(2,1)S(1)}, bf16[256,2048]{1,0:T(8,128)(2,1)}, u32[]{:S(2)}) copy-start(bf16[256,2048]{1,0:T(8,128)(2,1)} %x_ref.1) | copy-start | bytes 3145732
  135.4 29.9 %copy-start.9 = (bf16[2048,4,64]{0,2,1:T(8,128)(2,1)}, bf16[2048,4,64]{0,2,1:T(8,128)(2,1)S(1)}, u32[]{:S(2)}) copy-start(bf16[2048,4,64]{0,2,1:T(8,128)(2,1)S(1)} %copy.87) | copy-start | bytes 3145732
  136.9 22.5 %all-to-all-start.1 = ((bf16[8,256,256]{1,2,0:T(8,128)(2,1)}), bf16[8,256,256]{1,2,0:T(8,128)(2,1)S(1)}, u32[]{:S(2)}, u32[]{:S(2)}) async-start(bf16[8,256,256]{1,2,0:T(8,128)(2,1)} %copy.88), calls=%async_computation.1 | async-start | bytes 2097152 | tf_op jit(solution)/shard_map/all_to_all | solution.py:375
  139.2 223.4 %all-gather.11.cloned.1.call-start = ((), (), s32[]{:S(2)}) async-start(), calls=%async_computation.9 | async-start | bytes 9437184 | tf_op jit(solution)/shard_map/all_gather | solution.py:379
  167.8 362.6 %reduce-scatter.8.cloned.1.call-start = ((), (), s32[]{:S(2)}) async-start(), calls=%async_computation.12 | async-start | bytes 18874368 | tf_op jit(solution)/shard_map/reduce_scatter | solution.py:391
  362.6 13.9 %copy-start.11 = (bf16[1,8,256,1024]{3,2,1,0:T(8,128)(2,1)S(1)}, bf16[1,8,256,1024]{3,2,1,0:T(8,128)(2,1)}, u32[]{:S(2)}) copy-start(bf16[1,8,256,1024]{3,2,1,0:T(8,128)(2,1)} %copy.91) | copy-start | bytes 12582916
  362.6 13.9 %copy-start.28 = (bf16[2048,2048]{1,0:T(8,128)(2,1)S(1)}, bf16[2048,2048]{1,0:T(8,128)(2,1)}, u32[]{:S(2)}) copy-start(bf16[2048,2048]{1,0:T(8,128)(2,1)} %all-gather.11.cloned.1.call-done) | copy-start | bytes 25165828
  362.6 13.9 %copy-start.32 = (bf16[2048,1024]{1,0:T(8,128)(2,1)S(1)}, bf16[2048,1024]{1,0:T(8,128)(2,1)}, u32[]{:S(2)}) copy-start(bf16[2048,1024]{1,0:T(8,128)(2,1)} %convolution_convert_fusion) | copy-start | bytes 12582916
  391.2 11.9 %copy-start.34 = (bf16[2048,1024]{1,0:T(8,128)(2,1)}, bf16[2048,1024]{1,0:T(8,128)(2,1)S(1)}, u32[]{:S(2)}) copy-start(bf16[2048,1024]{1,0:T(8,128)(2,1)S(1)} %get-tuple-element.55) | copy-start | bytes 12582916
  423.6 217.0 %reduce-scatter.6.cloned.1.call-start = ((), (), s32[]{:S(2)}) async-start(), calls=%async_computation.10 | async-start | bytes 18874368 | tf_op jit(solution)/shard_map/reduce_scatter | solution.py:384
  440.1 90.3 %copy-start.4 = (bf16[256,2048]{1,0:T(8,128)(2,1)S(1)}, bf16[256,2048]{1,0:T(8,128)(2,1)}, u32[]{:S(2)}) copy-start(bf16[256,2048]{1,0:T(8,128)(2,1)} %copy-done.3) | copy-start | bytes 3145732
  440.1 90.3 %copy-start.20 = (f32[2048,1]{0,1:T(1,128)S(1)}, f32[2048,1]{0,1:T(1,128)}, u32[]{:S(2)}) copy-start(f32[2048,1]{0,1:T(1,128)} %copy-done.19) | copy-start | bytes 24580
  440.1 90.3 %copy-start.24 = (f32[256]{0:T(256)S(1)}, f32[256]{0:T(256)}, u32[]{:S(2)}) copy-start(f32[256]{0:T(256)} %copy-done.23) | copy-start | bytes 3076
  440.1 92.6 %copy-start.26 = (f32[256]{0:T(256)S(1)}, f32[256]{0:T(256)}, u32[]{:S(2)}) copy-start(f32[256]{0:T(256)} %copy-done.25) | copy-start | bytes 3076
  440.1 200.6 %copy-start.12 = (bf16[256,2048]{1,0:T(8,128)(2,1)S(1)}, bf16[256,2048]{1,0:T(8,128)(2,1)}, u32[]{:S(2)}) copy-start(bf16[256,2048]{1,0:T(8,128)(2,1)} %param.14) | copy-start | bytes 3145732
  440.1 265.9 %all-gather.15.cloned.1.call-start = ((), (), s32[]{:S(2)}) async-start(), calls=%async_computation.13 | async-start | bytes 9437184 | tf_op jit(solution)/shard_map/all_gather | solution.py:394
  532.6 112.5 %copy-start.1 = (bf16[256,2048]{1,0:T(8,128)(2,1)S(1)}, bf16[256,2048]{1,0:T(8,128)(2,1)}, u32[]{:S(2)}) copy-start(bf16[256,2048]{1,0:T(8,128)(2,1)} %x_ref.1) | copy-start | bytes 3145732
  532.7 112.8 %copy-start.22 = (f32[2048,1]{0,1:T(1,128)S(1)}, f32[2048,1]{0,1:T(1,128)}, u32[]{:S(2)}) copy-start(f32[2048,1]{0,1:T(1,128)} %copy-done.21) | copy-start | bytes 24580
  649.0 27.3 %all-to-all-start.3 = ((bf16[256,8,256]{0,2,1:T(8,128)(2,1)}), bf16[256,8,256]{0,2,1:T(8,128)(2,1)S(1)}, u32[]{:S(2)}, u32[]{:S(2)}) async-start(bf16[256,8,256]{0,2,1:T(8,128)(2,1)} %bitcast.94), calls=%async_computation.5 | async-start | bytes 2097152 | tf_op jit(solution)/shard_map/all_to_all | solution.py:395
  651.3 350.4 %reduce-scatter.10.cloned.1.call-start = ((), (), s32[]{:S(2)}) async-start(), calls=%async_computation.14 | async-start | bytes 1179648
  677.4 14.8 %copy-start.31 = (bf16[2048,1024]{1,0:T(8,128)(2,1)S(1)}, bf16[2048,1024]{1,0:T(8,128)(2,1)}, u32[]{:S(2)}) copy-start(bf16[2048,1024]{1,0:T(8,128)(2,1)} %get-tuple-element.56) | copy-start | bytes 12582916
  677.4 14.8 %copy-start.33 = (bf16[2048,1024]{1,0:T(8,128)(2,1)S(1)}, bf16[2048,1024]{1,0:T(8,128)(2,1)}, u32[]{:S(2)}) copy-start(bf16[2048,1024]{1,0:T(8,128)(2,1)} %convolution_convert_fusion) | copy-start | bytes 12582916
  974.0 30.1 %copy-start.16 = (bf16[256,2048]{1,0:T(8,128)(2,1)S(1)}, bf16[256,2048]{1,0:T(8,128)(2,1)}, u32[]{:S(2)}) copy-start(bf16[256,2048]{1,0:T(8,128)(2,1)} %get-tuple-element.71) | copy-start | bytes 3145732
  990.5 14.6 %copy-start.15 = (f32[2048,256]{1,0:T(8,128)S(1)}, f32[2048,256]{1,0:T(8,128)}, u32[]{:S(2)}) copy-start(f32[2048,256]{1,0:T(8,128)} %get-tuple-element.21) | copy-start | bytes 6291460
  (16 other events, 83.0 us)
Sparse Core Ops, SparseCore 0:
  9.8 66.5 all-gather.6
  78.2 48.3 all-gather.8
  128.4 59.5 all-gather.12
  190.2 106.3 all-gather.10
  423.8 106.5 reduce-scatter.7
  533.7 106.9 reduce-scatter.5
  645.2 59.5 all-gather.14
  974.1 27.5 reduce-scatter.9

commit v3 on v2

--- a/solution.py
+++ b/solution.py
@@ -302,9 +302,16 @@
     du_recv[:, rows_of(me)] = du_scr[tok_of(me), :]
     for copy in sends:
         copy.wait_recv()
-    d_norm, d_gain = norm_backward(x_ref[...].astype(F32), g1_ref[...], du_recv[...].astype(F32))
-    dx_ref[...] = (dh_ref[tok_of(me), :].astype(F32) + d_norm).astype(BF16)
-    dg1_ref[...] = d_gain
+    dg1_ref[...] = jnp.zeros_like(dg1_ref)
+
+    def input_grad(k, _):
+        part = pl.ds(pl.multiple_of(k * 16, 16), 16)
+        d_norm, d_gain = norm_backward(x_ref[part, :].astype(F32), g1_ref[...], du_recv[part, :].astype(F32))
+        dh_part = dh_ref[pl.ds(pl.multiple_of(me * tokens + k * 16, 16), 16), :]
+        dx_ref[part, :] = (dh_part.astype(F32) + d_norm).astype(BF16)
+        dg1_ref[...] += d_gain
+        return 0
+    lax.fori_loop(0, tokens // 16, input_grad, 0)
     for copy in sends:
         copy.wait_send()
     gather.drain()
@@ -338,6 +345,261 @@
     )(dh_all, wo_own, o_t, q_rot, k_rot, v_lin, *tables, d_w1, d_w3, w_own, u_t, x_in, g1)
 
 
+def mlp_comm_kernel(axis, m_ref, dout_ref, w1_ref, w3_ref, w2_ref, h_ref, g2_ref,
+                    dw1_ref, dw3_ref, dw2_ref, y_ref, dh_ref, dg2_ref,
+                    glu, d_gate, d_up, outbox, chip_sum, inbox, m_blk, do_blk, m_col, do_col, mt_scr, dot_scr, st1, st3, st2, dh_own,
+                    part_send, part_recv, mail_send, mail_recv, gat_send, gat_recv, in_sem, col_sem, out_sem, own_sem):
+    where = place(axis)
+    me, other, first, second = where
+    core = lax.rem(me, 2)
+    partner = other(1, 0, 0)
+    greet(other)
+    tokens, model = h_ref.shape
+    hid = w1_ref.shape[1]
+    tok_of = lambda d: pl.ds(pl.multiple_of(d * tokens, tokens), tokens)
+    off_first, off_second = 1 + core, 2 - core
+
+    def block_of(off, flip):
+        d_col, d_row = lax.rem(off, 2), lax.div(off, 2)
+        col, row = lax.rem(lax.div(me, 2), 2), lax.div(me, 4)
+        mix = lambda v, f: v + f - 2 * v * f
+        return mix(row, d_row) * 4 + mix(col, d_col) * 2 + mix(core, flip)
+
+    def step_off(step, flip):
+        mid_a = off_second * (1 - flip) + off_first * flip
+        mid_b = off_first * (1 - flip) + off_second * flip
+        return jnp.where(step == 0, 3, jnp.where(step == 1, mid_a, jnp.where(step == 2, mid_b, 0)))
+
+    def fetch(step):
+        off = step_off(lax.div(step, 2), 1 - lax.rem(step, 2))
+        rows = tok_of(block_of(off, 1 - lax.rem(step, 2)))
+        slot = lax.rem(step, 2)
+        return (pltpu.make_async_copy(m_ref.at[rows, :], m_blk.at[slot], in_sem.at[0, slot]),
+                pltpu.make_async_copy(dout_ref.at[rows, :], do_blk.at[slot], in_sem.at[1, slot]))
+
+    def fetch_cols(j):
+        cols = pl.ds(pl.multiple_of(j * 256, 256), 256)
+        return (pltpu.make_async_copy(m_ref.at[:, cols], m_col, col_sem.at[0]),
+                pltpu.make_async_copy(dout_ref.at[:, cols], do_col, col_sem.at[1]))
+
+    def activations(slot, rows):
+        def chunk(j, _):
+            cols = pl.ds(pl.multiple_of(j * 256, 256), 256)
+            gate = dot(m_blk[slot], w1_ref[:, cols], 1, 0).astype(BF16).astype(F32)
+            up = dot(m_blk[slot], w3_ref[:, cols], 1, 0).astype(BF16).astype(F32)
+            d_act = dot(do_blk[slot], w2_ref[cols, :], 1, 1).astype(BF16).astype(F32)
+            sig = 1.0 / (1.0 + jnp.exp(-gate))
+            silu = gate * sig
+            glu[rows, cols] = (silu * up).astype(BF16)
+            d_up[rows, cols] = (d_act * silu).astype(BF16)
+            d_gate[rows, cols] = (d_act * up * (sig + silu * (1.0 - sig))).astype(BF16)
+            return 0
+        lax.fori_loop(0, hid // 256, chunk, 0)
+
+    def add_mlp_grad(rows, put):
+        def chunk(j, _):
+            cols = pl.ds(pl.multiple_of(j * 256, 256), 256)
+            put(cols, dot(d_gate[rows, :], w1_ref[cols, :], 1, 1) + dot(d_up[rows, :], w3_ref[cols, :], 1, 1))
+            return 0
+        lax.fori_loop(0, model // 256, chunk, 0)
+
+    def add_mlp_out(rows, put):
+        def chunk(j, _):
+            cols = pl.ds(pl.multiple_of(j * 256, 256), 256)
+            put(cols, dot(glu[rows, :], w2_ref[:, cols], 1, 0))
+            return 0
+        lax.fori_loop(0, model // 256, chunk, 0)
+
+    def to_partner(step):
+        off = step_off(step, 1)
+        return pltpu.make_async_remote_copy(
+            src_ref=outbox.at[lax.rem(step, 2)], dst_ref=chip_sum.at[off], send_sem=part_send.at[step],
+            recv_sem=part_recv.at[off], device_id=(partner,), device_id_type=MESH)
+
+    def from_partner(off):
+        return pltpu.make_async_remote_copy(
+            src_ref=outbox.at[0], dst_ref=chip_sum.at[off], send_sem=part_send.at[0],
+            recv_sem=part_recv.at[off], device_id=(partner,), device_id_type=MESH)
+
+    def mail(kind):
+        off = (3, off_first, off_second)[kind]
+        dest = (first, first, second)[kind]
+        return pltpu.make_async_remote_copy(
+            src_ref=chip_sum.at[off], dst_ref=inbox.at[kind], send_sem=mail_send.at[kind],
+            recv_sem=mail_recv.at[kind], device_id=(dest,), device_id_type=MESH)
+
+    def scatter_round(prepare, partial):
+        def step_body(step, _):
+            @pl.when(step >= 2)
+            def _():
+                to_partner(step - 2).wait_send()
+
+            prepare(2 * step)
+            slot = lax.rem(step, 2)
+
+            def put_out(cols, value):
+                outbox[slot, :, cols] = value
+            partial(tok_of(block_of(step_off(step, 1), 1)), put_out)
+            to_partner(step).start()
+            prepare(2 * step + 1)
+            off = step_off(step, 0)
+            from_partner(off).wait_recv()
+
+            def put_sum(cols, value):
+                chip_sum[off, :, cols] += value
+            partial(tok_of(block_of(off, 0)), put_sum)
+
+            @pl.when(step == 0)
+            def _():
+                mail(0).start()
+
+            @pl.when(step == 2)
+            def _():
+                mail(1).start()
+                mail(0).wait_recv()
+
+                def add_mail(k, _):
+                    part = pl.ds(pl.multiple_of(k * 16, 16), 16)
+                    chip_sum[off_second, part, :] += inbox[0, part, :]
+                    return 0
+                lax.fori_loop(0, tokens // 16, add_mail, 0)
+                mail(2).start()
+            return 0
+        lax.fori_loop(0, 4, step_body, 0)
+
+    def scatter_end():
+        mail(1).wait_recv()
+        mail(2).wait_recv()
+
+    def scatter_drain():
+        to_partner(2).wait_send()
+        to_partner(3).wait_send()
+        for kind in range(3):
+            mail(kind).wait_send()
+
+    for copy in fetch(0):
+        copy.start()
+
+    def prepare_grad(half):
+        @pl.when(half < 7)
+        def _():
+            for copy in fetch(half + 1):
+                copy.start()
+        for copy in fetch(half):
+            copy.wait()
+        flip = 1 - lax.rem(half, 2)
+        activations(lax.rem(half, 2), tok_of(block_of(step_off(lax.div(half, 2), flip), flip)))
+
+    def weight_grads(begin, end):
+        for copy in fetch_cols(begin):
+            copy.start()
+
+        def body(j, _):
+            for copy in fetch_cols(j):
+                copy.wait()
+
+            def turn(k, _):
+                part = pl.ds(pl.multiple_of(k * 256, 256), 256)
+                mt_scr[:, part] = m_col[part, :].T
+                dot_scr[:, part] = do_col[part, :].T
+                return 0
+            lax.fori_loop(0, m_col.shape[0] // 256, turn, 0)
+
+            @pl.when(j + 1 < end)
+            def _():
+                for copy in fetch_cols(j + 1):
+                    copy.start()
+            rows = pl.ds(pl.multiple_of(j * 256, 256), 256)
+            out = (pltpu.make_async_copy(st1, dw1_ref.at[rows, :], out_sem.at[0]),
+                   pltpu.make_async_copy(st3, dw3_ref.at[rows, :], out_sem.at[1]),
+                   pltpu.make_async_copy(st2, dw2_ref.at[:, rows], out_sem.at[2]))
+
+            @pl.when(j > begin)
+            def _():
+                for copy in out:
+                    copy.wait()
+
+            def chunk(k, _):
+                cols = pl.ds(pl.multiple_of(k * 256, 256), 256)
+                st1[:, cols] = dot(mt_scr[...], d_gate[:, cols], 1, 0)
+                st3[:, cols] = dot(mt_scr[...], d_up[:, cols], 1, 0)
+                st2[cols, :] = dot(dot_scr[...], glu[:, cols], 1, 0).T
+                return 0
+            lax.fori_loop(0, hid // 256, chunk, 0)
+            for copy in out:
+                copy.start()
+            return 0
+        lax.fori_loop(begin, end, body, 0)
+        rows = pl.ds((end - 1) * 256, 256)
+        for copy in (pltpu.make_async_copy(st1, dw1_ref.at[rows, :], out_sem.at[0]),
+                     pltpu.make_async_copy(st3, dw3_ref.at[rows, :], out_sem.at[1]),
+                     pltpu.make_async_copy(st2, dw2_ref.at[:, rows], out_sem.at[2])):
+            copy.wait()
+
+    scatter_round(prepare_grad, add_mlp_grad)
+    own_do = pltpu.make_async_copy(dout_ref.at[tok_of(me), :], dh_own, own_sem.at[0])
+    own_do.start()
+    weight_grads(0, 4)
+    own_do.wait()
+    scatter_end()
+    dg2_ref[...] = jnp.zeros_like(dg2_ref)
+
+    def hidden_grad(k, _):
+        part = pl.ds(pl.multiple_of(k * 16, 16), 16)
+        d_mlp = (chip_sum[0, part, :] + inbox[1, part, :] + inbox[2, part, :]).astype(BF16).astype(F32)
+        d_norm, d_gain = norm_backward(h_ref[part, :].astype(F32), g2_ref[...], d_mlp)
+        dh_own[part, :] = (dh_own[part, :].astype(F32) + d_norm).astype(BF16)
+        dg2_ref[...] += d_gain
+        return 0
+    lax.fori_loop(0, tokens // 16, hidden_grad, 0)
+    scatter_drain()
+    gather = Gather(lambda d: dh_ref.at[tok_of(d), :], gat_send, gat_recv, where, own=dh_own)
+    gather.start()
+    own_out = pltpu.make_async_copy(dh_own, dh_ref.at[tok_of(me), :], own_sem.at[1])
+    own_out.start()
+    weight_grads(4, 8)
+    gather.got_first()
+    gather.got_second()
+    gather.got_partner(0)
+    scatter_round(lambda half: None, add_mlp_out)
+    gather.got_diag()
+    for i in range(1, 4):
+        gather.got_partner(i)
+    scatter_end()
+
+    def layer_out(k, _):
+        part = pl.ds(pl.multiple_of(k * 16, 16), 16)
+        y_ref[part, :] = (h_ref[part, :].astype(F32) + (chip_sum[0, part, :] + inbox[1, part, :] + inbox[2, part, :])).astype(BF16)
+        return 0
+    lax.fori_loop(0, tokens // 16, layer_out, 0)
+    scatter_drain()
+    gather.drain()
+    own_out.wait()
+
+
+def mlp_step(m_all, dout_all, w1, w3, w2, hidden, g2):
+    seq_len, model = m_all.shape
+    hid, tokens = w1.shape[1], hidden.shape[0]
+    shape = jax.ShapeDtypeStruct
+    vmem, hbm = pl.BlockSpec(memory_space=pltpu.VMEM), pl.BlockSpec(memory_space=pl.ANY)
+    dma = pltpu.SemaphoreType.DMA
+    return pl.pallas_call(
+        functools.partial(mlp_comm_kernel, 'sp'), name='mlp_comm',
+        in_specs=[hbm] * 2 + [vmem] * 5,
+        out_specs=[hbm] * 3 + [vmem, hbm, vmem],
+        out_shape=[shape((model, hid), F32), shape((model, hid), F32), shape((hid, model), F32),
+                   shape(hidden.shape, BF16), shape((seq_len, model), BF16), shape((1, model), F32)],
+        scratch_shapes=[pltpu.VMEM((seq_len, hid), BF16), pltpu.VMEM((seq_len, hid), BF16), pltpu.VMEM((seq_len, hid), BF16),
+                        pltpu.VMEM((2, tokens, model), F32), pltpu.VMEM((4, tokens, model), F32), pltpu.VMEM((3, tokens, model), F32),
+                        pltpu.VMEM((2, tokens, model), BF16), pltpu.VMEM((2, tokens, model), BF16),
+                        pltpu.VMEM((seq_len, 256), BF16), pltpu.VMEM((seq_len, 256), BF16), pltpu.VMEM((256, seq_len), BF16), pltpu.VMEM((256, seq_len), BF16),
+                        pltpu.VMEM((256, hid), F32), pltpu.VMEM((256, hid), F32), pltpu.VMEM((hid, 256), F32),
+                        pltpu.VMEM((tokens, model), BF16),
+                        dma((4,)), dma((4,)), dma((3,)), dma((3,)), dma((7,)), dma((7,)), dma((2, 2)), dma((2,)), dma((3,)), dma((2,))],
+        compiler_params=pltpu.CompilerParams(collective_id=1, has_side_effects=True, vmem_limit_bytes=63 * 1024 * 1024),
+    )(m_all, dout_all, w1, w3, w2, hidden, g2)
+
+
 def solution(mesh):
     n_dev = mesh.shape['sp']
     gather_rows = functools.partial(lax.all_gather, axis_name='sp', axis=0, tiled=True)
@@ -375,23 +637,8 @@
         o_tok = a2a(o_cols, split_axis=0, concat_axis=1)
         hidden = (x_in.astype(F32) + dot(o_tok, wo_all, 1, 0)).astype(BF16)
         hidden_f32 = hidden.astype(F32)
-        mlp_pre, norm2_pull = jax.vjp(norm_forward, hidden_f32, g2_full)
-        mlp_in = gather_rows(mlp_pre.astype(BF16))
-        gate_act = dot(mlp_in, w1, 1, 0).astype(BF16)
-        up_act = dot(mlp_in, w3, 1, 0).astype(BF16)
-        glu_pre, glu_pull = jax.vjp(lambda g, u: jax.nn.silu(g) * u, gate_act.astype(F32), up_act.astype(F32))
-        glu_out = glu_pre.astype(BF16)
-        y_out = (hidden_f32 + scatter_rows(dot(glu_out, w_down, 1, 0))).astype(BF16)
-
-        d_down = dot(glu_out, dout_all, 0, 0)
-        d_glu = dot(dout_all, w_down, 1, 1).astype(BF16)
-        d_gate_f, d_up_f = glu_pull(d_glu.astype(F32))
-        d_gate_act, d_up_act = d_gate_f.astype(BF16), d_up_f.astype(BF16)
-        d_w1s, d_w3s = dot(mlp_in, d_gate_act, 0, 0), dot(mlp_in, d_up_act, 0, 0)
-        d_mlp = scatter_rows(dot(d_gate_act, w1, 1, 1) + dot(d_up_act, w3, 1, 1)).astype(BF16)
-        d_hidden_norm, d_g2 = norm2_pull(d_mlp.astype(F32))
-        d_hidden = (d_out.astype(F32) + d_hidden_norm).astype(BF16)
-        dh_all = gather_rows(d_hidden)
+        mlp_in = gather_rows(norm_forward(hidden.astype(F32), g2_full).astype(BF16))
+        d_w1s, d_w3s, d_down, y_out, dh_all, d_g2 = mlp_step(mlp_in, dout_all, w1, w3, w_down, hidden, g2_full[None])
         normed_own = a2a(norm_forward(x_in.astype(F32), g1_full).astype(BF16), split_axis=1, concat_axis=0)
         w_own = qkv_rows.reshape(-1, rows_own)
         cos2, sin2 = cos_tab[:, 0], sin_tab[:, 0]
@@ -403,7 +650,7 @@
             heads, dh_all, w_o.reshape(-1, model), o_cols.T, q_rot, k_rot, v_lin, (cos_lanes, sin_lanes, cosk, sink),
             d_w1s, d_w3s, w_own, normed_own.T, x_in, g1_full[None])
         from_cols = lambda d, w: d.reshape(w.shape[1], w.shape[2], rows_own).transpose(2, 0, 1)
-        d_gains = scatter_rows(jnp.stack([d_g1[0], d_g2], axis=1))
+        d_gains = scatter_rows(jnp.stack([d_g1[0], d_g2[0]], axis=1))
         return (y_out, d_x, d_gains[:, 0], d_gains[:, 1], from_cols(d_wq_t, w_q), from_cols(d_wk_t, w_k), from_cols(d_wv_t, w_v),
                 d_wo.reshape(w_o.shape), d_w1, d_w3, d_down)
 

time: 1040 us -> 914 us (0.88)
  Pallas kernels: 287 us -> 503 us
  matrix products: 148 us -> 12.4 us
  blocking collectives: 173 us -> 47.4 us
  waiting for transfers between devices: 254 us -> 169 us
    pallas_call x0 -> x1, Pallas kernels: none -> 215 us  [mlp_step(): pl.pallas_call(functools.partial(mlp_comm_kernel, 'sp'), name='mlp_comm',...]
    reduce_scatter x2 -> x0, waiting for transfers between devices: 198 us -> none  [the longest x1 108 us: layer_step(): y_out = (hidden_f32 + scatter_rows(dot(glu_out, w_down, 1, 0))).astype(BF16)]
    dot_general x11 -> x2, matrix products: 148 us -> 12.4 us  [dot(): lax.dot_general(lhs, rhs, (((lhs_dim,), (rhs_dim,)), ((), ())), preferred...]
    all_to_all x1 -> x0, blocking collectives: 126 us -> none  [layer_step(): w13 = a2a(w13, split_axis=2, concat_axis=1)]
    all_to_all x0 -> x1, waiting for transfers between devices: none -> 118 us  [layer_step(): w13 = a2a(w13, split_axis=2, concat_axis=1)]
    all_to_all x1, waiting for transfers between devices: 19.6 us -> 0.01 us  [layer_step(): a2a(norm_forward(x_in.astype(F32), g1_full).astype(BF16), split_axis=1, c...]
    unnamed x9 -> x6, waiting for transfers between devices: 13.3 us -> 30 us
    all_to_all x1, local copies, waits for them, and re-layouts: 7.86 us -> 21 us  [layer_step(): w13 = a2a(w13, split_axis=2, concat_axis=1)]
  transfers between devices with their start and end apart: 11 -> 9, of which waited for: 6 -> 4; matrix products, arithmetic and copies ran while one was open for 19% -> 14% of each run, Pallas kernels for 2% -> 2%
where the time goes in v3:
time: 914 us; the launch traced here: 905 us
  Pallas kernels  503 us (55%)
  waiting for transfers between devices  169 us (18%)
  local copies, waits for them, and re-layouts  99.7 us (11%)
  blocking collectives  47.4 us (5%)
  other arithmetic  44.3 us (5%)
  between operations  14.5 us (2%)
  starting transfers between devices  13.6 us (1%)
  matrix products  12.4 us (1%)
    pallas_call x1, Pallas kernels, attention_backward_step(): pl.pallas_call(functools.partial(attn_bwd_comm_kernel, 'sp', heads), name...  267 us
    pallas_call x1, Pallas kernels, mlp_step(): pl.pallas_call(functools.partial(mlp_comm_kernel, 'sp'), name='mlp_comm',...  215 us
    all_to_all x1, waiting for transfers between devices, layer_step(): w13 = a2a(w13, split_axis=2, concat_axis=1)  118 us
    all_gather x1, blocking collectives, layer_step(): pos_all = gather_rows(positions)  36.5 us
    unnamed x50, local copies, waits for them, and re-layouts  34 us
    unnamed x6, waiting for transfers between devices  30 us
    pallas_call x1, Pallas kernels, attention_forward(): pl.pallas_call(attention_fwd_kernel, grid=(heads,), in_specs=[hs, fs, fs]...  21.1 us
    all_to_all x1, local copies, waits for them, and re-layouts, layer_step(): w13 = a2a(w13, split_axis=2, concat_axis=1)  21 us
  transfers between devices with their start and end apart: 9, of which 4 were waited for; matrix products, arithmetic and copies ran while one was open for 14% of the time, Pallas kernels for 2%

profile of v3, /device:TPU:0, one launch (start us, length us, event | category | flops | bytes accessed | tf_op | source)
XLA Modules:
  0.0 904.6 jit_solution(10994957460886681855)
XLA Ops:
  9.4 2.7 pad_maximum_fusion.1
  12.1 4.3 all-to-all-start
  16.4 36.5 %all-gather = s32[8,1,256]{2,1,0:T(1,128)S(1)} all-gather(s32[1,1,256]{2,1,0:T(1,128)S(1)} %bitcast.106), channel_id=1, replica_groups=mesh['sp'=8] {'sp'}, dimensions={0}, use_global_device_ids=true | all-gather | bytes 9216 | tf_op jit(solution)/shard_map/all_gather | solution.py:617
  52.9 10.9 %all_gather.19 = bf16[2048,2]{0,1:T(2,128)(2,1)S(1)} all-gather(bf16[256,2]{0,1:T(2,128)(2,1)S(1)} %pad_maximum_fusion.8), channel_id=1, replica_groups=mesh['sp'=8] {'sp'}, dimensions={0}, use_global_device_ids=true | all-gather | bytes 9216 | tf_op jit(solution)/shard_map/all_gather | solution.py:615
  64.5 5.3 fusion.33
  69.8 2.6 copy.76
  72.4 4.0 all-gather.6.cloned.1.call-done
  76.4 5.2 fusion
  82.1 6.2 fusion.11
  93.1 2.7 copy.79
  95.8 2.6 copy.93
  100.8 5.4 fusion.32
  107.3 2.8 fusion.8
  110.1 2.5 maximum_bitcast_fusion.q_ref
  112.6 21.1 %attn_fwd.1 = bf16[4,2048,64]{2,1,0:T(8,128)(2,1)} custom-call(bf16[4,2048,64]{2,1,0:T(8,128)(2,1)} %maximum_bitcast_fusion.q_ref, bf16[2048,64]{1,0:T(8,128)(2,1)} %pad_maximum_fusion.6.k_ref, bf16[2048,64]{1,0:T(8,128)(2,1)} %get-tuple-element.45.v_ref), custom_call_target="tpu_custom_call" | custom-call | flops 4294967296 | bytes 4194304 | tf_op jit(solution)/shard_map/attn_fwd/pallas_call | solution.py:97
  133.7 2.8 copy.82
  139.2 3.0 all-to-all-start.1
  142.2 17.3 %all-to-all-done.1 = bf16[8,256,256]{1,2,0:T(8,128)(2,1)} async-done(((bf16[8,256,256]{1,2,0:T(8,128)(2,1)}), bf16[8,256,256]{1,2,0:T(8,128)(2,1)}, u32[]{:S(2)}, u32[]{:S(2)}) %all-to-all-start.1) | async-done | bytes 1048608 | tf_op jit(solution)/shard_map/all_to_all | solution.py:637
  159.5 6.2 fusion.15
  174.3 7.6 pad_maximum_fusion
  181.9 21.0 %copy.84 = bf16[2,256,8192]{1,0,2:T(2,128)(2,1)} copy(bf16[2,256,8192]{2,1,0:T(8,128)(2,1)} %pad_maximum_fusion) | data formatting | bytes 16777216 | tf_op jit(solution)/shard_map/stack | solution.py:625
  202.9 3.7 all-to-all-start.2
  206.9 5.2 fusion.29
  213.2 118.2 %all-to-all-done.2 = bf16[2,256,8192]{1,0,2:T(2,128)(2,1)} async-done(((bf16[2,256,8192]{1,0,2:T(2,128)(2,1)}), bf16[2,256,8192]{1,0,2:T(2,128)(2,1)}, u32[]{:S(2)}, u32[]{:S(2)}) %all-to-all-start.2) | async-done | bytes 8388640 | tf_op jit(solution)/shard_map/all_to_all | solution.py:626
  331.4 21.0 %copy.85 = bf16[2,256,8,1024]{3,1,2,0:T(8,128)(2,1)} copy(bf16[2,256,8,1024]{1,0,3,2:T(2,128)(2,1)} %bitcast.22) | data formatting | bytes 16777216 | tf_op jit(solution)/shard_map/all_to_all | solution.py:626
  352.4 6.0 fusion.36
  358.4 215.3 %mlp_comm.1 = (f32[2048,1024]{1,0:T(8,128)}, f32[2048,1024]{1,0:T(8,128)}, f32[1024,2048]{1,0:T(8,128)}, bf16[256,2048]{1,0:T(8,128)(2,1)}, bf16[2048,2048]{1,0:T(8,128)(2,1)}, /*index=5*/f32[1,2048]{1,0:T(1,128)}) custom-call(bf16[2048,2048]{1,0:T(8,128)(2,1)} %all-gather.10.cloned.1.call-done.m_ref, ...), custom_call_target="tpu_custom_call" | custom-call | tf_op jit(solution)/shard_map/mlp_comm/pallas_call | solution.py:586
  573.8 266.7 %attn_bwd_comm.1 = (f32[256,2048]{1,0:T(8,128)}, f32[2048,256]{1,0:T(8,128)}, f32[512,256]{1,0:T(8,128)}, f32[512,256]{1,0:T(8,128)}, f32[256,8192]{1,0:T(8,128)...) custom-call(bf16[2048,2048]{1,0:T(8,128)(2,1)} %get-tuple-element.26.dh_ref, ...), custom_call_target="tpu_custom_call" | custom-call | tf_op jit(solution)/shard_map/attn_bwd_comm/pallas_call | solution.py:332
  842.8 27.9 %reduce-scatter.4.cloned.1.call-done = f32[256,2]{1,0:T(8,128)} async-done(((f32[2048,2]{1,0:T(8,128)}), f32[256,2]{1,0:T(8,128)}) %reduce-scatter.4.cloned.1.call-update) | async-done | bytes 2064
  880.7 8.4 copy.113
  889.1 4.3 copy.114
  894.3 3.4 copy.115
  (90 shorter events, 37.3 us)
Async XLA Ops:
  7.2 69.2 %all-gather.6.cloned.1.call-start = ((), (), s32[]{:S(2)}) async-start(), calls=%async_computation.5 | async-start | bytes 9437184 | tf_op jit(solution)/shard_map/all_gather | solution.py:619
  7.9 134.3 %all-gather.8.cloned.1.call-start = ((), (), s32[]{:S(2)}) async-start(), calls=%async_computation.6 | async-start | bytes 9437184 | tf_op jit(solution)/shard_map/all_gather | solution.py:620
  8.0 8.4 copy-start.12
  8.0 8.4 copy-start.13
  8.0 8.4 copy-start.11
  8.7 349.8 %all-gather.12.cloned.1.call-start = ((), (), s32[]{:S(2)}) async-start(), calls=%async_computation.8 | async-start | bytes 9437184 | tf_op jit(solution)/shard_map/all_gather | solution.py:621
  12.1 57.7 %all-to-all-start = ((bf16[8,384,256]{2,1,0:T(8,128)(2,1)}), bf16[8,384,256]{2,1,0:T(8,128)(2,1)}, u32[]{:S(2)}, u32[]{:S(2)}) async-start(bf16[8,384,256]{2,1,0:T(8,128)(2,1)} %pad_maximum_fusion.1), calls=%async_computation | async-start | bytes 3145728 | tf_op jit(solution)/shard_map/all_to_all | solution.py:624
  76.4 5.8 copy-start.3
  88.4 1.1 copy-start.4
  98.5 8.8 copy-start.1
  133.7 25.8 %copy-start = (bf16[256,2048]{1,0:T(8,128)(2,1)S(1)}, bf16[256,2048]{1,0:T(8,128)(2,1)}, u32[]{:S(2)}) copy-start(bf16[256,2048]{1,0:T(8,128)(2,1)} %x_ref.1) | copy-start | bytes 3145732
  139.2 20.3 %all-to-all-start.1 = ((bf16[8,256,256]{1,2,0:T(8,128)(2,1)}), bf16[8,256,256]{1,2,0:T(8,128)(2,1)}, u32[]{:S(2)}, u32[]{:S(2)}) async-start(bf16[8,256,256]{1,2,0:T(8,128)(2,1)} %copy.83), calls=%async_computation.1 | async-start | bytes 2097152 | tf_op jit(solution)/shard_map/all_to_all | solution.py:637
  142.1 216.3 %all-gather.10.cloned.1.call-start = ((), (), s32[]{:S(2)}) async-start(), calls=%async_computation.7 | async-start | bytes 9437184 | tf_op jit(solution)/shard_map/all_gather | solution.py:640
  165.7 1.0 copy-start.2
  171.8 31.1 %all-to-all-start.3 = ((bf16[256,8,256]{0,2,1:T(8,128)(2,1)}), bf16[256,8,256]{0,2,1:T(8,128)(2,1)S(1)}, u32[]{:S(2)}, u32[]{:S(2)}) async-start(bf16[256,8,256]{0,2,1:T(8,128)(2,1)} %bitcast.80), calls=%async_computation.3 | async-start | bytes 2097152 | tf_op jit(solution)/shard_map/all_to_all | solution.py:642
  202.9 128.5 %all-to-all-start.2 = ((bf16[2,256,8192]{1,0,2:T(2,128)(2,1)}), bf16[2,256,8192]{1,0,2:T(2,128)(2,1)}, u32[]{:S(2)}, u32[]{:S(2)}) async-start(bf16[2,256,8192]{1,0,2:T(2,128)(2,1)} %copy.84), calls=%async_computation.2 | async-start | bytes 16777216 | tf_op jit(solution)/shard_map/all_to_all | solution.py:626
  206.6 664.1 %reduce-scatter.4.cloned.1.call-start = ((), (), s32[]{:S(2)}) async-start(), calls=%async_computation.9 | async-start | bytes 1179648
  573.8 266.8 %copy-start.10 = (f32[1,2048]{1,0:T(1,128)S(1)}, f32[1,2048]{1,0:T(1,128)}, u32[]{:S(2)}) copy-start(f32[1,2048]{1,0:T(1,128)} %get-tuple-element.31) | copy-start | bytes 24580
  840.5 34.9 %copy-start.7 = (bf16[256,2048]{1,0:T(8,128)(2,1)S(1)}, bf16[256,2048]{1,0:T(8,128)(2,1)}, u32[]{:S(2)}) copy-start(bf16[256,2048]{1,0:T(8,128)(2,1)} %get-tuple-element.78) | copy-start | bytes 3145732
  840.5 35.9 %copy-start.6 = (f32[2048,256]{1,0:T(8,128)S(1)}, f32[2048,256]{1,0:T(8,128)}, u32[]{:S(2)}) copy-start(f32[2048,256]{1,0:T(8,128)} %get-tuple-element.32) | copy-start | bytes 6291460
  873.1 4.7 copy-start.9
  875.4 3.1 copy-start.8
  875.4 3.9 copy-start.5
  879.3 9.7 %slice-start.2 = ((s8[8388608]{0:T(1024)(128)(4,1)}), s8[4194304]{0:T(1024)(128)(4,1)S(1)}, s32[]{:S(2)}) async-start(s8[8388608]{0:T(1024)(128)(4,1)} %bitcast.77), calls=%async_computation.12 | async-start | bytes 8388608
  880.7 8.4 slice-start.3
  880.7 12.7 %slice-start = ((s8[8388608]{0:T(1024)(128)(4,1)}), s8[4194304]{0:T(1024)(128)(4,1)S(1)}, s32[]{:S(2)}) async-start(s8[8388608]{0:T(1024)(128)(4,1)} %bitcast.75), calls=%async_computation.10 | async-start | bytes 8388608
  889.1 5.2 slice-start.1
Sparse Core Ops, SparseCore 0:
  9.8 66.5 all-gather.5
  78.2 48.3 all-gather.7
  128.4 65.5 all-gather.11
  196.2 113.8 all-gather.9
  842.9 27.7 reduce-scatter.3

commit v4 on v3

--- a/solution.py
+++ b/solution.py
@@ -21,20 +21,6 @@
 def norm_forward(hidden, gain_vec):
     inv_rms = lax.rsqrt(jnp.mean(hidden * hidden, axis=-1, keepdims=True) + NORM_EPS)
     return hidden * inv_rms * gain_vec
-
-
-def rope_tables(positions, head_dim):
-    half_dim = head_dim // 2
-    inv_freq = 1.0 / (ROPE_BASE ** (jnp.arange(half_dim, dtype=F32) * (2.0 / head_dim)))
-    angles = positions.astype(F32)[:, None] * inv_freq[None, :]
-    return jnp.cos(angles)[:, None, :], jnp.sin(angles)[:, None, :]
-
-
-def rotate(values_in, cos_tab, sin_tab):
-    half_dim = values_in.shape[-1] // 2
-    first_half = values_in[..., :half_dim].astype(F32)
-    second_half = values_in[..., half_dim:].astype(F32)
-    return jnp.concatenate([first_half * cos_tab - second_half * sin_tab, second_half * cos_tab + first_half * sin_tab], axis=-1)
 
 
 def probs_transposed(k_rows, q_blk, start):
@@ -46,72 +32,6 @@
     top = jnp.max(scores, axis=0, keepdims=True)
     weights = jnp.exp((scores - top) * (q_blk.shape[1] ** -0.5))
     return weights * (1.0 / jnp.sum(weights, axis=0, keepdims=True))
-
-
-def attention_fwd_kernel(q_ref, k_ref, v_ref, o_ref):
-    seq_len = k_ref.shape[0]
-    for start in range(0, seq_len, BLK):
-        keys = pl.ds(0, start + BLK)
-        probs = probs_transposed(k_ref[keys, :], q_ref[0, pl.ds(start, BLK), :], start)
-        o_ref[0, pl.ds(start, BLK), :] = dot(probs.astype(BF16), v_ref[keys, :], 0, 0).astype(BF16)
-
-
-def attention_bwd_kernel(q_ref, k_ref, v_ref, do_ref, dq_ref, dk_ref, dv_ref, dk_acc, dv_acc):
-    seq_len, head_dim = k_ref.shape
-
-    @pl.when(pl.program_id(0) == 0)
-    def _():
-        dk_acc[...] = jnp.zeros_like(dk_acc)
-        dv_acc[...] = jnp.zeros_like(dv_acc)
-
-    for start in range(0, seq_len, BLK):
-        keys = pl.ds(0, start + BLK)
-        rows = pl.ds(start, BLK)
-        q_blk, do_blk = q_ref[0, rows, :], do_ref[0, rows, :]
-        probs = probs_transposed(k_ref[keys, :], q_blk, start)
-        d_probs = dot(v_ref[keys, :], do_blk, 1, 1).astype(BF16).astype(F32)
-        row_dot = jnp.sum(d_probs * probs, axis=0, keepdims=True)
-        d_scores = (probs * (d_probs - row_dot) * (head_dim ** -0.5)).astype(BF16)
-        dq_ref[0, rows, :] = dot(d_scores, k_ref[keys, :], 0, 0).astype(BF16)
-        dk_acc[keys, :] += dot(d_scores, q_blk, 1, 0)
-        dv_acc[keys, :] += dot(probs.astype(BF16), do_blk, 1, 0)
-
-    @pl.when(pl.program_id(0) == pl.num_programs(0) - 1)
-    def _():
-        dk_ref[...] = dk_acc[...].astype(BF16)
-        dv_ref[...] = dv_acc[...].astype(BF16)
-
-
-def head_spec(seq_len, head_dim):
-    return pl.BlockSpec((1, seq_len, head_dim), lambda h: (h, 0, 0))
-
-
-def full_spec(seq_len, head_dim):
-    return pl.BlockSpec((seq_len, head_dim), lambda h: (0, 0))
-
-
-def attention_forward(q_heads, keys, values):
-    heads, seq_len, head_dim = q_heads.shape
-    hs, fs = head_spec(seq_len, head_dim), full_spec(seq_len, head_dim)
-    flops = 4 * heads * seq_len * seq_len * head_dim
-    return pl.pallas_call(
-        attention_fwd_kernel, grid=(heads,), in_specs=[hs, fs, fs], out_specs=hs,
-        out_shape=jax.ShapeDtypeStruct(q_heads.shape, BF16), name='attn_fwd',
-        cost_estimate=pl.CostEstimate(flops=flops, bytes_accessed=8 * heads * seq_len * head_dim, transcendentals=heads * seq_len * seq_len // 2),
-    )(q_heads, keys, values)
-
-
-def attention_backward(q_heads, keys, values, d_attn):
-    heads, seq_len, head_dim = q_heads.shape
-    hs, fs = head_spec(seq_len, head_dim), full_spec(seq_len, head_dim)
-    flops = 10 * heads * seq_len * seq_len * head_dim
-    kv_shape = jax.ShapeDtypeStruct(keys.shape, BF16)
-    return pl.pallas_call(
-        attention_bwd_kernel, grid=(heads,), in_specs=[hs, fs, fs, hs], out_specs=[hs, fs, fs],
-        out_shape=[jax.ShapeDtypeStruct(q_heads.shape, BF16), kv_shape, kv_shape], name='attn_bwd',
-        scratch_shapes=[pltpu.VMEM((seq_len, head_dim), F32), pltpu.VMEM((seq_len, head_dim), F32)],
-        cost_estimate=pl.CostEstimate(flops=flops, bytes_accessed=8 * heads * seq_len * head_dim, transcendentals=heads * seq_len * seq_len // 2),
-    )(q_heads, keys, values, d_attn)
 
 
 MESH = pl.DeviceIdType.MESH
@@ -192,11 +112,11 @@
     return d_hidden, jnp.sum(d_out * (hidden * inv), axis=0, keepdims=True)
 
 
-def attn_bwd_comm_kernel(axis, heads, dh_ref, wo_ref, ot_ref, q_ref, k_ref, v_ref, cos_ref, sin_ref, cosk_ref, sink_ref,
-                         dw1_ref, dw3_ref, wown_ref, ut_ref, x_ref, g1_ref,
-                         dwo_ref, dwq_ref, dwk_ref, dwv_ref, out1_ref, out3_ref, dx_ref, dg1_ref,
-                         slots, do_scr, dk_acc, dv_acc, du_acc, du_scr, du_recv, stage,
-                         bulk_send, bulk_recv, gat_send, gat_recv, du_send, du_rsem, loc_sem):
+def attn_bwd_comm_kernel(axis, heads, dh_ref, wo_ref, ot_ref, q_ref, k_ref, v_ref, cos_ref, sin_ref,
+                         dw1_ref, dw3_ref, wown_ref, ut_ref, x_ref, g_ref, dg2_ref,
+                         dwo_ref, dwq_ref, dwk_ref, dwv_ref, out1_ref, out3_ref, dx_ref, dg_ref,
+                         slots, do_scr, dq_scr, dg_own, dg_all, dk_acc, dv_acc, du_acc, du_scr, du_recv, stage,
+                         bulk_send, bulk_recv, gat_send, gat_recv, du_send, du_rsem, dg_send, dg_recv, loc_sem):
     where = place(axis)
     me, other, first, second = where
     greet(other)
@@ -234,7 +154,7 @@
     dk_acc[...] = jnp.zeros_like(dk_acc)
     dv_acc[...] = jnp.zeros_like(dv_acc)
     mine = slots.at[me]
-    for h in range(heads):
+    def one_head(h, _):
         def one_block(start):
             keys = pl.ds(0, start + BLK)
             rows = pl.ds(start, BLK)
@@ -243,20 +163,27 @@
             d_probs = dot(v_ref[keys, :], do_blk, 1, 1).astype(BF16).astype(F32)
             row_dot = jnp.sum(d_probs * probs, axis=0, keepdims=True)
             d_scores = (probs * (d_probs - row_dot) * (head_dim ** -0.5)).astype(BF16)
-            mine[rows, h * head_dim:(h + 1) * head_dim] = dot(d_scores, k_ref[keys, :], 0, 0).astype(BF16)
+            dq_scr[h, rows, :] = dot(d_scores, k_ref[keys, :], 0, 0).astype(BF16)
             dk_acc[keys, :] += dot(d_scores, q_blk, 1, 0)
             dv_acc[keys, :] += dot(probs.astype(BF16), do_blk, 1, 0)
         for start in range(0, seq_len, BLK):
             one_block(start)
+        return 0
+    lax.fori_loop(0, heads, one_head, 0)
     mine[:, qw:qw + head_dim] = dk_acc[...].astype(BF16)
     mine[:, qw + head_dim:] = dv_acc[...].astype(BF16)
-    for start in range(0, seq_len, BLK):
-        rows = pl.ds(start, BLK)
-        for h in range(0, qw, 128):
-            cols = pl.ds(h, 128)
-            mine[rows, cols] = turn_halves(mine[rows, cols].astype(F32), cos_ref[rows, :], -sin_ref[rows, :]).astype(BF16)
-        cols = pl.ds(qw, 128)
-        mine[rows, cols] = turn_halves(mine[rows, cols].astype(F32), cosk_ref[rows, :], -sink_ref[rows, :]).astype(BF16)
+    low = lax.broadcasted_iota(jnp.int32, (BLK, 128), 1) < head_dim
+
+    def turn_back(k, _):
+        rows = pl.ds(pl.multiple_of(k * BLK, BLK), BLK)
+        cos_blk, sin_blk = cos_ref[rows, :], -sin_ref[rows, :]
+        for pair in range(heads // 2):
+            both = jnp.concatenate([dq_scr[2 * pair, rows, :], dq_scr[2 * pair + 1, rows, :]], axis=1)
+            mine[rows, pair * 128:(pair + 1) * 128] = turn_halves(both.astype(F32), cos_blk, sin_blk).astype(BF16)
+        kv = mine[rows, qw:].astype(F32)
+        mine[rows, qw:] = jnp.where(low, turn_halves(kv, cos_blk, sin_blk), kv).astype(BF16)
+        return 0
+    lax.fori_loop(0, seq_len // BLK, turn_back, 0)
 
     gather = Gather(lambda d: slots.at[d], gat_send, gat_recv, where)
     gather.start()
@@ -302,17 +229,29 @@
     du_recv[:, rows_of(me)] = du_scr[tok_of(me), :]
     for copy in sends:
         copy.wait_recv()
-    dg1_ref[...] = jnp.zeros_like(dg1_ref)
+    dg_own[...] = jnp.zeros_like(dg_own)
+    dg_own[1:2, :] = dg2_ref[...]
 
     def input_grad(k, _):
         part = pl.ds(pl.multiple_of(k * 16, 16), 16)
-        d_norm, d_gain = norm_backward(x_ref[part, :].astype(F32), g1_ref[...], du_recv[part, :].astype(F32))
+        d_norm, d_gain = norm_backward(x_ref[part, :].astype(F32), g_ref[0:1, :], du_recv[part, :].astype(F32))
         dh_part = dh_ref[pl.ds(pl.multiple_of(me * tokens + k * 16, 16), 16), :]
         dx_ref[part, :] = (dh_part.astype(F32) + d_norm).astype(BF16)
-        dg1_ref[...] += d_gain
+        dg_own[0:1, :] += d_gain
         return 0
     lax.fori_loop(0, tokens // 16, input_grad, 0)
-    for copy in sends:
+    gain_sends = []
+    for n, r in enumerate((6, 7, 2, 4, 3, 5, 1)):
+        dest = other(r & 1, (r >> 1) & 1, r >> 2)
+        gain_sends.append(pltpu.make_async_remote_copy(
+            src_ref=dg_own.at[:, rows_of(dest)], dst_ref=dg_all.at[me], send_sem=dg_send.at[n],
+            recv_sem=dg_recv.at[n], device_id=(dest,), device_id_type=MESH))
+        gain_sends[-1].start()
+    dg_all[me] = dg_own[:, rows_of(me)]
+    for copy in gain_sends:
+        copy.wait_recv()
+    dg_ref[...] = jnp.sum(dg_all[...], axis=0)
+    for copy in sends + gain_sends:
         copy.wait_send()
     gather.drain()
     for copy in bulk:
@@ -321,7 +260,7 @@
         pltpu.make_async_copy(stage.at[i], dst.at[:, hid_of(me)], loc_sem.at[2 + i]).wait()
 
 
-def attention_backward_step(heads, dh_all, wo_own, o_t, q_rot, k_rot, v_lin, tables, d_w1, d_w3, w_own, u_t, x_in, g1):
+def attention_backward_step(heads, dh_all, wo_own, o_t, q_rot, k_rot, v_lin, tables, d_w1, d_w3, w_own, u_t, x_in, gains, d_g2):
     seq_len, model = dh_all.shape
     head_dim = k_rot.shape[1]
     tokens = x_in.shape[0]
@@ -331,21 +270,22 @@
     dma = pltpu.SemaphoreType.DMA
     return pl.pallas_call(
         functools.partial(attn_bwd_comm_kernel, 'sp', heads), name='attn_bwd_comm',
-        in_specs=[vmem] * 10 + [hbm] * 2 + [vmem] * 4,
+        in_specs=[vmem] * 8 + [hbm] * 2 + [vmem] * 5,
         out_specs=[vmem] * 4 + [hbm] * 2 + [vmem] * 2,
         out_shape=[shape(wo_own.shape, F32), shape((8 * heads * head_dim, rows_own), F32), shape((8 * head_dim, rows_own), F32),
                    shape((8 * head_dim, rows_own), F32), shape((rows_own, 8 * hid), F32), shape((rows_own, 8 * hid), F32),
-                   shape(x_in.shape, BF16), shape((1, model), F32)],
-        scratch_shapes=[pltpu.VMEM((8, seq_len, 384), BF16), pltpu.VMEM((heads, seq_len, head_dim), BF16),
+                   shape(x_in.shape, BF16), shape((8, rows_own), F32)],
+        scratch_shapes=[pltpu.VMEM((8, seq_len, 384), BF16), pltpu.VMEM((heads, seq_len, head_dim), BF16), pltpu.VMEM((heads, seq_len, head_dim), BF16),
+                        pltpu.VMEM((8, model), F32), pltpu.VMEM((8, 8, rows_own), F32),
                         pltpu.VMEM((seq_len, head_dim), F32), pltpu.VMEM((seq_len, head_dim), F32),
                         pltpu.VMEM((seq_len, rows_own), F32), pltpu.VMEM((seq_len, rows_own), BF16),
                         pltpu.VMEM((tokens, model), BF16), pltpu.VMEM((2, rows_own, hid), F32),
-                        dma((14,)), dma((14,)), dma((7,)), dma((7,)), dma((7,)), dma((7,)), dma((4,))],
+                        dma((14,)), dma((14,)), dma((7,)), dma((7,)), dma((7,)), dma((7,)), dma((7,)), dma((7,)), dma((4,))],
         compiler_params=pltpu.CompilerParams(collective_id=2, has_side_effects=True, vmem_limit_bytes=63 * 1024 * 1024),
-    )(dh_all, wo_own, o_t, q_rot, k_rot, v_lin, *tables, d_w1, d_w3, w_own, u_t, x_in, g1)
-
-
-def mlp_comm_kernel(axis, m_ref, dout_ref, w1_ref, w3_ref, w2_ref, h_ref, g2_ref,
+    )(dh_all, wo_own, o_t, q_rot, k_rot, v_lin, *tables, d_w1, d_w3, w_own, u_t, x_in, gains, d_g2)
+
+
+def mlp_comm_kernel(axis, m_ref, dout_ref, w1_ref, w3_ref, w2_ref, h_ref, g_ref,
                     dw1_ref, dw3_ref, dw2_ref, y_ref, dh_ref, dg2_ref,
                     glu, d_gate, d_up, outbox, chip_sum, inbox, m_blk, do_blk, m_col, do_col, mt_scr, dot_scr, st1, st3, st2, dh_own,
                     part_send, part_recv, mail_send, mail_recv, gat_send, gat_recv, in_sem, col_sem, out_sem, own_sem):
@@ -547,7 +487,7 @@
     def hidden_grad(k, _):
         part = pl.ds(pl.multiple_of(k * 16, 16), 16)
         d_mlp = (chip_sum[0, part, :] + inbox[1, part, :] + inbox[2, part, :]).astype(BF16).astype(F32)
-        d_norm, d_gain = norm_backward(h_ref[part, :].astype(F32), g2_ref[...], d_mlp)
+        d_norm, d_gain = norm_backward(h_ref[part, :].astype(F32), g_ref[1:2, :], d_mlp)
         dh_own[part, :] = (dh_own[part, :].astype(F32) + d_norm).astype(BF16)
         dg2_ref[...] += d_gain
         return 0
@@ -577,7 +517,7 @@
     own_out.wait()
 
 
-def mlp_step(m_all, dout_all, w1, w3, w2, hidden, g2):
+def mlp_step(m_all, dout_all, w1, w3, w2, hidden, gains):
     seq_len, model = m_all.shape
     hid, tokens = w1.shape[1], hidden.shape[0]
     shape = jax.ShapeDtypeStruct
@@ -597,61 +537,281 @@
                         pltpu.VMEM((tokens, model), BF16),
                         dma((4,)), dma((4,)), dma((3,)), dma((3,)), dma((7,)), dma((7,)), dma((2, 2)), dma((2,)), dma((3,)), dma((2,))],
         compiler_params=pltpu.CompilerParams(collective_id=1, has_side_effects=True, vmem_limit_bytes=63 * 1024 * 1024),
-    )(m_all, dout_all, w1, w3, w2, hidden, g2)
+    )(m_all, dout_all, w1, w3, w2, hidden, gains)
+
+
+def spread_tables(packed, upper):
+    lanes = lax.broadcasted_iota(jnp.int32, packed.shape, 1)
+    swapped = pltpu.roll(packed, 64, 1)
+    both = jnp.where((lanes < 64) != upper, packed, swapped)
+    low = lax.rem(lanes, 64) < 32
+    return jnp.where(low, both, pltpu.roll(both, 32, 1)), jnp.where(low, -pltpu.roll(both, 96, 1), both)
+
+
+def attention_comm_kernel(axis, heads, x_ref, tab_ref, gain_ref, qkvw_ref, wo_ref, wg_ref, wu_ref, dout_ref,
+                          q_ref, k_ref, v_ref, ot_ref, ut_ref, cos_ref, sin_ref, gfull_ref, h_ref,
+                          m_ref, w1_ref, w3_ref, doutall_ref,
+                          x_all, tab_all, gain_all, w_head, wo_all, o_all, u_blk, qkv_blk, o_scr, o_own, h_scr, m_out, stage,
+                          g_send, g_recv, w_send, w_recv, x_send, x_recv, t_send, t_recv, wo_send, wo_recv, bulk_send, bulk_recv,
+                          o_send, o_recv, do_send, do_recv, m_loc, m_send, m_recv, loc_sem):
+    where = place(axis)
+    me, other, first, second = where
+    core = lax.rem(me, 2)
+    partner = other(1, 0, 0)
+    greet(other)
+    tokens, model = x_ref.shape
+    seq_len, head_dim = k_ref.shape
+    qw = heads * head_dim
+    rows_own, hid = wg_ref.shape[0], w1_ref.shape[1]
+    tok_of = lambda d: pl.ds(pl.multiple_of(d * tokens, tokens), tokens)
+    cols_of = lambda d: pl.ds(pl.multiple_of(d * rows_own, rows_own), rows_own)
+    hid_of = lambda d: pl.ds(pl.multiple_of(d * hid, hid), hid)
+    peers = [other(r & 1, (r >> 1) & 1, r >> 2) for r in (6, 2, 4, 7, 3, 5, 1)]
+
+    def to_all(src_of, dst, send_sem, recv_sem):
+        return [pltpu.make_async_remote_copy(
+            src_ref=src_of(dest), dst_ref=dst, send_sem=send_sem.at[n], recv_sem=recv_sem.at[n],
+            device_id=(dest,), device_id_type=MESH) for n, dest in enumerate(peers)]
+
+    small = to_all(lambda dest: gain_ref, gain_all.at[me], g_send, g_recv)
+    slices = to_all(lambda dest: qkvw_ref.at[dest], w_head.at[:, cols_of(me)], w_send, w_recv)
+    for copy in small + slices:
+        copy.start()
+    tab_slot = lambda d: tab_all.at[d]
+    x_gather = Gather(lambda d: x_all.at[tok_of(d), :], x_send, x_recv, where, own=x_ref)
+    t_gather = Gather(tab_slot, t_send, t_recv, where, own=tab_ref)
+    t_gather.start()
+    x_gather.start()
+    wo_gather = Gather(lambda d: wo_all.at[cols_of(d), :], wo_send, wo_recv, where, own=wo_ref)
+    do_gather = Gather(lambda d: doutall_ref.at[tok_of(d), :], do_send, do_recv, where, own=dout_ref)
+    bulk = []
+    for n, dest in enumerate(peers):
+        for i, (src, dst) in enumerate(((wg_ref, w1_ref), (wu_ref, w3_ref))):
+            bulk.append(pltpu.make_async_remote_copy(
+                src_ref=src.at[:, hid_of(dest)], dst_ref=dst.at[cols_of(me), :], send_sem=bulk_send.at[2 * n + i],
+                recv_sem=bulk_recv.at[2 * n + i], device_id=(dest,), device_id_type=MESH))
+
+    local = []
+    for i, (src, dst) in enumerate(((wg_ref, w1_ref), (wu_ref, w3_ref))):
+        local.append((pltpu.make_async_copy(src.at[:, hid_of(me)], stage.at[i], loc_sem.at[i]),
+                      pltpu.make_async_copy(stage.at[i], dst.at[cols_of(me), :], loc_sem.at[2 + i])))
+        local[-1][0].start()
+    own_dout = pltpu.make_async_copy(dout_ref, doutall_ref.at[tok_of(me), :], loc_sem.at[4])
+    own_dout.start()
+    x_all[tok_of(me), :] = x_ref[...]
+    tab_all[me] = tab_ref[...]
+    gain_all[me] = gain_ref[...]
+    w_head[:, cols_of(me)] = qkvw_ref[me]
+    wo_all[cols_of(me), :] = wo_ref[...]
+    for load, store in local:
+        load.wait()
+        store.start()
+    for copy in small:
+        copy.wait_recv()
+    for d in range(8):
+        gfull_ref[:, d * rows_own:(d + 1) * rows_own] = gain_all[d]
+    for copy in slices:
+        copy.wait_recv()
+
+    def use(d):
+        base = pl.multiple_of(d * tokens, tokens)
+
+        def norm(k, _):
+            part = pl.ds(pl.multiple_of(k * 16, 16), 16)
+            x_part = x_all[pl.ds(pl.multiple_of(base + k * 16, 16), 16), :].astype(F32)
+            u_blk[part, :] = norm_forward(x_part, gfull_ref[0:1, :]).astype(BF16)
+            return 0
+        lax.fori_loop(0, tokens // 16, norm, 0)
+        ut_ref[:, tok_of(d)] = u_blk[:, cols_of(me)].T
+        qkv_blk[...] = dot(u_blk[...], w_head[...], 1, 1).astype(BF16)
+        half = tokens // 2
+        for part in range(2):
+            rows = pl.ds(pl.multiple_of(base + part * half, half), half)
+            cos_blk, sin_blk = spread_tables(tab_all[d], part == 1)
+            cos_ref[rows, :] = cos_blk
+            sin_ref[rows, :] = sin_blk
+            source = slice(part * half, (part + 1) * half)
+            for pair in range(heads // 2):
+                turned = turn_halves(qkv_blk[source, pair * 128:(pair + 1) * 128].astype(F32), cos_blk, sin_blk).astype(BF16)
+                q_ref[2 * pair, rows, :] = turned[:, :head_dim]
+                q_ref[2 * pair + 1, rows, :] = turned[:, head_dim:]
+            turned = turn_halves(qkv_blk[source, qw:].astype(F32), cos_blk, sin_blk).astype(BF16)
+            k_ref[rows, :] = turned[:, :head_dim]
+            v_ref[rows, :] = qkv_blk[source, qw + head_dim:]
+
+    x_gather.got_first()
+    t_gather.got_first()
+    x_gather.got_second()
+    t_gather.got_second()
+    wo_gather.start()
+    for copy in bulk:
+        copy.start()
+    x_gather.got_partner(0)
+    t_gather.got_partner(0)
+
+    def use_near(i, _):
+        use(jnp.where(i == 0, me, jnp.where(i == 1, first, jnp.where(i == 2, second, partner))))
+        return 0
+    lax.fori_loop(0, 4, use_near, 0)
+    x_gather.got_diag()
+    t_gather.got_diag()
+    for i in range(1, 4):
+        x_gather.got_partner(i)
+        t_gather.got_partner(i)
+
+    def use_far(i, _):
+        use(jnp.where(i == 0, other(0, 1, 1), jnp.where(i == 1, other(1, 1, 0), jnp.where(i == 2, other(1, 0, 1), other(1, 1, 1)))))
+        return 0
+    lax.fori_loop(0, 4, use_far, 0)
+
+    def one_head(h, _):
+        for start in range(0, seq_len, BLK):
+            keys, rows = pl.ds(0, start + BLK), pl.ds(start, BLK)
+            probs = probs_transposed(k_ref[keys, :], q_ref[h, rows, :], start)
+            o_scr[h, rows, :] = dot(probs.astype(BF16), v_ref[keys, :], 0, 0).astype(BF16)
+        return 0
+    lax.fori_loop(0, heads, one_head, 0)
+    for h in range(heads):
+        o_own[:, h * head_dim:(h + 1) * head_dim] = o_scr[h]
+    wo_gather.got_first()
+    wo_gather.got_second()
+    o_gather = Gather(lambda d: o_all.at[:, cols_of(d)], o_send, o_recv, where, own=o_own)
+    o_gather.start()
+    o_all[:, cols_of(me)] = o_own[...]
+
+    def turn_out(k, _):
+        rows = tok_of(k)
+        ot_ref[:, rows] = o_own[rows, :].T
+        return 0
+    lax.fori_loop(0, 8, turn_out, 0)
+    wo_gather.got_diag()
+    for i in range(4):
+        wo_gather.got_partner(i)
+    o_gather.got_first()
+    o_gather.got_second()
+    do_gather.start()
+    o_gather.got_partner(0)
+    o_gather.got_diag()
+    for i in range(1, 4):
+        o_gather.got_partner(i)
+
+    def rows_at(i):
+        flips = lambda a, b: other(0, a, b)
+        return tok_of(jnp.where(i == 0, me, jnp.where(i == 1, flips(1, 0), jnp.where(i == 2, flips(0, 1), flips(1, 1)))))
+
+    def give(i):
+        slot = lax.rem(i, 2)
+        rows = rows_at(i)
+        return (pltpu.make_async_copy(m_out.at[slot], m_ref.at[rows, :], m_loc.at[slot]),
+                pltpu.make_async_remote_copy(src_ref=m_out.at[slot], dst_ref=m_ref.at[rows, :], send_sem=m_send.at[i],
+                                             recv_sem=m_recv.at[i], device_id=(partner,), device_id_type=MESH))
+
+    def hidden_block(i, _):
+        rows = rows_at(i)
+        base = rows.start
+        slot = lax.rem(i, 2)
+
+        @pl.when(i >= 2)
+        def _():
+            to_hbm, to_partner = give(i - 2)
+            to_hbm.wait()
+            to_partner.wait_send()
+
+        def chunk(j, _):
+            cols = pl.ds(pl.multiple_of(j * 256, 256), 256)
+            h_scr[:, cols] = dot(o_all[rows, :], wo_all[:, cols], 1, 0)
+            return 0
+        lax.fori_loop(0, model // 256, chunk, 0)
+
+        def norm(k, _):
+            part = pl.ds(pl.multiple_of(k * 16, 16), 16)
+            x_part = x_all[pl.ds(pl.multiple_of(base + k * 16, 16), 16), :].astype(F32)
+            hidden = (x_part + h_scr[part, :]).astype(BF16)
+
+            @pl.when(i == 0)
+            def _():
+                h_ref[part, :] = hidden
+            m_out[slot, part, :] = norm_forward(hidden.astype(F32), gfull_ref[1:2, :]).astype(BF16)
+            return 0
+        lax.fori_loop(0, tokens // 16, norm, 0)
+        for copy in give(i):
+            copy.start()
+
+        @pl.when(i == 1)
+        def _():
+            do_gather.got_first()
+            do_gather.got_second()
+        return 0
+    lax.fori_loop(0, 4, hidden_block, 0)
+    do_gather.got_diag()
+    for i in range(4):
+        do_gather.got_partner(i)
+        give(i)[1].wait_recv()
+    for i in range(2, 4):
+        give(i)[0].wait()
+        give(i)[1].wait_send()
+    for copy in small + slices:
+        copy.wait_send()
+    for gather in (x_gather, t_gather, wo_gather, o_gather, do_gather):
+        gather.drain()
+    for copy in bulk:
+        copy.wait()
+    for load, store in local:
+        store.wait()
+    own_dout.wait()
+
+
+def attention_step(heads, x_in, tab, gains, qkv_rows, wo_own, w_gate, w_up, d_out):
+    tokens, model = x_in.shape
+    seq_len = 8 * tokens
+    head_dim = wo_own.shape[0] // heads
+    rows_own, hid = w_gate.shape[0], w_gate.shape[1] // 8
+    shape = jax.ShapeDtypeStruct
+    vmem, hbm = pl.BlockSpec(memory_space=pltpu.VMEM), pl.BlockSpec(memory_space=pl.ANY)
+    dma = pltpu.SemaphoreType.DMA
+    return pl.pallas_call(
+        functools.partial(attention_comm_kernel, 'sp', heads), name='attention_comm',
+        in_specs=[vmem] * 5 + [hbm] * 2 + [vmem],
+        out_specs=[vmem] * 9 + [hbm] * 4,
+        out_shape=[shape((heads, seq_len, head_dim), BF16), shape((seq_len, head_dim), BF16), shape((seq_len, head_dim), BF16),
+                   shape((heads * head_dim, seq_len), BF16), shape((rows_own, seq_len), BF16),
+                   shape((seq_len, 128), F32), shape((seq_len, 128), F32), shape((8, model), F32), shape((tokens, model), BF16),
+                   shape((seq_len, model), BF16), shape((model, hid), BF16), shape((model, hid), BF16), shape((seq_len, model), BF16)],
+        scratch_shapes=[pltpu.VMEM((seq_len, model), BF16), pltpu.VMEM((8, tokens // 2, 128), F32), pltpu.VMEM((8, 8, rows_own), F32),
+                        pltpu.VMEM((384, model), BF16), pltpu.VMEM((model, model), BF16), pltpu.VMEM((seq_len, model), BF16),
+                        pltpu.VMEM((tokens, model), BF16), pltpu.VMEM((tokens, 384), BF16), pltpu.VMEM((heads, seq_len, head_dim), BF16),
+                        pltpu.VMEM((seq_len, heads * head_dim), BF16), pltpu.VMEM((tokens, model), F32), pltpu.VMEM((2, tokens, model), BF16),
+                        pltpu.VMEM((2, rows_own, hid), BF16),
+                        dma((7,)), dma((7,)), dma((7,)), dma((7,)), dma((7,)), dma((7,)), dma((7,)), dma((7,)), dma((7,)), dma((7,)),
+                        dma((14,)), dma((14,)), dma((7,)), dma((7,)), dma((7,)), dma((7,)), dma((2,)), dma((4,)), dma((4,)), dma((5,))],
+        compiler_params=pltpu.CompilerParams(collective_id=0, has_side_effects=True, vmem_limit_bytes=63 * 1024 * 1024),
+    )(x_in, tab, gains, qkv_rows, wo_own, w_gate, w_up, d_out)
 
 
 def solution(mesh):
     n_dev = mesh.shape['sp']
-    gather_rows = functools.partial(lax.all_gather, axis_name='sp', axis=0, tiled=True)
-    scatter_rows = functools.partial(lax.psum_scatter, axis_name='sp', scatter_dimension=0, tiled=True)
-    a2a = functools.partial(lax.all_to_all, axis_name='sp', tiled=True)
 
     def layer_step(x_in, positions, d_out, norm1_gain, norm2_gain, w_q, w_k, w_v, w_o, w_gate, w_up, w_down):
         tokens, model = x_in.shape
-        seq_len = tokens * n_dev
         head_dim = w_q.shape[2]
         heads = w_q.shape[1] // n_dev
         rows_own = w_q.shape[0]
-        gains = gather_rows(jnp.stack([norm1_gain, norm2_gain], axis=1))
-        g1_full, g2_full = gains[:, 0].astype(F32), gains[:, 1].astype(F32)
-        pos_all = gather_rows(positions)
-        cos_tab, sin_tab = rope_tables(pos_all, head_dim)
-        x_all = gather_rows(x_in)
-        wo_all = gather_rows(w_o.reshape(-1, model))
-        dout_all = gather_rows(d_out)
+        inv_freq = 1.0 / (ROPE_BASE ** (jnp.arange(head_dim // 2, dtype=F32) * (2.0 / head_dim)))
+        angles = positions.astype(F32)[:, None] * inv_freq[None, :]
+        table = jnp.concatenate([jnp.cos(angles), jnp.sin(angles)], axis=1)
+        table = jnp.concatenate([table[:tokens // 2], table[tokens // 2:]], axis=1)
+        gains = jnp.zeros((8, rows_own), F32).at[0].set(norm1_gain.astype(F32)).at[1].set(norm2_gain.astype(F32))
         to_cols = lambda w: w.transpose(1, 2, 0).reshape(n_dev, -1, rows_own)
         qkv_rows = jnp.concatenate([to_cols(w_q), to_cols(w_k), to_cols(w_v)], axis=1)
-        qkv_w = a2a(qkv_rows, split_axis=0, concat_axis=2)[0]
-        w13 = jnp.stack([w_gate, w_up])
-        w13 = a2a(w13, split_axis=2, concat_axis=1)
-        w1, w3 = w13[0], w13[1]
-
-        normed = norm_forward(x_all.astype(F32), g1_full).astype(BF16)
-        qkv = dot(normed, qkv_w, 1, 1).astype(BF16)
-        split_q, split_k = heads * head_dim, (heads + 1) * head_dim
-        q_rot = rotate(qkv[:, :split_q].reshape(seq_len, heads, head_dim), cos_tab, sin_tab).astype(BF16).transpose(1, 0, 2)
-        k_rot = rotate(qkv[:, split_q:split_k][:, None, :], cos_tab, sin_tab).astype(BF16)[:, 0]
-        v_lin = qkv[:, split_k:]
-        o_heads = attention_forward(q_rot, k_rot, v_lin)
-        o_cols = o_heads.transpose(1, 0, 2).reshape(seq_len, heads * head_dim)
-        o_tok = a2a(o_cols, split_axis=0, concat_axis=1)
-        hidden = (x_in.astype(F32) + dot(o_tok, wo_all, 1, 0)).astype(BF16)
-        hidden_f32 = hidden.astype(F32)
-        mlp_in = gather_rows(norm_forward(hidden.astype(F32), g2_full).astype(BF16))
-        d_w1s, d_w3s, d_down, y_out, dh_all, d_g2 = mlp_step(mlp_in, dout_all, w1, w3, w_down, hidden, g2_full[None])
-        normed_own = a2a(norm_forward(x_in.astype(F32), g1_full).astype(BF16), split_axis=1, concat_axis=0)
-        w_own = qkv_rows.reshape(-1, rows_own)
-        cos2, sin2 = cos_tab[:, 0], sin_tab[:, 0]
-        cos_lanes = jnp.concatenate([cos2] * 4, axis=1)
-        sin_lanes = jnp.concatenate([-sin2, sin2] * 2, axis=1)
-        cosk = jnp.concatenate([cos2, cos2, jnp.ones_like(cos2), jnp.ones_like(cos2)], axis=1)
-        sink = jnp.concatenate([-sin2, sin2, jnp.zeros_like(cos2), jnp.zeros_like(cos2)], axis=1)
-        d_wo, d_wq_t, d_wk_t, d_wv_t, d_w1, d_w3, d_x, d_g1 = attention_backward_step(
-            heads, dh_all, w_o.reshape(-1, model), o_cols.T, q_rot, k_rot, v_lin, (cos_lanes, sin_lanes, cosk, sink),
-            d_w1s, d_w3s, w_own, normed_own.T, x_in, g1_full[None])
+        wo_own = w_o.reshape(-1, model)
+        (q_rot, k_rot, v_lin, o_t, u_t, cos_tab, sin_tab, g_full, hidden,
+         mlp_in, w1, w3, dout_all) = attention_step(heads, x_in, table, gains, qkv_rows, wo_own, w_gate, w_up, d_out)
+        d_w1s, d_w3s, d_down, y_out, dh_all, d_g2 = mlp_step(mlp_in, dout_all, w1, w3, w_down, hidden, g_full)
+        d_wo, d_wq_t, d_wk_t, d_wv_t, d_w1, d_w3, d_x, d_gains = attention_backward_step(
+            heads, dh_all, wo_own, o_t, q_rot, k_rot, v_lin, (cos_tab, sin_tab),
+            d_w1s, d_w3s, qkv_rows.reshape(-1, rows_own), u_t, x_in, g_full, d_g2)
         from_cols = lambda d, w: d.reshape(w.shape[1], w.shape[2], rows_own).transpose(2, 0, 1)
-        d_gains = scatter_rows(jnp.stack([d_g1[0], d_g2[0]], axis=1))
-        return (y_out, d_x, d_gains[:, 0], d_gains[:, 1], from_cols(d_wq_t, w_q), from_cols(d_wk_t, w_k), from_cols(d_wv_t, w_v),
+        return (y_out, d_x, d_gains[0], d_gains[1], from_cols(d_wq_t, w_q), from_cols(d_wk_t, w_k), from_cols(d_wv_t, w_v),
                 d_wo.reshape(w_o.shape), d_w1, d_w3, d_down)
 
     all_rows = P('sp')

time: 914 us -> 798 us (0.87)
  Pallas kernels: 503 us -> 759 us
  waiting for transfers between devices: 169 us -> 0 us
  local copies, waits for them, and re-layouts: 99.7 us -> 28.2 us
  blocking collectives: 47.4 us -> 0 us
  other arithmetic: 44.3 us -> 5.34 us
  starting transfers between devices: 13.6 us -> 0 us
  between operations: 14.5 us -> 1.1 us
  matrix products: 12.4 us -> 0 us
    pallas_call x1, Pallas kernels: 21.1 us -> 265 us  [attention_step(): pl.pallas_call(functools.partial(attention_comm_kernel, 'sp', heads), nam...]
    all_to_all x4 -> x0, waiting for transfers between devices: 136 us -> none  [the longest x1 118 us: layer_step(): w13 = a2a(w13, split_axis=2, concat_axis=1)]
    all_gather x2 -> x0, blocking collectives: 47.4 us -> none  [the longest x1 36.5 us: layer_step(): pos_all = gather_rows(positions)]
    unnamed x6 -> x0, waiting for transfers between devices: 30 us -> none
    all_to_all x5 -> x0, local copies, waits for them, and re-layouts: 28.1 us -> none  [the longest x1 21 us: layer_step(): w13 = a2a(w13, split_axis=2, concat_axis=1)]
    another operation x3 -> x1, local copies, waits for them, and re-layouts: 21 us -> 0.66 us  [the longest x1 21 us: layer_step(): w13 = jnp.stack([w_gate, w_up])]
    all_to_all x4 -> x0, starting transfers between devices: 13.4 us -> none  [the longest x1 4.3 us: layer_step(): qkv_w = a2a(qkv_rows, split_axis=0, concat_axis=2)[0]]
    dot_general x2 -> x0, matrix products: 12.4 us -> none  [dot(): lax.dot_general(lhs, rhs, (((lhs_dim,), (rhs_dim,)), ((), ())), preferred...]
  transfers between devices with their start and end apart: 9 -> 0, of which waited for: 4 -> 0; matrix products, arithmetic and copies ran while one was open for 14% -> 0% of each run, Pallas kernels for 2% -> 0%
where the time goes in v4:
time: 798 us; the launch traced here: 794 us
  Pallas kernels  759 us (95%)
  local copies, waits for them, and re-layouts  28.2 us (4%)
    pallas_call x1, Pallas kernels, attention_backward_step(): pl.pallas_call(functools.partial(attn_bwd_comm_kernel, 'sp', heads), name...  270 us
    pallas_call x1, Pallas kernels, attention_step(): pl.pallas_call(functools.partial(attention_comm_kernel, 'sp', heads), nam...  265 us
    pallas_call x1, Pallas kernels, mlp_step(): pl.pallas_call(functools.partial(mlp_comm_kernel, 'sp'), name='mlp_comm',...  225 us
    unnamed x27, local copies, waits for them, and re-layouts  26.1 us

profile of v4, /device:TPU:0, one launch (start us, length us, event | category | flops | bytes accessed | tf_op | source)
XLA Modules:
  0.0 794.1 jit_solution(2188234322170402125)
XLA Ops:
  0.7 0.7 convert_element_type.2
  1.3 0.7 reshape.104
  2.0 0.7 convert.7
  2.7 0.0 copy-start.4
  2.7 0.5 multiply_cosine_fusion
  3.2 0.1 fusion
  3.3 0.7 fusion.1.tab_ref
  4.1 2.6 pad_maximum_fusion.qkvw_ref
  6.7 0.0 copy-done.4
  6.7 264.8 %attention_comm.1 = (bf16[4,2048,64]{2,1,0:T(8,128)(2,1)}, bf16[2048,64]{1,0:T(8,128)(2,1)}, bf16[2048,64]{1,0:T(8,128)(2,1)}, bf16[256,2048]{1,0:T(8,128)(2,1)}...) custom-call(bf16[256,2048]{1,0:T(8,128)(2,1)} %x_ref.3, ...), custom_call_target="tpu_custom_call" | custom-call | tf_op jit(solution)/shard_map/attention_comm/pallas_call | solution.py:772
  271.5 224.9 %mlp_comm.1 = (f32[2048,1024]{1,0:T(8,128)}, f32[2048,1024]{1,0:T(8,128)}, f32[1024,2048]{1,0:T(8,128)}, bf16[256,2048]{1,0:T(8,128)(2,1)}, bf16[2048,2048]{1,0:T(8,128)(2,1)}, /*index=5*/f32[1,2048]{1,0:T(1,128)}) custom-call(bf16[2048,2048]{1,0:T(8,128)(2,1)} %get-tuple-element.62.m_ref, bf16[2048,2048]{1,0:T(8,128)(2,1)} %get-tuple-element.63.dout_ref, ...), custom_call_target="tpu_custom_call" | custom-call | tf_op jit(solution)/shard_map/mlp_comm/pallas_call | solution.py:526
  496.4 269.8 %attn_bwd_comm.1 = (f32[256,2048]{1,0:T(8,128)}, f32[2048,256]{1,0:T(8,128)}, f32[512,256]{1,0:T(8,128)}, f32[512,256]{1,0:T(8,128)}, f32[256,8192]{1,0:T(8,128)...) custom-call(bf16[2048,2048]{1,0:T(8,128)(2,1)} %get-tuple-element.69.dh_ref, ...), custom_call_target="tpu_custom_call" | custom-call | tf_op jit(solution)/shard_map/attn_bwd_comm/pallas_call | solution.py:271
  766.2 0.0 copy-start.1
  766.2 1.4 fusion.2
  767.7 0.0 copy-start.3
  767.7 2.4 copy.34
  770.0 2.5 copy.35
  772.5 0.0 copy-done.1
  772.5 1.3 copy.36
  773.8 0.0 copy-done.3
  773.8 0.8 copy.37
  774.6 0.0 copy-done.2
  774.6 0.8 copy.38
  775.4 0.0 copy-done
  775.4 1.3 copy.39
  776.7 8.4 %copy.40 = f32[256,8192]{1,0:T(8,128)} copy(f32[256,8192]{1,0:T(8,128)} %get-tuple-element.112) | data formatting | bytes 16777216
  785.1 0.0 slice-done.2
  785.1 0.0 slice-done.3
  785.1 4.3 copy.41
  789.4 0.0 slice-done
  789.4 1.0 slice-done.1
  790.3 3.4 copy.42
  (11 shorter events, 0.1 us)
Async XLA Ops:
  2.7 4.0 copy-start.4
  766.2 6.3 copy-start.1
  767.7 6.1 copy-start.3
  770.0 4.6 copy-start.2
  770.0 5.4 copy-start
  775.4 9.7 %slice-start.2 = ((s8[8388608]{0:T(1024)(128)(4,1)}), s8[4194304]{0:T(1024)(128)(4,1)S(1)}, s32[]{:S(2)}) async-start(s8[8388608]{0:T(1024)(128)(4,1)} %bitcast.23), calls=%async_computation.2 | async-start | bytes 8388608
  776.7 8.4 %slice-start.3 = ((s8[8388608]{0:T(1024)(128)(4,1)}), s8[4194304]{0:T(1024)(128)(4,1)S(1)}, s32[]{:S(2)}) async-start(s8[8388608]{0:T(1024)(128)(4,1)} %bitcast.23), calls=%async_computation.3 | async-start | bytes 8388608
  776.7 12.7 %slice-start = ((s8[8388608]{0:T(1024)(128)(4,1)}), s8[4194304]{0:T(1024)(128)(4,1)S(1)}, s32[]{:S(2)}) async-start(s8[8388608]{0:T(1024)(128)(4,1)} %bitcast.21), calls=%async_computation | async-start | bytes 8388608
  785.1 5.2 slice-start.1

commit v5 on v4

v5 whole, which is shorter than its diff:
```python
import functools
import jax
import jax.numpy as jnp
from jax import lax
from jax.experimental import pallas as pl
from jax.experimental.pallas import tpu as pltpu
from jax.sharding import PartitionSpec as P

ROPE_BASE = 10000.0
NORM_EPS = 1e-5
NEG_LARGE = -1e30
F32 = jnp.float32
BF16 = jnp.bfloat16
BLK = 256


def dot(lhs, rhs, lhs_dim, rhs_dim):
    return lax.dot_general(lhs, rhs, (((lhs_dim,), (rhs_dim,)), ((), ())), preferred_element_type=F32)


def norm_forward(hidden, gain_vec):
    inv_rms = lax.rsqrt(jnp.mean(hidden * hidden, axis=-1, keepdims=True) + NORM_EPS)
    return hidden * inv_rms * gain_vec


def probs_transposed(k_rows, q_blk, start):
    scores = dot(k_rows, q_blk, 1, 1)
    rows = lax.broadcasted_iota(jnp.int32, (BLK, BLK), 0)
    cols = lax.broadcasted_iota(jnp.int32, (BLK, BLK), 1)
    tail = jnp.where(rows <= cols, scores[start:], NEG_LARGE)
    scores = jnp.concatenate([scores[:start], tail], axis=0) if start else tail
    top = jnp.max(scores, axis=0, keepdims=True)
    weights = jnp.exp((scores - top) * (q_blk.shape[1] ** -0.5))
    return weights * (1.0 / jnp.sum(weights, axis=0, keepdims=True))


MESH = pl.DeviceIdType.MESH


def place(axis):
    me = lax.axis_index(axis)
    core = lax.rem(me, 2)
    col = lax.rem(lax.div(me, 2), 2)
    row = lax.div(me, 4)

    def other(flip_core, flip_col, flip_row):
        pick = lambda v, f: 1 - v if f else v
        return pick(row, flip_row) * 4 + pick(col, flip_col) * 2 + pick(core, flip_core)

    nbr_x, nbr_y = other(0, 1, 0), other(0, 0, 1)
    first = nbr_x * (1 - core) + nbr_y * core
    second = nbr_y * (1 - core) + nbr_x * core
    return me, other, first, second


def greet(other):
    barrier = pltpu.get_barrier_semaphore()
    for r in range(1, 8):
        pl.semaphore_signal(barrier, inc=1, device_id=(other(r & 1, (r >> 1) & 1, r >> 2),), device_id_type=MESH)
    pl.semaphore_wait(barrier, 7)


class Gather:
    def __init__(self, slot, send_sem, recv_sem, where, own=None):
        me, other, first, second = where
        partner, diag = other(1, 0, 0), other(0, 1, 1)
        own = slot(me) if own is None else own
        self.copies = []
        plan = [(own, me, first), (own, me, second), (own, me, partner), (slot(first), first, second),
                (slot(first), first, partner), (slot(second), second, partner), (slot(diag), diag, partner)]
        for i, (src, what, dest) in enumerate(plan):
            self.copies.append(pltpu.make_async_remote_copy(
                src_ref=src, dst_ref=slot(what), send_sem=send_sem.at[i], recv_sem=recv_sem.at[i],
                device_id=(dest,), device_id_type=MESH))

    def start(self):
        for i in range(3):
            self.copies[i].start()

    def got_first(self):
        self.copies[0].wait_recv()
        self.copies[3].start()
        self.copies[4].start()

    def got_second(self):
        self.copies[1].wait_recv()
        self.copies[5].start()

    def got_diag(self):
        self.copies[3].wait_recv()
        self.copies[6].start()

    def got_partner(self, i):
        self.copies[(2, 4, 5, 6)[i]].wait_recv()

    def drain(self):
        for copy in self.copies:
            copy.wait_send()


def turn_halves(values, cos_blk, sin_blk):
    width = values.shape[1]
    lanes = lax.broadcasted_iota(jnp.int32, values.shape, 1)
    partner = jnp.where(lax.rem(lanes, 64) < 32, pltpu.roll(values, width - 32, 1), pltpu.roll(values, 32, 1))
    return values * cos_blk + partner * sin_blk


def norm_backward(hidden, gain, d_out):
    inv = lax.rsqrt(jnp.mean(hidden * hidden, axis=-1, keepdims=True) + NORM_EPS)
    d_scaled = d_out * gain
    d_hidden = d_scaled * inv - hidden * (inv * inv * inv * jnp.mean(d_scaled * hidden, axis=-1, keepdims=True))
    return d_hidden, jnp.sum(d_out * (hidden * inv), axis=0, keepdims=True)


def attn_bwd_comm_kernel(axis, heads, dh_hbm, wo_hbm, ot_hbm, q_hbm, k_hbm, v_hbm, cos_hbm, sin_hbm,
                         dw1_ref, dw3_ref, wq_hbm, wk_hbm, wv_hbm, ut_hbm, x_hbm, g_hbm, dg2_hbm,
                         dwo_hbm, dwq_hbm, dwk_hbm, dwv_hbm, out1_ref, out3_ref, dx_hbm, dg_hbm,
                         dh_ref, wo_ref, ot_ref, q_ref, k_ref, v_ref, cos_ref, sin_ref, wq_ref, wk_ref, wv_ref, ut_ref, x_ref, g_ref, dg2_ref,
                         dwo_ref, dwq_ref, dwk_ref, dwv_ref, dx_ref, dg_ref,
                         slots, do_scr, dq_scr, dg_own, dg_all, dk_acc, dv_acc, du_acc, du_scr, du_recv, stage,
                         bulk_send, bulk_recv, hg_send, hg_recv, gat_send, gat_recv, du_send, du_rsem, dg_send, dg_recv, loc_sem, ld_sem, st_sem):
    loads = {}
    for i, (name, src, dst) in enumerate((
            ('wo', wo_hbm, wo_ref), ('ot', ot_hbm, ot_ref), ('q', q_hbm, q_ref), ('k', k_hbm, k_ref),
            ('v', v_hbm, v_ref), ('cos', cos_hbm, cos_ref), ('sin', sin_hbm, sin_ref), ('wq', wq_hbm, wq_ref), ('wk', wk_hbm, wk_ref),
            ('wv', wv_hbm, wv_ref), ('ut', ut_hbm, ut_ref), ('x', x_hbm, x_ref), ('g', g_hbm, g_ref), ('dg2', dg2_hbm, dg2_ref),
            ('dh', dh_hbm, dh_ref.at[pl.ds(pl.multiple_of(lax.axis_index(axis) * x_ref.shape[0], x_ref.shape[0]), x_ref.shape[0]), :]))):
        loads[name] = pltpu.make_async_copy(src, dst, ld_sem.at[i])
        loads[name].start()

    def need(*names):
        for name in names:
            loads[name].wait()

    stores = [pltpu.make_async_copy(src, dst, st_sem.at[i]) for i, (src, dst) in enumerate((
        (dwo_ref, dwo_hbm), (dwq_ref, dwq_hbm), (dwk_ref, dwk_hbm), (dwv_ref, dwv_hbm), (dx_ref, dx_hbm), (dg_ref, dg_hbm)))]
    where = place(axis)
    me, other, first, second = where
    greet(other)
    seq_len, head_dim = k_ref.shape
    rows_own, hid = stage.shape[1], stage.shape[2]
    tokens = x_ref.shape[0]
    qw = heads * head_dim
    half_rows = rows_own // 2

    rows_of = lambda d: pl.ds(pl.multiple_of(d * rows_own, rows_own), rows_own)
    hid_of = lambda d: pl.ds(pl.multiple_of(d * hid, hid), hid)
    pairs = ((dw1_ref, out1_ref), (dw3_ref, out3_ref))
    peers = [other(r & 1, (r >> 1) & 1, r >> 2) for r in (2, 4, 6, 3, 5, 7, 1)]
    bulk = []
    for part in range(4):
        src, dst = pairs[part // 2]
        for n, dest in enumerate(peers):
            low = (part % 2) * half_rows
            bulk.append(pltpu.make_async_remote_copy(
                src_ref=src.at[pl.ds(pl.multiple_of(dest * rows_own + low, half_rows), half_rows), :],
                dst_ref=dst.at[pl.ds(low, half_rows), hid_of(me)], send_sem=bulk_send.at[part * 7 + n],
                recv_sem=bulk_recv.at[part * 7 + n], device_id=(dest,), device_id_type=MESH))

    def start_bulk(part):
        for copy in bulk[part * 7:part * 7 + 7]:
            copy.start()
    tok_of = lambda d: pl.ds(pl.multiple_of(d * tokens, tokens), tokens)
    h_gather = Gather(lambda d: dh_ref.at[tok_of(d), :], hg_send, hg_recv, where, own=dh_hbm)
    h_gather.start()
    for i, (src, dst) in enumerate(pairs):
        pltpu.make_async_copy(src.at[rows_of(me), :], stage.at[i], loc_sem.at[i]).start()
    need('dh', 'wo', 'ot')
    h_gather.got_first()
    h_gather.got_second()
    start_bulk(0)
    start_bulk(1)
    h_gather.got_diag()
    for i in range(4):
        h_gather.got_partner(i)

    def split_out_grad(k, _):
        rows = pl.ds(pl.multiple_of(k * BLK, BLK), BLK)
        do_blk = dot(dh_ref[rows, :], wo_ref[...], 1, 1).astype(BF16)
        for h in range(heads):
            do_scr[h, rows, :] = do_blk[:, h * head_dim:(h + 1) * head_dim]
        cols = rows
        dwo_ref[:, cols] = dot(ot_ref[...], dh_ref[:, cols], 1, 0)
        return 0
    lax.fori_loop(0, seq_len // BLK, split_out_grad, 0)
    stores[0].start()

    for i, (src, dst) in enumerate(pairs):
        pltpu.make_async_copy(src.at[rows_of(me), :], stage.at[i], loc_sem.at[i]).wait()
        pltpu.make_async_copy(stage.at[i], dst.at[:, hid_of(me)], loc_sem.at[2 + i]).start()

    need('q', 'k', 'v')
    dk_acc[...] = jnp.zeros_like(dk_acc)
    dv_acc[...] = jnp.zeros_like(dv_acc)
    mine = slots.at[me]

    def one_head(h, _):
        def one_block(start):
            keys = pl.ds(0, start + BLK)
            rows = pl.ds(start, BLK)
            q_blk, do_blk = q_ref[h, rows, :], do_scr[h, rows, :]
            probs = probs_transposed(k_ref[keys, :], q_blk, start)
            d_probs = dot(v_ref[keys, :], do_blk, 1, 1).astype(BF16).astype(F32)
            row_dot = jnp.sum(d_probs * probs, axis=0, keepdims=True)
            d_scores = (probs * (d_probs - row_dot) * (head_dim ** -0.5)).astype(BF16)
            dq_scr[h, rows, :] = dot(d_scores, k_ref[keys, :], 0, 0).astype(BF16)
            dk_acc[keys, :] += dot(d_scores, q_blk, 1, 0)
            dv_acc[keys, :] += dot(probs.astype(BF16), do_blk, 1, 0)
        for start in range(0, seq_len, BLK):
            one_block(start)
        return 0
    lax.fori_loop(0, heads, one_head, 0)
    need('cos', 'sin')
    mine[:, qw:qw + head_dim] = dk_acc[...].astype(BF16)
    mine[:, qw + head_dim:] = dv_acc[...].astype(BF16)
    low = lax.broadcasted_iota(jnp.int32, (BLK, 128), 1) < head_dim

    def turn_back(k, _):
        rows = pl.ds(pl.multiple_of(k * BLK, BLK), BLK)
        cos_blk, sin_blk = cos_ref[rows, :], -sin_ref[rows, :]
        for pair in range(heads // 2):
            both = jnp.concatenate([dq_scr[2 * pair, rows, :], dq_scr[2 * pair + 1, rows, :]], axis=1)
            mine[rows, pair * 128:(pair + 1) * 128] = turn_halves(both.astype(F32), cos_blk, sin_blk).astype(BF16)
        kv = mine[rows, qw:].astype(F32)
        mine[rows, qw:] = jnp.where(low, turn_halves(kv, cos_blk, sin_blk), kv).astype(BF16)
        return 0
    lax.fori_loop(0, seq_len // BLK, turn_back, 0)

    gather = Gather(lambda d: slots.at[d], gat_send, gat_recv, where)
    gather.start()
    du_acc[...] = jnp.zeros_like(du_acc)
    need('wq', 'wk', 'wv', 'ut')

    def use(d):
        q_rows = pl.ds(pl.multiple_of(d * qw, qw), qw)
        kv_rows = pl.ds(pl.multiple_of(d * head_dim, head_dim), head_dim)
        w_all = jnp.concatenate([wq_ref[q_rows, :], wk_ref[kv_rows, :], wv_ref[kv_rows, :]], axis=0)

        def add_rows(k, _):
            rows = pl.ds(pl.multiple_of(k * 512, 512), 512)
            du_acc[rows, :] += dot(slots[d, rows, :], w_all, 1, 0)
            return 0
        lax.fori_loop(0, seq_len // 512, add_rows, 0)
        d_w = dot(ut_ref[...], slots[d], 1, 0).T
        dwq_ref[q_rows, :] = d_w[:qw]
        dwk_ref[kv_rows, :] = d_w[qw:qw + head_dim]
        dwv_ref[kv_rows, :] = d_w[qw + head_dim:]

    def use_many(*devices):
        def body(i, _):
            d = devices[0]
            for n in range(1, len(devices)):
                d = jnp.where(i == n, devices[n], d)
            use(d)
            return 0
        lax.fori_loop(0, len(devices), body, 0)

    use_many(me)
    gather.got_first()
    gather.got_second()
    start_bulk(2)
    gather.got_partner(0)
    use_many(first, second, other(1, 0, 0))
    gather.got_diag()
    for i in range(1, 4):
        gather.got_partner(i)
    use_many(other(0, 1, 1), other(1, 1, 0), other(1, 0, 1), other(1, 1, 1))
    du_scr[...] = du_acc[...].astype(BF16)
    for i in range(1, 4):
        stores[i].start()

    sends = []
    for n, dest in enumerate(peers):
        sends.append(pltpu.make_async_remote_copy(
            src_ref=du_scr.at[tok_of(dest), :], dst_ref=du_recv.at[:, rows_of(me)], send_sem=du_send.at[n],
            recv_sem=du_rsem.at[n], device_id=(dest,), device_id_type=MESH))
        sends[-1].start()
    start_bulk(3)
    du_recv[:, rows_of(me)] = du_scr[tok_of(me), :]
    need('x', 'g', 'dg2')
    for copy in sends:
        copy.wait_recv()
    dg_own[...] = jnp.zeros_like(dg_own)
    dg_own[1:2, :] = dg2_ref[...]

    def input_grad(k, _):
        part = pl.ds(pl.multiple_of(k * 16, 16), 16)
        d_norm, d_gain = norm_backward(x_ref[part, :].astype(F32), g_ref[0:1, :], du_recv[part, :].astype(F32))
        dh_part = dh_ref[pl.ds(pl.multiple_of(me * tokens + k * 16, 16), 16), :]
        dx_ref[part, :] = (dh_part.astype(F32) + d_norm).astype(BF16)
        dg_own[0:1, :] += d_gain
        return 0
    lax.fori_loop(0, tokens // 16, input_grad, 0)
    stores[4].start()
    gain_sends = []
    for n, dest in enumerate(peers):
        gain_sends.append(pltpu.make_async_remote_copy(
            src_ref=dg_own.at[:, rows_of(dest)], dst_ref=dg_all.at[me], send_sem=dg_send.at[n],
            recv_sem=dg_recv.at[n], device_id=(dest,), device_id_type=MESH))
        gain_sends[-1].start()
    dg_all[me] = dg_own[:, rows_of(me)]
    for copy in gain_sends:
        copy.wait_recv()
    dg_ref[...] = jnp.sum(dg_all[...], axis=0)
    stores[5].start()
    for copy in sends + gain_sends:
        copy.wait_send()
    gather.drain()
    h_gather.drain()
    for copy in bulk:
        copy.wait()
    for i, (src, dst) in enumerate(pairs):
        pltpu.make_async_copy(stage.at[i], dst.at[:, hid_of(me)], loc_sem.at[2 + i]).wait()
    for copy in stores:
        copy.wait()


def attention_backward_step(heads, dh_own, wo_own, o_t, q_rot, k_rot, v_lin, tables, d_w1, d_w3, w_q, w_k, w_v, u_t, x_in, gains, d_g2):
    seq_len, model = k_rot.shape[0], x_in.shape[1]
    head_dim = k_rot.shape[1]
    tokens = x_in.shape[0]
    rows_own, hid = model // 8, d_w1.shape[1]
    shape = jax.ShapeDtypeStruct
    hbm = pl.BlockSpec(memory_space=pl.ANY)
    dma = pltpu.SemaphoreType.DMA
    vm = lambda *dims, dtype=BF16: pltpu.VMEM(dims, dtype)
    early = (dh_own, wo_own, o_t, q_rot, k_rot, v_lin, *tables)
    late = (w_q, w_k, w_v, u_t, x_in, gains, d_g2)
    outs = (shape(wo_own.shape, F32), shape(w_q.shape, F32), shape(w_k.shape, F32), shape(w_v.shape, F32))
    ends = (shape(x_in.shape, BF16), shape((8, rows_own), F32))
    return pl.pallas_call(
        functools.partial(attn_bwd_comm_kernel, 'sp', heads), name='attn_bwd_comm',
        in_specs=[hbm] * 17, out_specs=[hbm] * 8,
        out_shape=[*outs, shape((rows_own, 8 * hid), F32), shape((rows_own, 8 * hid), F32), *ends],
        scratch_shapes=[vm(seq_len, model)] + [vm(*t.shape, dtype=t.dtype) for t in early[1:] + late + outs + ends] + [
            vm(8, seq_len, 384), vm(heads, seq_len, head_dim), vm(heads, seq_len, head_dim),
            vm(8, model, dtype=F32), vm(8, 8, rows_own, dtype=F32),
            vm(seq_len, head_dim, dtype=F32), vm(seq_len, head_dim, dtype=F32),
            vm(seq_len, rows_own, dtype=F32), vm(seq_len, rows_own), vm(tokens, model), vm(2, rows_own, hid, dtype=F32),
            dma((28,)), dma((28,)), dma((7,)), dma((7,)), dma((7,)), dma((7,)), dma((7,)), dma((7,)), dma((7,)), dma((7,)), dma((4,)), dma((15,)), dma((6,))],
        compiler_params=pltpu.CompilerParams(collective_id=2, has_side_effects=True, vmem_limit_bytes=63 * 1024 * 1024),
    )(*early, d_w1, d_w3, *late)


def mlp_comm_kernel(axis, m_ref, dout_own, w1_hbm, w3_hbm, w2_hbm, h_hbm, g_hbm,
                    dw1_ref, dw3_ref, dw2_ref, y_hbm, dh_hbm, dg2_hbm, dout_ref,
                    w1_ref, w3_ref, w2_ref, h_ref, g_ref, y_ref, dg2_ref,
                    glu, gate_s, up_s, outbox, chip_sum, inbox, blk, m_col, do_col, mt_scr, dot_scr, st1, st3, st2, dh_own,
                    part_send, part_recv, mail_send, mail_recv, do_send, do_recv,
                    in_sem, col_sem, out_sem, own_sem, ld_sem, credit):
    loads = [pltpu.make_async_copy(src, dst, ld_sem.at[i]) for i, (src, dst) in enumerate((
        (w1_hbm, w1_ref), (w3_hbm, w3_ref), (w2_hbm, w2_ref), (h_hbm, h_ref), (g_hbm, g_ref)))]
    own_in = pltpu.make_async_copy(dout_own, dh_own, own_sem.at[0])
    for copy in loads + [own_in]:
        copy.start()
    where = place(axis)
    me, other, first, second = where
    core = lax.rem(me, 2)
    partner = other(1, 0, 0)
    tokens, model = h_ref.shape
    hid = w1_ref.shape[1]
    tok_of = lambda d: pl.ds(pl.multiple_of(d * tokens, tokens), tokens)
    off_first, off_second = 1 + core, 2 - core

    def block_of(off, flip):
        d_col, d_row = lax.rem(off, 2), lax.div(off, 2)
        col, row = lax.rem(lax.div(me, 2), 2), lax.div(me, 4)
        mix = lambda v, f: v + f - 2 * v * f
        return mix(row, d_row) * 4 + mix(col, d_col) * 2 + mix(core, flip)

    def step_off(step, flip):
        mid_a = off_second * (1 - flip) + off_first * flip
        mid_b = off_first * (1 - flip) + off_second * flip
        return jnp.where(step == 0, 3, jnp.where(step == 1, mid_a, jnp.where(step == 2, mid_b, 0)))

    def half_rows(half):
        flip = 1 - lax.rem(half, 2)
        return tok_of(block_of(step_off(lax.div(half, 2), flip), flip))

    def fetch(half):
        slot = lax.rem(half, 2)
        return pltpu.make_async_copy(m_ref.at[half_rows(half), :], blk.at[slot], in_sem.at[slot])

    def fetch_dout(d):
        slot = lax.rem(d, 2)
        return pltpu.make_async_copy(dout_ref.at[tok_of(d), :], blk.at[slot], in_sem.at[slot])

    def fetch_cols(j):
        cols = pl.ds(pl.multiple_of(j * 256, 256), 256)
        return (pltpu.make_async_copy(m_ref.at[:, cols], m_col, col_sem.at[0]),
                pltpu.make_async_copy(dout_ref.at[:, cols], do_col, col_sem.at[1]))

    def sigmoid(value):
        return 1.0 / (1.0 + jnp.exp(-value))

    def activations(slot, rows):
        def chunk(j, _):
            cols = pl.ds(pl.multiple_of(j * 512, 512), 512)
            gate = dot(blk[slot], w1_ref[:, cols], 1, 0).astype(BF16)
            up = dot(blk[slot], w3_ref[:, cols], 1, 0).astype(BF16)
            gate_s[rows, cols] = gate
            up_s[rows, cols] = up
            gate = gate.astype(F32)
            glu[rows, cols] = (gate * sigmoid(gate) * up.astype(F32)).astype(BF16)
            return 0
        lax.fori_loop(0, hid // 512, chunk, 0)

    def activation_grads(slot, rows):
        def chunk(j, _):
            cols = pl.ds(pl.multiple_of(j * 512, 512), 512)
            d_act = dot(blk[slot], w2_ref[cols, :], 1, 1).astype(BF16).astype(F32)
            gate, up = gate_s[rows, cols].astype(F32), up_s[rows, cols].astype(F32)
            sig = sigmoid(gate)
            silu = gate * sig
            up_s[rows, cols] = (d_act * silu).astype(BF16)
            gate_s[rows, cols] = (d_act * up * (sig + silu * (1.0 - sig))).astype(BF16)
            return 0
        lax.fori_loop(0, hid // 512, chunk, 0)

    def add_mlp_grad(rows, put):
        def chunk(j, _):
            cols = pl.ds(pl.multiple_of(j * 512, 512), 512)
            put(cols, dot(gate_s[rows, :], w1_ref[cols, :], 1, 1) + dot(up_s[rows, :], w3_ref[cols, :], 1, 1))
            return 0
        lax.fori_loop(0, model // 512, chunk, 0)

    def add_mlp_out(rows, put):
        def chunk(j, _):
            cols = pl.ds(pl.multiple_of(j * 512, 512), 512)
            put(cols, dot(glu[rows, :], w2_ref[:, cols], 1, 0))
            return 0
        lax.fori_loop(0, model // 512, chunk, 0)

    def signal(index, device):
        pl.semaphore_signal(credit.at[index], inc=1, device_id=(device,), device_id_type=MESH)

    class Scatter:
        def __init__(self, turn):
            self.turn = turn

        def to_partner(self, step):
            off = step_off(step, 1)
            return pltpu.make_async_remote_copy(
                src_ref=outbox.at[lax.rem(step, 2)], dst_ref=chip_sum.at[off], send_sem=part_send.at[self.turn, step],
                recv_sem=part_recv.at[self.turn, off], device_id=(partner,), device_id_type=MESH)

        def from_partner(self, off):
            return pltpu.make_async_remote_copy(
                src_ref=outbox.at[0], dst_ref=chip_sum.at[off], send_sem=part_send.at[self.turn, 0],
                recv_sem=part_recv.at[self.turn, off], device_id=(partner,), device_id_type=MESH)

        def mail(self, kind):
            off = (3, off_first, off_second)[kind]
            dest = (first, first, second)[kind]
            return pltpu.make_async_remote_copy(
                src_ref=chip_sum.at[off], dst_ref=inbox.at[kind], send_sem=mail_send.at[self.turn, kind],
                recv_sem=mail_recv.at[self.turn, kind], device_id=(dest,), device_id_type=MESH)

        def step(self, step, prepare, partial):
            slot = lax.rem(step, 2)
            prepare(2 * step)

            def put_out(cols, value):
                outbox[slot, :, cols] = value
            partial(half_rows(2 * step), put_out)
            self.to_partner(step).start()
            prepare(2 * step + 1)
            off = step_off(step, 0)
            self.from_partner(off).wait_recv()

            def put_sum(cols, value):
                chip_sum[off, :, cols] += value
            partial(half_rows(2 * step + 1), put_sum)

        def pass_on(self):
            self.mail(0).wait_recv()

            def add_mail(k, _):
                part = pl.ds(pl.multiple_of(k * 16, 16), 16)
                chip_sum[off_second, part, :] += inbox[0, part, :]
                return 0
            lax.fori_loop(0, tokens // 16, add_mail, 0)

    out_round, grad_round = Scatter(0), Scatter(1)

    def prepare_out(half):
        @pl.when(half < 7)
        def _():
            fetch(half + 1).start()
        fetch(half).wait()
        activations(lax.rem(half, 2), half_rows(half))

    def weight_grads(begin, end):
        for copy in fetch_cols(begin):
            copy.start()

        def body(j, _):
            for copy in fetch_cols(j):
                copy.wait()

            def turn(k, _):
                part = pl.ds(pl.multiple_of(k * 256, 256), 256)
                mt_scr[:, part] = m_col[part, :].T
                dot_scr[:, part] = do_col[part, :].T
                return 0
            lax.fori_loop(0, m_col.shape[0] // 256, turn, 0)

            @pl.when(j + 1 < end)
            def _():
                for copy in fetch_cols(j + 1):
                    copy.start()
            rows = pl.ds(pl.multiple_of(j * 256, 256), 256)
            out = (pltpu.make_async_copy(st1, dw1_ref.at[rows, :], out_sem.at[0]),
                   pltpu.make_async_copy(st3, dw3_ref.at[rows, :], out_sem.at[1]),
                   pltpu.make_async_copy(st2, dw2_ref.at[:, rows], out_sem.at[2]))

            @pl.when(j > begin)
            def _():
                for copy in out:
                    copy.wait()

            def chunk(k, _):
                cols = pl.ds(pl.multiple_of(k * 512, 512), 512)
                st1[:, cols] = dot(mt_scr[...], gate_s[:, cols], 1, 0)
                st3[:, cols] = dot(mt_scr[...], up_s[:, cols], 1, 0)
                st2[cols, :] = dot(dot_scr[...], glu[:, cols], 1, 0).T
                return 0
            lax.fori_loop(0, hid // 512, chunk, 0)
            for copy in out:
                copy.start()
            return 0
        lax.fori_loop(begin, end, body, 0)
        rows = pl.ds((end - 1) * 256, 256)
        for copy in (pltpu.make_async_copy(st1, dw1_ref.at[rows, :], out_sem.at[0]),
                     pltpu.make_async_copy(st3, dw3_ref.at[rows, :], out_sem.at[1]),
                     pltpu.make_async_copy(st2, dw2_ref.at[:, rows], out_sem.at[2])):
            copy.wait()

    fetch(0).start()
    greet(other)
    do_gather = Gather(lambda d: dout_ref.at[tok_of(d), :], do_send, do_recv, where, own=dout_own)
    do_gather.start()
    own_in.wait()
    own_out = pltpu.make_async_copy(dh_own, dout_ref.at[tok_of(me), :], own_sem.at[1])
    own_out.start()
    for copy in loads:
        copy.wait()

    def out_step(step, _):
        @pl.when(step >= 2)
        def _():
            out_round.to_partner(step - 2).wait_send()
        out_round.step(step, prepare_out, add_mlp_out)

        @pl.when(step == 0)
        def _():
            out_round.mail(0).start()

        @pl.when(step == 2)
        def _():
            out_round.mail(1).start()
            do_gather.got_first()
            do_gather.got_second()
        return 0
    lax.fori_loop(0, 4, out_step, 0)
    out_round.pass_on()
    out_round.mail(2).start()
    for step in (2, 3):
        out_round.to_partner(step).wait_send()
    out_round.mail(0).wait_send()
    signal(0, partner)
    signal(1, first)
    do_gather.got_diag()
    for i in range(4):
        do_gather.got_partner(i)
    own_out.wait()
    fetch_dout(0).start()

    def grad_block(d, _):
        @pl.when(d < 7)
        def _():
            fetch_dout(d + 1).start()
        fetch_dout(d).wait()
        activation_grads(lax.rem(d, 2), tok_of(d))
        return 0
    lax.fori_loop(0, 8, grad_block, 0)

    pl.semaphore_wait(credit.at[0], 1)
    grad_round.step(0, lambda half: None, add_mlp_grad)
    pl.semaphore_wait(credit.at[1], 1)
    grad_round.mail(0).start()
    weight_grads(0, 2)
    out_round.mail(1).wait_recv()
    out_round.mail(2).wait_recv()

    def layer_out(k, _):
        part = pl.ds(pl.multiple_of(k * 16, 16), 16)
        y_ref[part, :] = (h_ref[part, :].astype(F32) + (chip_sum[0, part, :] + inbox[1, part, :] + inbox[2, part, :])).astype(BF16)
        return 0
    lax.fori_loop(0, tokens // 16, layer_out, 0)
    y_store = pltpu.make_async_copy(y_ref, y_hbm, own_sem.at[2])
    y_store.start()
    out_round.mail(1).wait_send()
    out_round.mail(2).wait_send()
    signal(2, partner)
    signal(3, first)
    signal(4, second)
    pl.semaphore_wait(credit.at[2], 1)

    def grad_step(step, _):
        @pl.when(step >= 2)
        def _():
            grad_round.to_partner(step - 2).wait_send()
        grad_round.step(step, lambda half: None, add_mlp_grad)

        @pl.when(step == 2)
        def _():
            pl.semaphore_wait(credit.at[3], 1)
            grad_round.mail(1).start()
            grad_round.pass_on()
            pl.semaphore_wait(credit.at[4], 1)
            grad_round.mail(2).start()
        return 0
    lax.fori_loop(1, 4, grad_step, 0)
    weight_grads(2, 8)
    grad_round.mail(1).wait_recv()
    grad_round.mail(2).wait_recv()
    dg2_ref[...] = jnp.zeros_like(dg2_ref)

    def hidden_grad(k, _):
        part = pl.ds(pl.multiple_of(k * 16, 16), 16)
        d_mlp = (chip_sum[0, part, :] + inbox[1, part, :] + inbox[2, part, :]).astype(BF16).astype(F32)
        d_norm, d_gain = norm_backward(h_ref[part, :].astype(F32), g_ref[1:2, :], d_mlp)
        dh_own[part, :] = (dh_own[part, :].astype(F32) + d_norm).astype(BF16)
        dg2_ref[...] += d_gain
        return 0
    lax.fori_loop(0, tokens // 16, hidden_grad, 0)
    own_out = pltpu.make_async_copy(dh_own, dh_hbm, own_sem.at[3])
    own_out.start()
    dg2_store = pltpu.make_async_copy(dg2_ref, dg2_hbm, own_sem.at[4])
    dg2_store.start()
    for step in (2, 3):
        grad_round.to_partner(step).wait_send()
    for kind in range(3):
        grad_round.mail(kind).wait_send()
    do_gather.drain()
    own_out.wait()
    y_store.wait()
    dg2_store.wait()


def mlp_step(m_all, d_out, w1, w3, w2, hidden, gains):
    seq_len, model = m_all.shape
    hid, tokens = w1.shape[1], hidden.shape[0]
    shape = jax.ShapeDtypeStruct
    hbm = pl.BlockSpec(memory_space=pl.ANY)
    dma = pltpu.SemaphoreType.DMA
    vm = lambda *dims, dtype=BF16: pltpu.VMEM(dims, dtype)
    return pl.pallas_call(
        functools.partial(mlp_comm_kernel, 'sp'), name='mlp_comm',
        in_specs=[hbm] * 7, out_specs=[hbm] * 7,
        out_shape=[shape((model, hid), F32), shape((model, hid), F32), shape((hid, model), F32),
                   shape(hidden.shape, BF16), shape(hidden.shape, BF16), shape((1, model), F32), shape((seq_len, model), BF16)],
        scratch_shapes=[vm(*t.shape, dtype=t.dtype) for t in (w1, w3, w2, hidden, gains)] + [
            vm(tokens, model), vm(1, model, dtype=F32),
            vm(seq_len, hid), vm(seq_len, hid), vm(seq_len, hid),
            vm(2, tokens, model, dtype=F32), vm(4, tokens, model, dtype=F32), vm(3, tokens, model, dtype=F32),
            vm(2, tokens, model), vm(seq_len, 256), vm(seq_len, 256), vm(256, seq_len), vm(256, seq_len),
            vm(256, hid, dtype=F32), vm(256, hid, dtype=F32), vm(hid, 256, dtype=F32), vm(tokens, model),
            dma((2, 4)), dma((2, 4)), dma((2, 3)), dma((2, 3)), dma((7,)), dma((7,)),
            dma((2,)), dma((2,)), dma((3,)), dma((5,)), dma((5,)), pltpu.SemaphoreType.REGULAR((5,))],
        compiler_params=pltpu.CompilerParams(collective_id=1, has_side_effects=True, vmem_limit_bytes=63 * 1024 * 1024),
    )(m_all, d_out, w1, w3, w2, hidden, gains)[:6]


def spread_tables(packed, upper):
    lanes = lax.broadcasted_iota(jnp.int32, packed.shape, 1)
    swapped = pltpu.roll(packed, 64, 1)
    both = jnp.where((lanes < 64) != upper, packed, swapped)
    low = lax.rem(lanes, 64) < 32
    return jnp.where(low, both, pltpu.roll(both, 32, 1)), jnp.where(low, -pltpu.roll(both, 96, 1), both)


def attention_comm_kernel(axis, heads, x_ref, ang_hbm, gain_ref, wq_ref, wk_ref, wv_ref, wo_ref, wg_ref, wu_ref,
                          q_hbm, k_hbm, v_hbm, ot_hbm, ut_hbm, cos_hbm, sin_hbm, gfull_hbm, h_hbm, m_ref, w1_ref, w3_ref,
                          q_ref, k_ref, v_ref, ot_ref, ut_ref, cos_ref, sin_ref, gfull_ref, h_ref, ang_ref, tab_ref, x_all, tab_all, gain_all, w_head, wo_all, o_all, u_blk, qkv_blk, o_scr, o_own, h_scr, m_out, stage,
                          g_send, g_recv, w_send, w_recv, x_send, x_recv, t_send, t_recv, wo_send, wo_recv, bulk_send, bulk_recv,
                          o_send, o_recv, m_loc, m_send, m_recv, loc_sem, own_sem, st_sem):
    ang_load = pltpu.make_async_copy(ang_hbm, ang_ref, own_sem.at[7])
    ang_load.start()
    where = place(axis)
    me, other, first, second = where
    core = lax.rem(me, 2)
    partner = other(1, 0, 0)
    greet(other)
    tokens, model = x_ref.shape
    seq_len, head_dim = k_ref.shape
    qw = heads * head_dim
    rows_own, hid = wg_ref.shape[0], w1_ref.shape[1]
    tok_of = lambda d: pl.ds(pl.multiple_of(d * tokens, tokens), tokens)
    cols_of = lambda d: pl.ds(pl.multiple_of(d * rows_own, rows_own), rows_own)
    hid_of = lambda d: pl.ds(pl.multiple_of(d * hid, hid), hid)
    peers = [other(r & 1, (r >> 1) & 1, r >> 2) for r in (6, 2, 4, 7, 3, 5, 1)]

    def to_all(src_of, dst, send_sem, recv_sem):
        return [pltpu.make_async_remote_copy(
            src_ref=src_of(dest), dst_ref=dst, send_sem=send_sem.at[n], recv_sem=recv_sem.at[n],
            device_id=(dest,), device_id_type=MESH) for n, dest in enumerate(peers)]

    small = to_all(lambda dest: gain_ref, gain_all.at[me], g_send, g_recv)
    q_of = lambda d: pl.ds(pl.multiple_of(d * qw, qw), qw)
    kv_of = lambda d: pl.ds(pl.multiple_of(d * head_dim, head_dim), head_dim)
    slices = (to_all(lambda dest: wq_ref.at[q_of(dest), :], w_head.at[0:qw, cols_of(me)], w_send.at[0], w_recv.at[0])
              + to_all(lambda dest: wk_ref.at[kv_of(dest), :], w_head.at[qw:qw + head_dim, cols_of(me)], w_send.at[1], w_recv.at[1])
              + to_all(lambda dest: wv_ref.at[kv_of(dest), :], w_head.at[qw + head_dim:, cols_of(me)], w_send.at[2], w_recv.at[2]))
    for copy in small + slices:
        copy.start()
    tab_slot = lambda d: tab_all.at[d]
    x_gather = Gather(lambda d: x_all.at[tok_of(d), :], x_send, x_recv, where, own=x_ref)
    t_gather = Gather(tab_slot, t_send, t_recv, where, own=tab_ref)
    x_gather.start()
    ang_load.wait()
    low = lax.rem(lax.broadcasted_iota(jnp.int32, ang_ref.shape, 1), head_dim) < head_dim // 2
    tab_ref[...] = jnp.where(low, jnp.cos(ang_ref[...]), jnp.sin(ang_ref[...]))
    t_gather.start()
    wo_gather = Gather(lambda d: wo_all.at[cols_of(d), :], wo_send, wo_recv, where, own=wo_ref)
    bulk = []
    part_rows = rows_own // 4
    for part in range(8):
        src, dst = ((wg_ref, w1_ref), (wu_ref, w3_ref))[part // 4]
        low = (part % 4) * part_rows
        for n, dest in enumerate(peers):
            bulk.append(pltpu.make_async_remote_copy(
                src_ref=src.at[pl.ds(low, part_rows), hid_of(dest)],
                dst_ref=dst.at[pl.ds(pl.multiple_of(me * rows_own + low, part_rows), part_rows), :],
                send_sem=bulk_send.at[part * 7 + n], recv_sem=bulk_recv.at[part * 7 + n], device_id=(dest,), device_id_type=MESH))

    def start_bulk(*parts):
        for part in parts:
            for copy in bulk[part * 7:part * 7 + 7]:
                copy.start()

    stores = [pltpu.make_async_copy(src, dst, st_sem.at[i]) for i, (src, dst) in enumerate((
        (q_ref, q_hbm), (k_ref, k_hbm), (v_ref, v_hbm), (ot_ref, ot_hbm), (ut_ref, ut_hbm), (cos_ref, cos_hbm),
        (sin_ref, sin_hbm), (gfull_ref, gfull_hbm), (h_ref, h_hbm)))]
    own = [pltpu.make_async_copy(src, dst, own_sem.at[i]) for i, (src, dst) in enumerate((
        (gain_ref, gain_all.at[me]), (wq_ref.at[q_of(me), :], w_head.at[0:qw, cols_of(me)]),
        (wk_ref.at[kv_of(me), :], w_head.at[qw:qw + head_dim, cols_of(me)]),
        (wv_ref.at[kv_of(me), :], w_head.at[qw + head_dim:, cols_of(me)]),
        (x_ref, x_all.at[tok_of(me), :]), (wo_ref, wo_all.at[cols_of(me), :])))]
    for copy in own:
        copy.start()
    local = []
    for i, (src, dst) in enumerate(((wg_ref, w1_ref), (wu_ref, w3_ref))):
        local.append((pltpu.make_async_copy(src.at[:, hid_of(me)], stage.at[i], loc_sem.at[i]),
                      pltpu.make_async_copy(stage.at[i], dst.at[cols_of(me), :], loc_sem.at[2 + i])))
        local[-1][0].start()
    tab_all[me] = tab_ref[...]
    for load, store in local:
        load.wait()
        store.start()
    for copy in own:
        copy.wait()
    for copy in small:
        copy.wait_recv()
    for d in range(8):
        gfull_ref[:, d * rows_own:(d + 1) * rows_own] = gain_all[d]
    for copy in slices:
        copy.wait_recv()

    def use(d):
        base = pl.multiple_of(d * tokens, tokens)

        def norm(k, _):
            part = pl.ds(pl.multiple_of(k * 16, 16), 16)
            x_part = x_all[pl.ds(pl.multiple_of(base + k * 16, 16), 16), :].astype(F32)
            u_blk[part, :] = norm_forward(x_part, gfull_ref[0:1, :]).astype(BF16)
            return 0
        lax.fori_loop(0, tokens // 16, norm, 0)
        ut_ref[:, tok_of(d)] = u_blk[:, cols_of(me)].T
        qkv_blk[...] = dot(u_blk[...], w_head[...], 1, 1).astype(BF16)
        half = tokens // 2
        for part in range(2):
            rows = pl.ds(pl.multiple_of(base + part * half, half), half)
            cos_blk, sin_blk = spread_tables(tab_all[d], part == 1)
            cos_ref[rows, :] = cos_blk
            sin_ref[rows, :] = sin_blk
            source = slice(part * half, (part + 1) * half)
            for pair in range(heads // 2):
                turned = turn_halves(qkv_blk[source, pair * 128:(pair + 1) * 128].astype(F32), cos_blk, sin_blk).astype(BF16)
                q_ref[2 * pair, rows, :] = turned[:, :head_dim]
                q_ref[2 * pair + 1, rows, :] = turned[:, head_dim:]
            turned = turn_halves(qkv_blk[source, qw:].astype(F32), cos_blk, sin_blk).astype(BF16)
            k_ref[rows, :] = turned[:, :head_dim]
            v_ref[rows, :] = qkv_blk[source, qw + head_dim:]

    x_gather.got_first()
    t_gather.got_first()
    x_gather.got_second()
    t_gather.got_second()
    wo_gather.start()
    start_bulk(0, 1)
    x_gather.got_partner(0)
    t_gather.got_partner(0)

    def use_near(i, _):
        use(jnp.where(i == 0, me, jnp.where(i == 1, first, jnp.where(i == 2, second, partner))))
        return 0
    lax.fori_loop(0, 4, use_near, 0)
    x_gather.got_diag()
    t_gather.got_diag()
    for i in range(1, 4):
        x_gather.got_partner(i)
        t_gather.got_partner(i)

    def use_far(i, _):
        use(jnp.where(i == 0, other(0, 1, 1), jnp.where(i == 1, other(1, 1, 0), jnp.where(i == 2, other(1, 0, 1), other(1, 1, 1)))))
        return 0
    lax.fori_loop(0, 4, use_far, 0)

    def one_head(h, _):
        for start in range(0, seq_len, BLK):
            keys, rows = pl.ds(0, start + BLK), pl.ds(start, BLK)
            probs = probs_transposed(k_ref[keys, :], q_ref[h, rows, :], start)
            o_scr[h, rows, :] = dot(probs.astype(BF16), v_ref[keys, :], 0, 0).astype(BF16)
        return 0
    for i in (0, 1, 2, 4, 5, 6, 7):
        stores[i].start()
    lax.fori_loop(0, heads, one_head, 0)
    for h in range(heads):
        o_own[:, h * head_dim:(h + 1) * head_dim] = o_scr[h]
    o_gather = Gather(lambda d: o_all.at[:, cols_of(d)], o_send, o_recv, where, own=o_own)
    o_gather.start()
    wo_gather.got_first()
    wo_gather.got_second()
    start_bulk(2)
    o_all[:, cols_of(me)] = o_own[...]

    def turn_out(k, _):
        rows = tok_of(k)
        ot_ref[:, rows] = o_own[rows, :].T
        return 0
    lax.fori_loop(0, 8, turn_out, 0)
    stores[3].start()
    wo_gather.got_diag()
    for i in range(4):
        wo_gather.got_partner(i)
    o_gather.got_first()
    o_gather.got_second()
    start_bulk(3)
    o_gather.got_partner(0)
    o_gather.got_diag()
    for i in range(1, 4):
        o_gather.got_partner(i)
    start_bulk(4, 5, 6, 7)

    def rows_at(i):
        flips = lambda a, b: other(0, a, b)
        return tok_of(jnp.where(i == 0, me, jnp.where(i == 1, flips(1, 0), jnp.where(i == 2, flips(0, 1), flips(1, 1)))))

    def give(i):
        slot = lax.rem(i, 2)
        rows = rows_at(i)
        return (pltpu.make_async_copy(m_out.at[slot], m_ref.at[rows, :], m_loc.at[slot]),
                pltpu.make_async_remote_copy(src_ref=m_out.at[slot], dst_ref=m_ref.at[rows, :], send_sem=m_send.at[i],
                                             recv_sem=m_recv.at[i], device_id=(partner,), device_id_type=MESH))

    def hidden_block(i, _):
        rows = rows_at(i)
        base = rows.start
        slot = lax.rem(i, 2)

        @pl.when(i >= 2)
        def _():
            to_hbm, to_partner = give(i - 2)
            to_hbm.wait()
            to_partner.wait_send()

        def chunk(j, _):
            cols = pl.ds(pl.multiple_of(j * 256, 256), 256)
            h_scr[:, cols] = dot(o_all[rows, :], wo_all[:, cols], 1, 0)
            return 0
        lax.fori_loop(0, model // 256, chunk, 0)

        def norm(k, _):
            part = pl.ds(pl.multiple_of(k * 16, 16), 16)
            x_part = x_all[pl.ds(pl.multiple_of(base + k * 16, 16), 16), :].astype(F32)
            hidden = (x_part + h_scr[part, :]).astype(BF16)

            @pl.when(i == 0)
            def _():
                h_ref[part, :] = hidden
            m_out[slot, part, :] = norm_forward(hidden.astype(F32), gfull_ref[1:2, :]).astype(BF16)
            return 0
        lax.fori_loop(0, tokens // 16, norm, 0)
        for copy in give(i):
            copy.start()
        return 0
    lax.fori_loop(0, 4, hidden_block, 0)
    stores[8].start()
    for i in range(4):
        give(i)[1].wait_recv()
    for i in range(2, 4):
        give(i)[0].wait()
        give(i)[1].wait_send()
    for copy in small + slices:
        copy.wait_send()
    for gather in (x_gather, t_gather, wo_gather, o_gather):
        gather.drain()
    for copy in bulk:
        copy.wait()
    for load, store in local:
        store.wait()
    for copy in stores:
        copy.wait()


def attention_step(heads, x_in, angles, gains, w_q, w_k, w_v, wo_own, w_gate, w_up):
    tokens, model = x_in.shape
    seq_len = 8 * tokens
    head_dim = wo_own.shape[0] // heads
    rows_own, hid = w_gate.shape[0], w_gate.shape[1] // 8
    shape = jax.ShapeDtypeStruct
    hbm = pl.BlockSpec(memory_space=pl.ANY)
    dma = pltpu.SemaphoreType.DMA
    vm = lambda *dims, dtype=BF16: pltpu.VMEM(dims, dtype)
    outs = (shape((heads, seq_len, head_dim), BF16), shape((seq_len, head_dim), BF16), shape((seq_len, head_dim), BF16),
            shape((heads * head_dim, seq_len), BF16), shape((rows_own, seq_len), BF16),
            shape((seq_len, 128), F32), shape((seq_len, 128), F32), shape((8, model), F32), shape((tokens, model), BF16))
    pairs = [dma((7,)), dma((7,)), dma((3, 7)), dma((3, 7)), dma((7,)), dma((7,)), dma((7,)), dma((7,)), dma((7,)), dma((7,)),
             dma((56,)), dma((56,)), dma((7,)), dma((7,))]
    return pl.pallas_call(
        functools.partial(attention_comm_kernel, 'sp', heads), name='attention_comm',
        in_specs=[hbm] * 9, out_specs=[hbm] * 12,
        out_shape=[*outs, shape((seq_len, model), BF16), shape((model, hid), BF16), shape((model, hid), BF16)],
        scratch_shapes=[vm(*t.shape, dtype=t.dtype) for t in outs] + [
            vm(tokens // 2, 128, dtype=F32), vm(tokens // 2, 128, dtype=F32), vm(seq_len, model), vm(8, tokens // 2, 128, dtype=F32), vm(8, 8, rows_own, dtype=F32),
            vm(384, model), vm(model, model), vm(seq_len, model), vm(tokens, model), vm(tokens, 384), vm(heads, seq_len, head_dim),
            vm(seq_len, heads * head_dim), vm(tokens, model, dtype=F32), vm(2, tokens, model), vm(2, rows_own, hid)] + pairs + [
            dma((2,)), dma((4,)), dma((4,)), dma((4,)), dma((8,)), dma((9,))],
        compiler_params=pltpu.CompilerParams(collective_id=0, has_side_effects=True, vmem_limit_bytes=63 * 1024 * 1024),
    )(x_in, angles, gains, w_q, w_k, w_v, wo_own, w_gate, w_up)


def hand_over_kernel(plan, *refs):
    n_in = len(plan)
    sources, gains, results = refs[:n_in], refs[n_in], refs[n_in + 1:2 * n_in + 1]
    gain_outs, stages = refs[2 * n_in + 1:2 * n_in + 3], refs[2 * n_in + 3:3 * n_in + 3]
    in_sem, out_sem = refs[3 * n_in + 3:]
    pieces, count = [], 0
    for src, stage, dst, parts in zip(sources, stages, results, plan):
        rows = src.shape[0] // parts
        for p in range(parts):
            part = pl.ds(p * rows, rows)
            pieces.append((pltpu.make_async_copy(src.at[part], stage.at[part], in_sem.at[count]),
                           pltpu.make_async_copy(stage.at[part], dst.at[part], out_sem.at[count])))
            count += 1
    for load, _ in pieces:
        load.start()
    for i in range(2):
        gain_outs[i][...] = gains[i, :]
    for load, store in pieces:
        load.wait()
        store.start()
    for _, store in pieces:
        store.wait()


def hand_over(arrays, gains):
    shape = jax.ShapeDtypeStruct
    plan = tuple(max(1, a.size * a.dtype.itemsize // (1 << 20)) for a in arrays)
    hbm, vmem = pl.BlockSpec(memory_space=pl.ANY), pl.BlockSpec(memory_space=pltpu.VMEM)
    dma = pltpu.SemaphoreType.DMA
    out = pl.pallas_call(
        functools.partial(hand_over_kernel, plan), name='hand_over',
        in_specs=[hbm] * len(arrays) + [vmem], out_specs=[hbm] * len(arrays) + [vmem] * 2,
        out_shape=[shape(a.shape, a.dtype) for a in arrays] + [shape((gains.shape[1],), F32)] * 2,
        scratch_shapes=[pltpu.VMEM(a.shape, a.dtype) for a in arrays] + [dma((sum(plan),)), dma((sum(plan),))],
        compiler_params=pltpu.CompilerParams(vmem_limit_bytes=63 * 1024 * 1024),
    )(*arrays, gains)
    return out


def solution(mesh):
    n_dev = mesh.shape['sp']

    def layer_step(x_in, positions, d_out, norm1_gain, norm2_gain, w_q, w_k, w_v, w_o, w_gate, w_up, w_down):
        tokens, model = x_in.shape
        head_dim = w_q.shape[2]
        heads = w_q.shape[1] // n_dev
        rows_own = w_q.shape[0]
        inv_freq = 1.0 / (ROPE_BASE ** (jnp.arange(head_dim // 2, dtype=F32) * (2.0 / head_dim)))
        half = tokens // 2
        lane = jnp.arange(4 * head_dim // 2)
        turn = jnp.where((lane < head_dim)[None, :], positions[:half, None], positions[half:, None])
        angles = turn.astype(F32) * jnp.tile(inv_freq, 4)[None, :]
        row = jnp.arange(8)[:, None]
        gains = jnp.where(row == 0, norm1_gain[None].astype(F32), jnp.where(row == 1, norm2_gain[None].astype(F32), 0.0))
        flat = lambda w: w.transpose(1, 2, 0).reshape(-1, rows_own)
        wo_own = w_o.reshape(-1, model)
        (q_rot, k_rot, v_lin, o_t, u_t, cos_tab, sin_tab, g_full, hidden,
         mlp_in, w1, w3) = attention_step(heads, x_in, angles, gains, flat(w_q), flat(w_k), flat(w_v), wo_own, w_gate, w_up)
        d_w1s, d_w3s, d_down, y_out, dh_own, d_g2 = mlp_step(mlp_in, d_out, w1, w3, w_down, hidden, g_full)
        d_wo, d_wq_t, d_wk_t, d_wv_t, d_w1, d_w3, d_x, d_gains = attention_backward_step(
            heads, dh_own, wo_own, o_t, q_rot, k_rot, v_lin, (cos_tab, sin_tab),
            d_w1s, d_w3s, flat(w_q), flat(w_k), flat(w_v), u_t, x_in, g_full, d_g2)
        from_cols = lambda d, w: d.reshape(w.shape[1], w.shape[2], rows_own).transpose(2, 0, 1)
        (d_w1, d_w3, d_down, d_wo, d_wq_t, d_wk_t, d_wv_t, y_out, d_x, d_g1, d_g2) = hand_over(
            (d_w1, d_w3, d_down, d_wo, d_wq_t, d_wk_t, d_wv_t, y_out, d_x), d_gains)
        return (y_out, d_x, d_g1, d_g2, from_cols(d_wq_t, w_q), from_cols(d_wk_t, w_k), from_cols(d_wv_t, w_v),
                d_wo.reshape(w_o.shape), d_w1, d_w3, d_down)

    all_rows = P('sp')
    return jax.shard_map(layer_step, mesh=mesh, in_specs=(all_rows,) * 12, out_specs=(all_rows,) * 11, check_vma=False)
```

time: 798 us -> 712 us (0.89)
  Pallas kernels: 759 us -> 707 us
  local copies, waits for them, and re-layouts: 28.2 us -> 0.84 us
    pallas_call x1, Pallas kernels: 225 us -> 179 us  [mlp_step(): pl.pallas_call(functools.partial(mlp_comm_kernel, 'sp'), name='mlp_comm',...]
    pallas_call x1, Pallas kernels: 265 us -> 221 us  [attention_step(): pl.pallas_call(functools.partial(attention_comm_kernel, 'sp', heads), nam...]
    unnamed x27 -> x0, local copies, waits for them, and re-layouts: 26.1 us -> none
    pallas_call x0 -> x1, Pallas kernels: none -> 24 us  [hand_over(): pl.pallas_call(functools.partial(hand_over_kernel, plan), name='hand_over...]
    pallas_call x1, Pallas kernels: 270 us -> 283 us  [attention_backward_step(): pl.pallas_call(functools.partial(attn_bwd_comm_kernel, 'sp', heads), name...]
where the time goes in v5:
time: 712 us; the launch traced here: 711 us
  Pallas kernels  707 us (99%)
    pallas_call x1, Pallas kernels, attention_backward_step(): pl.pallas_call(functools.partial(attn_bwd_comm_kernel, 'sp', heads), name...  283 us
    pallas_call x1, Pallas kernels, attention_step(): pl.pallas_call(functools.partial(attention_comm_kernel, 'sp', heads), nam...  221 us
    pallas_call x1, Pallas kernels, mlp_step(): pl.pallas_call(functools.partial(mlp_comm_kernel, 'sp'), name='mlp_comm',...  179 us
    pallas_call x1, Pallas kernels, hand_over(): pl.pallas_call(functools.partial(hand_over_kernel, plan), name='hand_over...  24 us

profile of v5, /device:TPU:0, one launch (start us, length us, event | category | flops | bytes accessed | tf_op | source)
XLA Modules:
  0.0 711.5 jit_solution(5774705413920252902)
XLA Ops:
  0.7 0.7 convert_element_type.12
  1.3 0.7 convert_element_type.13
  2.0 0.8 fusion
  2.8 0.1 mul.22
  2.8 0.7 select_select_fusion.gain_ref
  3.5 0.7 convert_multiply_fusion.ang_hbm
  4.2 220.7 %attention_comm.1 = (bf16[4,2048,64]{2,1,0:T(8,128)(2,1)}, bf16[2048,64]{1,0:T(8,128)(2,1)}, bf16[2048,64]{1,0:T(8,128)(2,1)}, bf16[256,2048]{1,0:T(8,128)(2,1)}...) custom-call(bf16[256,2048]{1,0:T(8,128)(2,1)} %x_hbm.1, ...), custom_call_target="tpu_custom_call" | custom-call | tf_op jit(solution)/shard_map/attention_comm/pallas_call | solution.py:932
  225.0 179.1 %mlp_comm.1 = (f32[2048,1024]{1,0:T(8,128)}, f32[2048,1024]{1,0:T(8,128)}, f32[1024,2048]{1,0:T(8,128)}, bf16[256,2048]{1,0:T(8,128)(2,1)}, bf16[256,2048]{1,0:T...) custom-call(bf16[2048,2048]{1,0:T(8,128)(2,1)} %get-tuple-element.48.m_ref, bf16[256,2048]{1,0:T(8,128)(2,1)} %dout_own.1, ...), custom_call_target="tpu_custom_call" | custom-call | tf_op jit(solution)/shard_map/mlp_comm/pallas_call | solution.py:659
  404.1 283.2 %attn_bwd_comm.1 = (f32[256,2048]{1,0:T(8,128)}, f32[2048,256]{1,0:T(8,128)}, f32[512,256]{1,0:T(8,128)}, f32[512,256]{1,0:T(8,128)}, f32[256,8192]{1,0:T(8,128)...) custom-call(bf16[256,2048]{1,0:T(8,128)(2,1)} %get-tuple-element.53.dh_hbm, ...), custom_call_target="tpu_custom_call" | custom-call | tf_op jit(solution)/shard_map/attn_bwd_comm/pallas_call | solution.py:331
  687.3 24.0 %hand_over.1 = (f32[256,8192]{1,0:T(8,128)}, f32[256,8192]{1,0:T(8,128)}, f32[1024,2048]{1,0:T(8,128)}, f32[256,2048]{1,0:T(8,128)}, f32[2048,256]{1,0:T(8,128)}...) custom-call(f32[256,8192]{1,0:T(8,128)} %get-tuple-element.64.refs_0, ...), custom_call_target="tpu_custom_call" | custom-call | tf_op jit(solution)/shard_map/hand_over/pallas_call | solution.py:974
  (4 shorter events, 0.0 us)

commit v6 on v5

--- a/solution.py
+++ b/solution.py
@@ -1,6 +1,7 @@
 import functools
 import jax
 import jax.numpy as jnp
+import numpy as np
 from jax import lax
 from jax.experimental import pallas as pl
 from jax.experimental.pallas import tpu as pltpu
@@ -114,17 +115,16 @@
 
 def attn_bwd_comm_kernel(axis, heads, dh_hbm, wo_hbm, ot_hbm, q_hbm, k_hbm, v_hbm, cos_hbm, sin_hbm,
                          dw1_ref, dw3_ref, wq_hbm, wk_hbm, wv_hbm, ut_hbm, x_hbm, g_hbm, dg2_hbm,
-                         dwo_hbm, dwq_hbm, dwk_hbm, dwv_hbm, out1_ref, out3_ref, dx_hbm, dg_hbm,
-                         dh_ref, wo_ref, ot_ref, q_ref, k_ref, v_ref, cos_ref, sin_ref, wq_ref, wk_ref, wv_ref, ut_ref, x_ref, g_ref, dg2_ref,
-                         dwo_ref, dwq_ref, dwk_ref, dwv_ref, dx_ref, dg_ref,
-                         slots, do_scr, dq_scr, dg_own, dg_all, dk_acc, dv_acc, du_acc, du_scr, du_recv, stage,
-                         bulk_send, bulk_recv, hg_send, hg_recv, gat_send, gat_recv, du_send, du_rsem, dg_send, dg_recv, loc_sem, ld_sem, st_sem):
+                         dwo_ref, dwq_ref, dwk_ref, dwv_ref, out1_ref, out3_ref, dx_ref, dg_ref,
+                         dh_ref, wo_ref, ot_ref, q_ref, k_ref, v_ref, cos_ref, sin_ref, wq_ref, wk_ref, wv_ref, ut_ref, g_ref, dg2_ref,
+                         slots, do_scr, dg_own, dg_all, dk_acc, dv_acc, du_acc, du_scr,
+                         bulk_send, bulk_recv, hg_send, hg_recv, gat_send, gat_recv, du_send, du_rsem, dg_send, dg_recv, loc_sem, ld_sem):
     loads = {}
     for i, (name, src, dst) in enumerate((
             ('wo', wo_hbm, wo_ref), ('ot', ot_hbm, ot_ref), ('q', q_hbm, q_ref), ('k', k_hbm, k_ref),
             ('v', v_hbm, v_ref), ('cos', cos_hbm, cos_ref), ('sin', sin_hbm, sin_ref), ('wq', wq_hbm, wq_ref), ('wk', wk_hbm, wk_ref),
-            ('wv', wv_hbm, wv_ref), ('ut', ut_hbm, ut_ref), ('x', x_hbm, x_ref), ('g', g_hbm, g_ref), ('dg2', dg2_hbm, dg2_ref),
-            ('dh', dh_hbm, dh_ref.at[pl.ds(pl.multiple_of(lax.axis_index(axis) * x_ref.shape[0], x_ref.shape[0]), x_ref.shape[0]), :]))):
+            ('wv', wv_hbm, wv_ref), ('ut', ut_hbm, ut_ref), ('g', g_hbm, g_ref), ('dg2', dg2_hbm, dg2_ref),
+            ('dh', dh_hbm, dh_ref.at[pl.ds(pl.multiple_of(lax.axis_index(axis) * x_hbm.shape[0], x_hbm.shape[0]), x_hbm.shape[0]), :]))):
         loads[name] = pltpu.make_async_copy(src, dst, ld_sem.at[i])
         loads[name].start()
 
@@ -132,14 +132,12 @@
         for name in names:
             loads[name].wait()
 
-    stores = [pltpu.make_async_copy(src, dst, st_sem.at[i]) for i, (src, dst) in enumerate((
-        (dwo_ref, dwo_hbm), (dwq_ref, dwq_hbm), (dwk_ref, dwk_hbm), (dwv_ref, dwv_hbm), (dx_ref, dx_hbm), (dg_ref, dg_hbm)))]
     where = place(axis)
     me, other, first, second = where
     greet(other)
     seq_len, head_dim = k_ref.shape
-    rows_own, hid = stage.shape[1], stage.shape[2]
-    tokens = x_ref.shape[0]
+    rows_own, hid = out1_ref.shape[0], dw1_ref.shape[1]
+    tokens = x_hbm.shape[0]
     qw = heads * head_dim
     half_rows = rows_own // 2
 
@@ -163,8 +161,9 @@
     tok_of = lambda d: pl.ds(pl.multiple_of(d * tokens, tokens), tokens)
     h_gather = Gather(lambda d: dh_ref.at[tok_of(d), :], hg_send, hg_recv, where, own=dh_hbm)
     h_gather.start()
-    for i, (src, dst) in enumerate(pairs):
-        pltpu.make_async_copy(src.at[rows_of(me), :], stage.at[i], loc_sem.at[i]).start()
+    local = [pltpu.make_async_copy(src.at[rows_of(me), :], dst.at[:, hid_of(me)], loc_sem.at[i]) for i, (src, dst) in enumerate(pairs)]
+    for copy in local:
+        copy.start()
     need('dh', 'wo', 'ot')
     h_gather.got_first()
     h_gather.got_second()
@@ -183,11 +182,10 @@
         dwo_ref[:, cols] = dot(ot_ref[...], dh_ref[:, cols], 1, 0)
         return 0
     lax.fori_loop(0, seq_len // BLK, split_out_grad, 0)
-    stores[0].start()
-
-    for i, (src, dst) in enumerate(pairs):
-        pltpu.make_async_copy(src.at[rows_of(me), :], stage.at[i], loc_sem.at[i]).wait()
-        pltpu.make_async_copy(stage.at[i], dst.at[:, hid_of(me)], loc_sem.at[2 + i]).start()
+    x_ref = wo_ref
+    x_load = pltpu.make_async_copy(x_hbm, x_ref, ld_sem.at[14])
+    x_load.start()
+
 
     need('q', 'k', 'v')
     dk_acc[...] = jnp.zeros_like(dk_acc)
@@ -203,7 +201,7 @@
             d_probs = dot(v_ref[keys, :], do_blk, 1, 1).astype(BF16).astype(F32)
             row_dot = jnp.sum(d_probs * probs, axis=0, keepdims=True)
             d_scores = (probs * (d_probs - row_dot) * (head_dim ** -0.5)).astype(BF16)
-            dq_scr[h, rows, :] = dot(d_scores, k_ref[keys, :], 0, 0).astype(BF16)
+            do_scr[h, rows, :] = dot(d_scores, k_ref[keys, :], 0, 0).astype(BF16)
             dk_acc[keys, :] += dot(d_scores, q_blk, 1, 0)
             dv_acc[keys, :] += dot(probs.astype(BF16), do_blk, 1, 0)
         for start in range(0, seq_len, BLK):
@@ -219,7 +217,7 @@
         rows = pl.ds(pl.multiple_of(k * BLK, BLK), BLK)
         cos_blk, sin_blk = cos_ref[rows, :], -sin_ref[rows, :]
         for pair in range(heads // 2):
-            both = jnp.concatenate([dq_scr[2 * pair, rows, :], dq_scr[2 * pair + 1, rows, :]], axis=1)
+            both = jnp.concatenate([do_scr[2 * pair, rows, :], do_scr[2 * pair + 1, rows, :]], axis=1)
             mine[rows, pair * 128:(pair + 1) * 128] = turn_halves(both.astype(F32), cos_blk, sin_blk).astype(BF16)
         kv = mine[rows, qw:].astype(F32)
         mine[rows, qw:] = jnp.where(low, turn_halves(kv, cos_blk, sin_blk), kv).astype(BF16)
@@ -266,18 +264,16 @@
         gather.got_partner(i)
     use_many(other(0, 1, 1), other(1, 1, 0), other(1, 0, 1), other(1, 1, 1))
     du_scr[...] = du_acc[...].astype(BF16)
-    for i in range(1, 4):
-        stores[i].start()
-
     sends = []
     for n, dest in enumerate(peers):
         sends.append(pltpu.make_async_remote_copy(
-            src_ref=du_scr.at[tok_of(dest), :], dst_ref=du_recv.at[:, rows_of(me)], send_sem=du_send.at[n],
+            src_ref=du_scr.at[tok_of(dest), :], dst_ref=ot_ref.at[:, rows_of(me)], send_sem=du_send.at[n],
             recv_sem=du_rsem.at[n], device_id=(dest,), device_id_type=MESH))
         sends[-1].start()
     start_bulk(3)
-    du_recv[:, rows_of(me)] = du_scr[tok_of(me), :]
-    need('x', 'g', 'dg2')
+    ot_ref[:, rows_of(me)] = du_scr[tok_of(me), :]
+    need('g', 'dg2')
+    x_load.wait()
     for copy in sends:
         copy.wait_recv()
     dg_own[...] = jnp.zeros_like(dg_own)
@@ -285,13 +281,12 @@
 
     def input_grad(k, _):
         part = pl.ds(pl.multiple_of(k * 16, 16), 16)
-        d_norm, d_gain = norm_backward(x_ref[part, :].astype(F32), g_ref[0:1, :], du_recv[part, :].astype(F32))
+        d_norm, d_gain = norm_backward(x_ref[part, :].astype(F32), g_ref[0:1, :], ot_ref[part, :].astype(F32))
         dh_part = dh_ref[pl.ds(pl.multiple_of(me * tokens + k * 16, 16), 16), :]
         dx_ref[part, :] = (dh_part.astype(F32) + d_norm).astype(BF16)
         dg_own[0:1, :] += d_gain
         return 0
     lax.fori_loop(0, tokens // 16, input_grad, 0)
-    stores[4].start()
     gain_sends = []
     for n, dest in enumerate(peers):
         gain_sends.append(pltpu.make_async_remote_copy(
@@ -302,16 +297,13 @@
     for copy in gain_sends:
         copy.wait_recv()
     dg_ref[...] = jnp.sum(dg_all[...], axis=0)
-    stores[5].start()
     for copy in sends + gain_sends:
         copy.wait_send()
     gather.drain()
     h_gather.drain()
     for copy in bulk:
         copy.wait()
-    for i, (src, dst) in enumerate(pairs):
-        pltpu.make_async_copy(stage.at[i], dst.at[:, hid_of(me)], loc_sem.at[2 + i]).wait()
-    for copy in stores:
+    for copy in local:
         copy.wait()
 
 
@@ -326,19 +318,20 @@
     vm = lambda *dims, dtype=BF16: pltpu.VMEM(dims, dtype)
     early = (dh_own, wo_own, o_t, q_rot, k_rot, v_lin, *tables)
     late = (w_q, w_k, w_v, u_t, x_in, gains, d_g2)
-    outs = (shape(wo_own.shape, F32), shape(w_q.shape, F32), shape(w_k.shape, F32), shape(w_v.shape, F32))
-    ends = (shape(x_in.shape, BF16), shape((8, rows_own), F32))
+    outs = [(wo_own.shape, F32), (w_q.shape, F32), (w_k.shape, F32), (w_v.shape, F32), ((rows_own, 8 * hid), F32),
+            ((rows_own, 8 * hid), F32), (x_in.shape, BF16), ((8, rows_own), F32)]
+    vmem = pl.BlockSpec(memory_space=pltpu.VMEM)
     return pl.pallas_call(
         functools.partial(attn_bwd_comm_kernel, 'sp', heads), name='attn_bwd_comm',
-        in_specs=[hbm] * 17, out_specs=[hbm] * 8,
-        out_shape=[*outs, shape((rows_own, 8 * hid), F32), shape((rows_own, 8 * hid), F32), *ends],
-        scratch_shapes=[vm(seq_len, model)] + [vm(*t.shape, dtype=t.dtype) for t in early[1:] + late + outs + ends] + [
-            vm(8, seq_len, 384), vm(heads, seq_len, head_dim), vm(heads, seq_len, head_dim),
+        in_specs=[hbm] * 17, out_specs=[vmem] * 8,
+        out_shape=[pltpu.VMEM(dims, dtype) for dims, dtype in outs],
+        scratch_shapes=[vm(seq_len, model)] + [vm(*t.shape, dtype=t.dtype) for t in early[1:] + late[:4] + late[5:]] + [
+            vm(8, seq_len, 384), vm(heads, seq_len, head_dim),
             vm(8, model, dtype=F32), vm(8, 8, rows_own, dtype=F32),
             vm(seq_len, head_dim, dtype=F32), vm(seq_len, head_dim, dtype=F32),
-            vm(seq_len, rows_own, dtype=F32), vm(seq_len, rows_own), vm(tokens, model), vm(2, rows_own, hid, dtype=F32),
-            dma((28,)), dma((28,)), dma((7,)), dma((7,)), dma((7,)), dma((7,)), dma((7,)), dma((7,)), dma((7,)), dma((7,)), dma((4,)), dma((15,)), dma((6,))],
-        compiler_params=pltpu.CompilerParams(collective_id=2, has_side_effects=True, vmem_limit_bytes=63 * 1024 * 1024),
+            vm(seq_len, rows_own, dtype=F32), vm(seq_len, rows_own),
+            dma((28,)), dma((28,)), dma((7,)), dma((7,)), dma((7,)), dma((7,)), dma((7,)), dma((7,)), dma((7,)), dma((7,)), dma((2,)), dma((15,))],
+        compiler_params=pltpu.CompilerParams(collective_id=2, has_side_effects=True, vmem_limit_bytes=43515904),
     )(*early, d_w1, d_w3, *late)
 
 
@@ -681,13 +674,15 @@
     return jnp.where(low, both, pltpu.roll(both, 32, 1)), jnp.where(low, -pltpu.roll(both, 96, 1), both)
 
 
-def attention_comm_kernel(axis, heads, x_ref, ang_hbm, gain_ref, wq_ref, wk_ref, wv_ref, wo_ref, wg_ref, wu_ref,
+def attention_comm_kernel(axis, heads, x_ref, pos_ref, gain1_ref, gain2_ref, freq_ref, wq_ref, wk_ref, wv_ref, wo_ref, wg_ref, wu_ref,
                           q_hbm, k_hbm, v_hbm, ot_hbm, ut_hbm, cos_hbm, sin_hbm, gfull_hbm, h_hbm, m_ref, w1_ref, w3_ref,
-                          q_ref, k_ref, v_ref, ot_ref, ut_ref, cos_ref, sin_ref, gfull_ref, h_ref, ang_ref, tab_ref, x_all, tab_all, gain_all, w_head, wo_all, o_all, u_blk, qkv_blk, o_scr, o_own, h_scr, m_out, stage,
-                          g_send, g_recv, w_send, w_recv, x_send, x_recv, t_send, t_recv, wo_send, wo_recv, bulk_send, bulk_recv,
+                          q_ref, k_ref, v_ref, ot_ref, ut_ref, cos_ref, sin_ref, gfull_ref, h_ref, gain_ref, x_all, gain_all, w_head, wo_all, o_all, u_blk, qkv_blk, o_scr, o_own, h_scr, m_out, stage,
+                          g_send, g_recv, w_send, w_recv, x_send, x_recv, wo_send, wo_recv, bulk_send, bulk_recv,
                           o_send, o_recv, m_loc, m_send, m_recv, loc_sem, own_sem, st_sem):
-    ang_load = pltpu.make_async_copy(ang_hbm, ang_ref, own_sem.at[7])
-    ang_load.start()
+    gain_ref[...] = jnp.zeros_like(gain_ref)
+    gain_ref[0:1, :] = gain1_ref[...].astype(F32).reshape(1, -1)
+    gain_ref[1:2, :] = gain2_ref[...].astype(F32).reshape(1, -1)
+    gain_ref[2:3, :] = pos_ref[...].astype(F32).reshape(1, -1)
     where = place(axis)
     me, other, first, second = where
     core = lax.rem(me, 2)
@@ -715,14 +710,8 @@
               + to_all(lambda dest: wv_ref.at[kv_of(dest), :], w_head.at[qw + head_dim:, cols_of(me)], w_send.at[2], w_recv.at[2]))
     for copy in small + slices:
         copy.start()
-    tab_slot = lambda d: tab_all.at[d]
     x_gather = Gather(lambda d: x_all.at[tok_of(d), :], x_send, x_recv, where, own=x_ref)
-    t_gather = Gather(tab_slot, t_send, t_recv, where, own=tab_ref)
     x_gather.start()
-    ang_load.wait()
-    low = lax.rem(lax.broadcasted_iota(jnp.int32, ang_ref.shape, 1), head_dim) < head_dim // 2
-    tab_ref[...] = jnp.where(low, jnp.cos(ang_ref[...]), jnp.sin(ang_ref[...]))
-    t_gather.start()
     wo_gather = Gather(lambda d: wo_all.at[cols_of(d), :], wo_send, wo_recv, where, own=wo_ref)
     bulk = []
     part_rows = rows_own // 4
@@ -755,7 +744,6 @@
         local.append((pltpu.make_async_copy(src.at[:, hid_of(me)], stage.at[i], loc_sem.at[i]),
                       pltpu.make_async_copy(stage.at[i], dst.at[cols_of(me), :], loc_sem.at[2 + i])))
         local[-1][0].start()
-    tab_all[me] = tab_ref[...]
     for load, store in local:
         load.wait()
         store.start()
@@ -780,9 +768,14 @@
         ut_ref[:, tok_of(d)] = u_blk[:, cols_of(me)].T
         qkv_blk[...] = dot(u_blk[...], w_head[...], 1, 1).astype(BF16)
         half = tokens // 2
+        where_to = gain_all[d, 2:3, :]
+        lanes = lax.broadcasted_iota(jnp.int32, (half, 2 * head_dim), 1)
+        by_row = lambda lo: jnp.broadcast_to(where_to[:, lo:lo + half], (2 * head_dim, half)).T
+        angles = jnp.where(lanes < head_dim, by_row(0), by_row(half)) * freq_ref[...]
+        packed = jnp.where(lax.rem(lanes, head_dim) < head_dim // 2, jnp.cos(angles), jnp.sin(angles))
         for part in range(2):
             rows = pl.ds(pl.multiple_of(base + part * half, half), half)
-            cos_blk, sin_blk = spread_tables(tab_all[d], part == 1)
+            cos_blk, sin_blk = spread_tables(packed, part == 1)
             cos_ref[rows, :] = cos_blk
             sin_ref[rows, :] = sin_blk
             source = slice(part * half, (part + 1) * half)
@@ -795,23 +788,18 @@
             v_ref[rows, :] = qkv_blk[source, qw + head_dim:]
 
     x_gather.got_first()
-    t_gather.got_first()
     x_gather.got_second()
-    t_gather.got_second()
     wo_gather.start()
     start_bulk(0, 1)
     x_gather.got_partner(0)
-    t_gather.got_partner(0)
 
     def use_near(i, _):
         use(jnp.where(i == 0, me, jnp.where(i == 1, first, jnp.where(i == 2, second, partner))))
         return 0
     lax.fori_loop(0, 4, use_near, 0)
     x_gather.got_diag()
-    t_gather.got_diag()
     for i in range(1, 4):
         x_gather.got_partner(i)
-        t_gather.got_partner(i)
 
     def use_far(i, _):
         use(jnp.where(i == 0, other(0, 1, 1), jnp.where(i == 1, other(1, 1, 0), jnp.where(i == 2, other(1, 0, 1), other(1, 1, 1)))))
@@ -905,7 +893,7 @@
         give(i)[1].wait_send()
     for copy in small + slices:
         copy.wait_send()
-    for gather in (x_gather, t_gather, wo_gather, o_gather):
+    for gather in (x_gather, wo_gather, o_gather):
         gather.drain()
     for copy in bulk:
         copy.wait()
@@ -915,70 +903,68 @@
         copy.wait()
 
 
-def attention_step(heads, x_in, angles, gains, w_q, w_k, w_v, wo_own, w_gate, w_up):
+def attention_step(heads, x_in, positions, gain1, gain2, w_q, w_k, w_v, wo_own, w_gate, w_up):
     tokens, model = x_in.shape
     seq_len = 8 * tokens
     head_dim = wo_own.shape[0] // heads
     rows_own, hid = w_gate.shape[0], w_gate.shape[1] // 8
     shape = jax.ShapeDtypeStruct
-    hbm = pl.BlockSpec(memory_space=pl.ANY)
+    hbm, vmem = pl.BlockSpec(memory_space=pl.ANY), pl.BlockSpec(memory_space=pltpu.VMEM)
     dma = pltpu.SemaphoreType.DMA
     vm = lambda *dims, dtype=BF16: pltpu.VMEM(dims, dtype)
+    steps = np.arange(head_dim // 2, dtype=np.float32) * np.float32(2.0 / head_dim)
+    freq = np.tile(np.float32(1.0) / (np.float32(ROPE_BASE) ** steps), 4)[None]
     outs = (shape((heads, seq_len, head_dim), BF16), shape((seq_len, head_dim), BF16), shape((seq_len, head_dim), BF16),
             shape((heads * head_dim, seq_len), BF16), shape((rows_own, seq_len), BF16),
             shape((seq_len, 128), F32), shape((seq_len, 128), F32), shape((8, model), F32), shape((tokens, model), BF16))
-    pairs = [dma((7,)), dma((7,)), dma((3, 7)), dma((3, 7)), dma((7,)), dma((7,)), dma((7,)), dma((7,)), dma((7,)), dma((7,)),
+    pairs = [dma((7,)), dma((7,)), dma((3, 7)), dma((3, 7)), dma((7,)), dma((7,)), dma((7,)), dma((7,)),
              dma((56,)), dma((56,)), dma((7,)), dma((7,))]
     return pl.pallas_call(
         functools.partial(attention_comm_kernel, 'sp', heads), name='attention_comm',
-        in_specs=[hbm] * 9, out_specs=[hbm] * 12,
+        in_specs=[hbm] + [vmem] * 4 + [hbm] * 6, out_specs=[hbm] * 12,
         out_shape=[*outs, shape((seq_len, model), BF16), shape((model, hid), BF16), shape((model, hid), BF16)],
         scratch_shapes=[vm(*t.shape, dtype=t.dtype) for t in outs] + [
-            vm(tokens // 2, 128, dtype=F32), vm(tokens // 2, 128, dtype=F32), vm(seq_len, model), vm(8, tokens // 2, 128, dtype=F32), vm(8, 8, rows_own, dtype=F32),
+            vm(8, rows_own, dtype=F32), vm(seq_len, model), vm(8, 8, rows_own, dtype=F32),
             vm(384, model), vm(model, model), vm(seq_len, model), vm(tokens, model), vm(tokens, 384), vm(heads, seq_len, head_dim),
             vm(seq_len, heads * head_dim), vm(tokens, model, dtype=F32), vm(2, tokens, model), vm(2, rows_own, hid)] + pairs + [
             dma((2,)), dma((4,)), dma((4,)), dma((4,)), dma((8,)), dma((9,))],
         compiler_params=pltpu.CompilerParams(collective_id=0, has_side_effects=True, vmem_limit_bytes=63 * 1024 * 1024),
-    )(x_in, angles, gains, w_q, w_k, w_v, wo_own, w_gate, w_up)
-
-
-def hand_over_kernel(plan, *refs):
-    n_in = len(plan)
+    )(x_in, positions, gain1, gain2, jnp.asarray(freq), w_q, w_k, w_v, wo_own, w_gate, w_up)
+
+
+def hand_over_kernel(n_far, n_near, *refs):
+    n_in = n_far + n_near
     sources, gains, results = refs[:n_in], refs[n_in], refs[n_in + 1:2 * n_in + 1]
-    gain_outs, stages = refs[2 * n_in + 1:2 * n_in + 3], refs[2 * n_in + 3:3 * n_in + 3]
-    in_sem, out_sem = refs[3 * n_in + 3:]
-    pieces, count = [], 0
-    for src, stage, dst, parts in zip(sources, stages, results, plan):
-        rows = src.shape[0] // parts
-        for p in range(parts):
-            part = pl.ds(p * rows, rows)
-            pieces.append((pltpu.make_async_copy(src.at[part], stage.at[part], in_sem.at[count]),
-                           pltpu.make_async_copy(stage.at[part], dst.at[part], out_sem.at[count])))
-            count += 1
-    for load, _ in pieces:
+    gain_outs, stages = refs[2 * n_in + 1:2 * n_in + 3], refs[2 * n_in + 3:2 * n_in + 3 + n_far]
+    in_sem, out_sem = refs[2 * n_in + 3 + n_far:]
+    loads = [pltpu.make_async_copy(sources[i], stages[i], in_sem.at[i]) for i in range(n_far)]
+    stores = [pltpu.make_async_copy(stages[i] if i < n_far else sources[i], results[i], out_sem.at[i]) for i in range(n_in)]
+    for load in loads:
         load.start()
+    for store in stores[n_far:]:
+        store.start()
     for i in range(2):
         gain_outs[i][...] = gains[i, :]
-    for load, store in pieces:
+    for load, store in zip(loads, stores):
         load.wait()
         store.start()
-    for _, store in pieces:
+    for store in stores:
         store.wait()
 
 
-def hand_over(arrays, gains):
+def hand_over(far, near, gains):
     shape = jax.ShapeDtypeStruct
-    plan = tuple(max(1, a.size * a.dtype.itemsize // (1 << 20)) for a in arrays)
-    hbm, vmem = pl.BlockSpec(memory_space=pl.ANY), pl.BlockSpec(memory_space=pltpu.VMEM)
+    arrays = far + near
+    hbm, vmem = pl.BlockSpec(memory_space=pltpu.HBM), pl.BlockSpec(memory_space=pltpu.VMEM)
     dma = pltpu.SemaphoreType.DMA
-    out = pl.pallas_call(
-        functools.partial(hand_over_kernel, plan), name='hand_over',
-        in_specs=[hbm] * len(arrays) + [vmem], out_specs=[hbm] * len(arrays) + [vmem] * 2,
+    return pl.pallas_call(
+        functools.partial(hand_over_kernel, len(far), len(near)), name='hand_over',
+        in_specs=[hbm] * len(far) + [vmem] * (len(near) + 1), out_specs=[hbm] * len(arrays) + [vmem] * 2,
         out_shape=[shape(a.shape, a.dtype) for a in arrays] + [shape((gains.shape[1],), F32)] * 2,
-        scratch_shapes=[pltpu.VMEM(a.shape, a.dtype) for a in arrays] + [dma((sum(plan),)), dma((sum(plan),))],
-        compiler_params=pltpu.CompilerParams(vmem_limit_bytes=63 * 1024 * 1024),
-    )(*arrays, gains)
-    return out
+        scratch_shapes=[pltpu.VMEM(a.shape, a.dtype) for a in far] + [dma((len(far),)), dma((len(arrays),))],
+        compiler_params=pltpu.CompilerParams(vmem_limit_bytes=12 * 1024 * 1024),
+    )(*[pltpu.with_memory_space_constraint(a, pltpu.HBM) for a in far],
+      *[pltpu.with_memory_space_constraint(a, pltpu.VMEM) for a in near + (gains,)])
 
 
 def solution(mesh):
@@ -989,24 +975,17 @@
         head_dim = w_q.shape[2]
         heads = w_q.shape[1] // n_dev
         rows_own = w_q.shape[0]
-        inv_freq = 1.0 / (ROPE_BASE ** (jnp.arange(head_dim // 2, dtype=F32) * (2.0 / head_dim)))
-        half = tokens // 2
-        lane = jnp.arange(4 * head_dim // 2)
-        turn = jnp.where((lane < head_dim)[None, :], positions[:half, None], positions[half:, None])
-        angles = turn.astype(F32) * jnp.tile(inv_freq, 4)[None, :]
-        row = jnp.arange(8)[:, None]
-        gains = jnp.where(row == 0, norm1_gain[None].astype(F32), jnp.where(row == 1, norm2_gain[None].astype(F32), 0.0))
         flat = lambda w: w.transpose(1, 2, 0).reshape(-1, rows_own)
         wo_own = w_o.reshape(-1, model)
         (q_rot, k_rot, v_lin, o_t, u_t, cos_tab, sin_tab, g_full, hidden,
-         mlp_in, w1, w3) = attention_step(heads, x_in, angles, gains, flat(w_q), flat(w_k), flat(w_v), wo_own, w_gate, w_up)
+         mlp_in, w1, w3) = attention_step(heads, x_in, positions, norm1_gain, norm2_gain, flat(w_q), flat(w_k), flat(w_v), wo_own, w_gate, w_up)
         d_w1s, d_w3s, d_down, y_out, dh_own, d_g2 = mlp_step(mlp_in, d_out, w1, w3, w_down, hidden, g_full)
         d_wo, d_wq_t, d_wk_t, d_wv_t, d_w1, d_w3, d_x, d_gains = attention_backward_step(
             heads, dh_own, wo_own, o_t, q_rot, k_rot, v_lin, (cos_tab, sin_tab),
             d_w1s, d_w3s, flat(w_q), flat(w_k), flat(w_v), u_t, x_in, g_full, d_g2)
         from_cols = lambda d, w: d.reshape(w.shape[1], w.shape[2], rows_own).transpose(2, 0, 1)
-        (d_w1, d_w3, d_down, d_wo, d_wq_t, d_wk_t, d_wv_t, y_out, d_x, d_g1, d_g2) = hand_over(
-            (d_w1, d_w3, d_down, d_wo, d_wq_t, d_wk_t, d_wv_t, y_out, d_x), d_gains)
+        (d_down, y_out, d_w1, d_w3, d_wo, d_wq_t, d_wk_t, d_wv_t, d_x, d_g1, d_g2) = hand_over(
+            (d_down, y_out), (d_w1, d_w3, d_wo, d_wq_t, d_wk_t, d_wv_t, d_x), d_gains)
         return (y_out, d_x, d_g1, d_g2, from_cols(d_wq_t, w_q), from_cols(d_wk_t, w_k), from_cols(d_wv_t, w_v),
                 d_wo.reshape(w_o.shape), d_w1, d_w3, d_down)
 

time: 712 us -> 697 us (0.979)
  Pallas kernels: 707 us -> 696 us
    pallas_call x1, Pallas kernels: 24 us -> 14 us  [hand_over(): pl.pallas_call(functools.partial(hand_over_kernel, len(far), len(near)),...]
where the time goes in v6:
time: 697 us
  Pallas kernels  696 us (100%)
    pallas_call x1, Pallas kernels, attention_backward_step(): pl.pallas_call(functools.partial(attn_bwd_comm_kernel, 'sp', heads), name...  283 us
    pallas_call x1, Pallas kernels, attention_step(): pl.pallas_call(functools.partial(attention_comm_kernel, 'sp', heads), nam...  220 us
    pallas_call x1, Pallas kernels, mlp_step(): pl.pallas_call(functools.partial(mlp_comm_kernel, 'sp'), name='mlp_comm',...  180 us
    pallas_call x1, Pallas kernels, hand_over(): pl.pallas_call(functools.partial(hand_over_kernel, len(far), len(near)),...  14 us

profile of v6, /device:TPU:0, one launch (start us, length us, event | category | flops | bytes accessed | tf_op | source)
XLA Modules:
  0.0 696.9 jit_solution(7223142918227969310)
XLA Ops:
  0.6 219.9 %attention_comm.1 = (bf16[4,2048,64]{2,1,0:T(8,128)(2,1)}, bf16[2048,64]{1,0:T(8,128)(2,1)}, bf16[2048,64]{1,0:T(8,128)(2,1)}, bf16[256,2048]{1,0:T(8,128)(2,1)}...) custom-call(bf16[256,2048]{1,0:T(8,128)(2,1)} %x_hbm.1, ...), custom_call_target="tpu_custom_call" | custom-call | tf_op jit(solution)/shard_map/attention_comm/pallas_call | solution.py:922
  220.6 179.5 %mlp_comm.1 = (f32[2048,1024]{1,0:T(8,128)}, f32[2048,1024]{1,0:T(8,128)}, f32[1024,2048]{1,0:T(8,128)}, bf16[256,2048]{1,0:T(8,128)(2,1)}, bf16[256,2048]{1,0:T...) custom-call(bf16[2048,2048]{1,0:T(8,128)(2,1)} %get-tuple-element.48.m_ref, bf16[256,2048]{1,0:T(8,128)(2,1)} %dout_own.1, ...), custom_call_target="tpu_custom_call" | custom-call | tf_op jit(solution)/shard_map/mlp_comm/pallas_call | solution.py:652
  400.1 282.7 %attn_bwd_comm.1 = (f32[256,2048]{1,0:T(8,128)S(1)}, f32[2048,256]{1,0:T(8,128)S(1)}, f32[512,256]{1,0:T(8,128)S(1)}, f32[512,256]{1,0:T(8,128)S(1)}, f32[256,81...) custom-call(bf16[256,2048]{1,0:T(8,128)(2,1)} %get-tuple-element.55.dh_hbm, ...), custom_call_target="tpu_custom_call" | custom-call | tf_op jit(solution)/shard_map/attn_bwd_comm/pallas_call | solution.py:324
  682.8 14.0 %hand_over.1 = (f32[1024,2048]{1,0:T(8,128)}, bf16[256,2048]{1,0:T(8,128)(2,1)}, f32[256,8192]{1,0:T(8,128)}, f32[256,8192]{1,0:T(8,128)}, f32[256,2048]{1,0:T(8...) custom-call(f32[1024,2048]{1,0:T(8,128)} %get-tuple-element.53.refs_, ...), custom_call_target="tpu_custom_call" | custom-call | tf_op jit(solution)/shard_map/hand_over/pallas_call | solution.py:960

commit v7 on v6

--- a/solution.py
+++ b/solution.py
@@ -139,36 +139,36 @@
     rows_own, hid = out1_ref.shape[0], dw1_ref.shape[1]
     tokens = x_hbm.shape[0]
     qw = heads * head_dim
-    half_rows = rows_own // 2
 
     rows_of = lambda d: pl.ds(pl.multiple_of(d * rows_own, rows_own), rows_own)
     hid_of = lambda d: pl.ds(pl.multiple_of(d * hid, hid), hid)
     pairs = ((dw1_ref, out1_ref), (dw3_ref, out3_ref))
     peers = [other(r & 1, (r >> 1) & 1, r >> 2) for r in (2, 4, 6, 3, 5, 7, 1)]
-    bulk = []
-    for part in range(4):
-        src, dst = pairs[part // 2]
-        for n, dest in enumerate(peers):
-            low = (part % 2) * half_rows
-            bulk.append(pltpu.make_async_remote_copy(
-                src_ref=src.at[pl.ds(pl.multiple_of(dest * rows_own + low, half_rows), half_rows), :],
-                dst_ref=dst.at[pl.ds(low, half_rows), hid_of(me)], send_sem=bulk_send.at[part * 7 + n],
-                recv_sem=bulk_recv.at[part * 7 + n], device_id=(dest,), device_id_type=MESH))
-
-    def start_bulk(part):
-        for copy in bulk[part * 7:part * 7 + 7]:
-            copy.start()
+    bulk, parts = [], []
+    for src, dst in pairs:
+        for low, high in ((0, 8), (8, rows_own // 2), (rows_own // 2, rows_own)):
+            parts.append(range(len(bulk), len(bulk) + len(peers)))
+            for dest in peers:
+                bulk.append(pltpu.make_async_remote_copy(
+                    src_ref=src.at[pl.ds(pl.multiple_of(dest * rows_own + low, 8), high - low), :],
+                    dst_ref=dst.at[pl.ds(low, high - low), hid_of(me)], send_sem=bulk_send.at[len(bulk)],
+                    recv_sem=bulk_recv.at[len(bulk)], device_id=(dest,), device_id_type=MESH))
+
+    def start_bulk(*which):
+        for part in which:
+            for i in parts[part]:
+                bulk[i].start()
     tok_of = lambda d: pl.ds(pl.multiple_of(d * tokens, tokens), tokens)
     h_gather = Gather(lambda d: dh_ref.at[tok_of(d), :], hg_send, hg_recv, where, own=dh_hbm)
     h_gather.start()
+    start_bulk(0)
     local = [pltpu.make_async_copy(src.at[rows_of(me), :], dst.at[:, hid_of(me)], loc_sem.at[i]) for i, (src, dst) in enumerate(pairs)]
     for copy in local:
         copy.start()
     need('dh', 'wo', 'ot')
     h_gather.got_first()
     h_gather.got_second()
-    start_bulk(0)
-    start_bulk(1)
+    start_bulk(1, 2)
     h_gather.got_diag()
     for i in range(4):
         h_gather.got_partner(i)
@@ -226,6 +226,7 @@
 
     gather = Gather(lambda d: slots.at[d], gat_send, gat_recv, where)
     gather.start()
+    start_bulk(3)
     du_acc[...] = jnp.zeros_like(du_acc)
     need('wq', 'wk', 'wv', 'ut')
 
@@ -256,7 +257,7 @@
     use_many(me)
     gather.got_first()
     gather.got_second()
-    start_bulk(2)
+    start_bulk(4)
     gather.got_partner(0)
     use_many(first, second, other(1, 0, 0))
     gather.got_diag()
@@ -270,7 +271,7 @@
             src_ref=du_scr.at[tok_of(dest), :], dst_ref=ot_ref.at[:, rows_of(me)], send_sem=du_send.at[n],
             recv_sem=du_rsem.at[n], device_id=(dest,), device_id_type=MESH))
         sends[-1].start()
-    start_bulk(3)
+    start_bulk(5)
     ot_ref[:, rows_of(me)] = du_scr[tok_of(me), :]
     need('g', 'dg2')
     x_load.wait()
@@ -330,7 +331,7 @@
             vm(8, model, dtype=F32), vm(8, 8, rows_own, dtype=F32),
             vm(seq_len, head_dim, dtype=F32), vm(seq_len, head_dim, dtype=F32),
             vm(seq_len, rows_own, dtype=F32), vm(seq_len, rows_own),
-            dma((28,)), dma((28,)), dma((7,)), dma((7,)), dma((7,)), dma((7,)), dma((7,)), dma((7,)), dma((7,)), dma((7,)), dma((2,)), dma((15,))],
+            dma((42,)), dma((42,)), dma((7,)), dma((7,)), dma((7,)), dma((7,)), dma((7,)), dma((7,)), dma((7,)), dma((7,)), dma((2,)), dma((15,))],
         compiler_params=pltpu.CompilerParams(collective_id=2, has_side_effects=True, vmem_limit_bytes=43515904),
     )(*early, d_w1, d_w3, *late)
 
@@ -450,12 +451,18 @@
                 recv_sem=mail_recv.at[self.turn, kind], device_id=(dest,), device_id_type=MESH)
 
         def step(self, step, prepare, partial):
+            self.first_half(step, prepare, partial)
+            self.second_half(step, prepare, partial)
+
+        def first_half(self, step, prepare, partial):
             slot = lax.rem(step, 2)
             prepare(2 * step)
 
             def put_out(cols, value):
                 outbox[slot, :, cols] = value
             partial(half_rows(2 * step), put_out)
+
+        def second_half(self, step, prepare, partial):
             self.to_partner(step).start()
             prepare(2 * step + 1)
             off = step_off(step, 0)
@@ -578,11 +585,14 @@
         return 0
     lax.fori_loop(0, 8, grad_block, 0)
 
+    as_is = lambda half: None
+    grad_round.first_half(0, as_is, add_mlp_grad)
     pl.semaphore_wait(credit.at[0], 1)
-    grad_round.step(0, lambda half: None, add_mlp_grad)
+    grad_round.second_half(0, as_is, add_mlp_grad)
     pl.semaphore_wait(credit.at[1], 1)
     grad_round.mail(0).start()
     weight_grads(0, 2)
+    grad_round.first_half(1, as_is, add_mlp_grad)
     out_round.mail(1).wait_recv()
     out_round.mail(2).wait_recv()
 
@@ -600,11 +610,11 @@
     signal(4, second)
     pl.semaphore_wait(credit.at[2], 1)
 
+    grad_round.second_half(1, as_is, add_mlp_grad)
+
     def grad_step(step, _):
-        @pl.when(step >= 2)
-        def _():
-            grad_round.to_partner(step - 2).wait_send()
-        grad_round.step(step, lambda half: None, add_mlp_grad)
+        grad_round.to_partner(step - 2).wait_send()
+        grad_round.step(step, as_is, add_mlp_grad)
 
         @pl.when(step == 2)
         def _():
@@ -614,7 +624,7 @@
             pl.semaphore_wait(credit.at[4], 1)
             grad_round.mail(2).start()
         return 0
-    lax.fori_loop(1, 4, grad_step, 0)
+    lax.fori_loop(2, 4, grad_step, 0)
     weight_grads(2, 8)
     grad_round.mail(1).wait_recv()
     grad_round.mail(2).wait_recv()
@@ -713,21 +723,22 @@
     x_gather = Gather(lambda d: x_all.at[tok_of(d), :], x_send, x_recv, where, own=x_ref)
     x_gather.start()
     wo_gather = Gather(lambda d: wo_all.at[cols_of(d), :], wo_send, wo_recv, where, own=wo_ref)
-    bulk = []
-    part_rows = rows_own // 4
-    for part in range(8):
-        src, dst = ((wg_ref, w1_ref), (wu_ref, w3_ref))[part // 4]
-        low = (part % 4) * part_rows
-        for n, dest in enumerate(peers):
-            bulk.append(pltpu.make_async_remote_copy(
-                src_ref=src.at[pl.ds(low, part_rows), hid_of(dest)],
-                dst_ref=dst.at[pl.ds(pl.multiple_of(me * rows_own + low, part_rows), part_rows), :],
-                send_sem=bulk_send.at[part * 7 + n], recv_sem=bulk_recv.at[part * 7 + n], device_id=(dest,), device_id_type=MESH))
-
-    def start_bulk(*parts):
-        for part in parts:
-            for copy in bulk[part * 7:part * 7 + 7]:
-                copy.start()
+    bulk, parts = [], []
+    quarter = rows_own // 4
+    for src, dst in ((wg_ref, w1_ref), (wu_ref, w3_ref)):
+        for low, high in ((0, 16), (16, quarter), (quarter, 2 * quarter), (2 * quarter, 3 * quarter), (3 * quarter, rows_own)):
+            parts.append(range(len(bulk), len(bulk) + len(peers)))
+            for dest in peers:
+                bulk.append(pltpu.make_async_remote_copy(
+                    src_ref=src.at[pl.ds(low, high - low), hid_of(dest)],
+                    dst_ref=dst.at[pl.ds(pl.multiple_of(me * rows_own + low, 16), high - low), :],
+                    send_sem=bulk_send.at[len(bulk)], recv_sem=bulk_recv.at[len(bulk)], device_id=(dest,), device_id_type=MESH))
+
+    def start_bulk(*which):
+        for part in which:
+            for i in parts[part]:
+                bulk[i].start()
+    start_bulk(0)
 
     stores = [pltpu.make_async_copy(src, dst, st_sem.at[i]) for i, (src, dst) in enumerate((
         (q_ref, q_hbm), (k_ref, k_hbm), (v_ref, v_hbm), (ot_ref, ot_hbm), (ut_ref, ut_hbm), (cos_ref, cos_hbm),
@@ -790,7 +801,7 @@
     x_gather.got_first()
     x_gather.got_second()
     wo_gather.start()
-    start_bulk(0, 1)
+    start_bulk(1, 2, 3)
     x_gather.got_partner(0)
 
     def use_near(i, _):
@@ -821,7 +832,7 @@
     o_gather.start()
     wo_gather.got_first()
     wo_gather.got_second()
-    start_bulk(2)
+    start_bulk(4)
     o_all[:, cols_of(me)] = o_own[...]
 
     def turn_out(k, _):
@@ -835,12 +846,12 @@
         wo_gather.got_partner(i)
     o_gather.got_first()
     o_gather.got_second()
-    start_bulk(3)
+    start_bulk(5, 6)
     o_gather.got_partner(0)
     o_gather.got_diag()
     for i in range(1, 4):
         o_gather.got_partner(i)
-    start_bulk(4, 5, 6, 7)
+    start_bulk(7, 8, 9)
 
     def rows_at(i):
         flips = lambda a, b: other(0, a, b)
@@ -918,7 +929,7 @@
             shape((heads * head_dim, seq_len), BF16), shape((rows_own, seq_len), BF16),
             shape((seq_len, 128), F32), shape((seq_len, 128), F32), shape((8, model), F32), shape((tokens, model), BF16))
     pairs = [dma((7,)), dma((7,)), dma((3, 7)), dma((3, 7)), dma((7,)), dma((7,)), dma((7,)), dma((7,)),
-             dma((56,)), dma((56,)), dma((7,)), dma((7,))]
+             dma((70,)), dma((70,)), dma((7,)), dma((7,))]
     return pl.pallas_call(
         functools.partial(attention_comm_kernel, 'sp', heads), name='attention_comm',
         in_specs=[hbm] + [vmem] * 4 + [hbm] * 6, out_specs=[hbm] * 12,

time: 697 us -> 691 us (level)
  no operation moved by 1% of the time
where the time goes in v7:
time: 691 us
  Pallas kernels  690 us (100%)
    pallas_call x1, Pallas kernels, attention_backward_step(): pl.pallas_call(functools.partial(attn_bwd_comm_kernel, 'sp', heads), name...  282 us
    pallas_call x1, Pallas kernels, attention_step(): pl.pallas_call(functools.partial(attention_comm_kernel, 'sp', heads), nam...  218 us
    pallas_call x1, Pallas kernels, mlp_step(): pl.pallas_call(functools.partial(mlp_comm_kernel, 'sp'), name='mlp_comm',...  177 us
    pallas_call x1, Pallas kernels, hand_over(): pl.pallas_call(functools.partial(hand_over_kernel, len(far), len(near)),...  14 us

profile of v7, /device:TPU:0, one launch (start us, length us, event | category | flops | bytes accessed | tf_op | source)
XLA Modules:
  0.0 690.9 jit_solution(13408006363185934029)
XLA Ops:
  0.6 217.6 %attention_comm.1 = (bf16[4,2048,64]{2,1,0:T(8,128)(2,1)}, bf16[2048,64]{1,0:T(8,128)(2,1)}, bf16[2048,64]{1,0:T(8,128)(2,1)}, bf16[256,2048]{1,0:T(8,128)(2,1)}...) custom-call(bf16[256,2048]{1,0:T(8,128)(2,1)} %x_hbm.1, ...), custom_call_target="tpu_custom_call" | custom-call | tf_op jit(solution)/shard_map/attention_comm/pallas_call | solution.py:933
  218.3 176.6 %mlp_comm.1 = (f32[2048,1024]{1,0:T(8,128)}, f32[2048,1024]{1,0:T(8,128)}, f32[1024,2048]{1,0:T(8,128)}, bf16[256,2048]{1,0:T(8,128)(2,1)}, bf16[256,2048]{1,0:T...) custom-call(bf16[2048,2048]{1,0:T(8,128)(2,1)} %get-tuple-element.48.m_ref, bf16[256,2048]{1,0:T(8,128)(2,1)} %dout_own.1, ...), custom_call_target="tpu_custom_call" | custom-call | tf_op jit(solution)/shard_map/mlp_comm/pallas_call | solution.py:662
  394.9 281.8 %attn_bwd_comm.1 = (f32[256,2048]{1,0:T(8,128)S(1)}, f32[2048,256]{1,0:T(8,128)S(1)}, f32[512,256]{1,0:T(8,128)S(1)}, f32[512,256]{1,0:T(8,128)S(1)}, f32[256,81...) custom-call(bf16[256,2048]{1,0:T(8,128)(2,1)} %get-tuple-element.55.dh_hbm, ...), custom_call_target="tpu_custom_call" | custom-call | tf_op jit(solution)/shard_map/attn_bwd_comm/pallas_call | solution.py:325
  676.7 14.0 %hand_over.1 = (f32[1024,2048]{1,0:T(8,128)}, bf16[256,2048]{1,0:T(8,128)(2,1)}, f32[256,8192]{1,0:T(8,128)}, f32[256,8192]{1,0:T(8,128)}, f32[256,2048]{1,0:T(8...) custom-call(f32[1024,2048]{1,0:T(8,128)} %get-tuple-element.53.refs_, ...), custom_call_target="tpu_custom_call" | custom-call | tf_op jit(solution)/shard_map/hand_over/pallas_call | solution.py:971

commit v8 on v7

--- a/solution.py
+++ b/solution.py
@@ -62,7 +62,7 @@
 
 
 class Gather:
-    def __init__(self, slot, send_sem, recv_sem, where, own=None):
+    def __init__(self, slot, send_sem, recv_sem, where, seven, own=None):
         me, other, first, second = where
         partner, diag = other(1, 0, 0), other(0, 1, 1)
         own = slot(me) if own is None else own
@@ -71,8 +71,11 @@
                 (slot(first), first, partner), (slot(second), second, partner), (slot(diag), diag, partner)]
         for i, (src, what, dest) in enumerate(plan):
             self.copies.append(pltpu.make_async_remote_copy(
-                src_ref=src, dst_ref=slot(what), send_sem=send_sem.at[i], recv_sem=recv_sem.at[i],
+                src_ref=src, dst_ref=slot(what), send_sem=send_sem.at[0], recv_sem=recv_sem.at[i],
                 device_id=(dest,), device_id_type=MESH))
+        self.sent = pltpu.make_async_remote_copy(
+            src_ref=seven, dst_ref=seven, send_sem=send_sem.at[0], recv_sem=recv_sem.at[0],
+            device_id=(partner,), device_id_type=MESH)
 
     def start(self):
         for i in range(3):
@@ -95,8 +98,7 @@
         self.copies[(2, 4, 5, 6)[i]].wait_recv()
 
     def drain(self):
-        for copy in self.copies:
-            copy.wait_send()
+        self.sent.wait_send()
 
 
 def turn_halves(values, cos_blk, sin_blk):
@@ -114,17 +116,17 @@
 
 
 def attn_bwd_comm_kernel(axis, heads, dh_hbm, wo_hbm, ot_hbm, q_hbm, k_hbm, v_hbm, cos_hbm, sin_hbm,
-                         dw1_ref, dw3_ref, wq_hbm, wk_hbm, wv_hbm, ut_hbm, x_hbm, g_hbm, dg2_hbm,
-                         dwo_ref, dwq_ref, dwk_ref, dwv_ref, out1_ref, out3_ref, dx_ref, dg_ref,
-                         dh_ref, wo_ref, ot_ref, q_ref, k_ref, v_ref, cos_ref, sin_ref, wq_ref, wk_ref, wv_ref, ut_ref, g_ref, dg2_ref,
-                         slots, do_scr, dg_own, dg_all, dk_acc, dv_acc, du_acc, du_scr,
-                         bulk_send, bulk_recv, hg_send, hg_recv, gat_send, gat_recv, du_send, du_rsem, dg_send, dg_recv, loc_sem, ld_sem):
+                         dw1_ref, dw3_ref, wq_hbm, wk_hbm, wv_hbm, ut_hbm, x_hbm, g_hbm, dg2_hbm, ddown_hbm, y_hbm,
+                         dwo_ref, dwq_ref, dwk_ref, dwv_ref, out1_ref, out3_ref, dx_ref, dg_ref, ddown_ref, y_ref,
+                         dh_own, wo_ref, ot_ref, q_ref, k_ref, v_ref, cos_ref, sin_ref, wq_ref, wk_ref, wv_ref, ut_ref, g_ref, dg2_ref,
+                         pool, do_scr, dg_own, dg_all, dk_acc, dv_acc, du_acc,
+                         bulk_send, bulk_recv, hg_send, hg_recv, gat_send, gat_recv, du_send, du_rsem, dg_send, dg_recv, loc_sem, ld_sem, credit):
     loads = {}
     for i, (name, src, dst) in enumerate((
             ('wo', wo_hbm, wo_ref), ('ot', ot_hbm, ot_ref), ('q', q_hbm, q_ref), ('k', k_hbm, k_ref),
             ('v', v_hbm, v_ref), ('cos', cos_hbm, cos_ref), ('sin', sin_hbm, sin_ref), ('wq', wq_hbm, wq_ref), ('wk', wk_hbm, wk_ref),
             ('wv', wv_hbm, wv_ref), ('ut', ut_hbm, ut_ref), ('g', g_hbm, g_ref), ('dg2', dg2_hbm, dg2_ref),
-            ('dh', dh_hbm, dh_ref.at[pl.ds(pl.multiple_of(lax.axis_index(axis) * x_hbm.shape[0], x_hbm.shape[0]), x_hbm.shape[0]), :]))):
+            ('dh', dh_hbm, dh_own), ('ddown', ddown_hbm, ddown_ref), ('y', y_hbm, y_ref))):
         loads[name] = pltpu.make_async_copy(src, dst, ld_sem.at[i])
         loads[name].start()
 
@@ -137,7 +139,7 @@
     greet(other)
     seq_len, head_dim = k_ref.shape
     rows_own, hid = out1_ref.shape[0], dw1_ref.shape[1]
-    tokens = x_hbm.shape[0]
+    tokens, model = x_hbm.shape
     qw = heads * head_dim
 
     rows_of = lambda d: pl.ds(pl.multiple_of(d * rows_own, rows_own), rows_own)
@@ -145,27 +147,29 @@
     pairs = ((dw1_ref, out1_ref), (dw3_ref, out3_ref))
     peers = [other(r & 1, (r >> 1) & 1, r >> 2) for r in (2, 4, 6, 3, 5, 7, 1)]
     bulk, parts = [], []
-    for src, dst in pairs:
+    for mat, (src, dst) in enumerate(pairs):
         for low, high in ((0, 8), (8, rows_own // 2), (rows_own // 2, rows_own)):
             parts.append(range(len(bulk), len(bulk) + len(peers)))
             for dest in peers:
                 bulk.append(pltpu.make_async_remote_copy(
                     src_ref=src.at[pl.ds(pl.multiple_of(dest * rows_own + low, 8), high - low), :],
-                    dst_ref=dst.at[pl.ds(low, high - low), hid_of(me)], send_sem=bulk_send.at[len(bulk)],
-                    recv_sem=bulk_recv.at[len(bulk)], device_id=(dest,), device_id_type=MESH))
+                    dst_ref=dst.at[pl.ds(low, high - low), hid_of(me)], send_sem=bulk_send.at[mat],
+                    recv_sem=bulk_recv.at[mat], device_id=(dest,), device_id_type=MESH))
 
     def start_bulk(*which):
         for part in which:
             for i in parts[part]:
                 bulk[i].start()
     tok_of = lambda d: pl.ds(pl.multiple_of(d * tokens, tokens), tokens)
-    h_gather = Gather(lambda d: dh_ref.at[tok_of(d), :], hg_send, hg_recv, where, own=dh_hbm)
+    dh_ref = pool.at[:, 0:model]
+    h_gather = Gather(lambda d: dh_ref.at[tok_of(d), :], hg_send, hg_recv, where, dh_ref.at[pl.ds(0, 7 * tokens), :], own=dh_hbm)
     h_gather.start()
     start_bulk(0)
     local = [pltpu.make_async_copy(src.at[rows_of(me), :], dst.at[:, hid_of(me)], loc_sem.at[i]) for i, (src, dst) in enumerate(pairs)]
     for copy in local:
         copy.start()
     need('dh', 'wo', 'ot')
+    pool[tok_of(me), 0:model] = dh_own[...]
     h_gather.got_first()
     h_gather.got_second()
     start_bulk(1, 2)
@@ -175,22 +179,25 @@
 
     def split_out_grad(k, _):
         rows = pl.ds(pl.multiple_of(k * BLK, BLK), BLK)
-        do_blk = dot(dh_ref[rows, :], wo_ref[...], 1, 1).astype(BF16)
+        do_blk = dot(pool[rows, 0:model], wo_ref[...], 1, 1).astype(BF16)
         for h in range(heads):
             do_scr[h, rows, :] = do_blk[:, h * head_dim:(h + 1) * head_dim]
         cols = rows
-        dwo_ref[:, cols] = dot(ot_ref[...], dh_ref[:, cols], 1, 0)
+        dwo_ref[:, cols] = dot(ot_ref[...], pool[:, cols], 1, 0)
         return 0
     lax.fori_loop(0, seq_len // BLK, split_out_grad, 0)
+    h_gather.drain()
+    for i, device in enumerate((first, second, other(1, 0, 0))):
+        pl.semaphore_signal(credit.at[i], inc=1, device_id=(device,), device_id_type=MESH)
     x_ref = wo_ref
-    x_load = pltpu.make_async_copy(x_hbm, x_ref, ld_sem.at[14])
+    x_load = pltpu.make_async_copy(x_hbm, x_ref, ld_sem.at[16])
     x_load.start()
 
 
     need('q', 'k', 'v')
     dk_acc[...] = jnp.zeros_like(dk_acc)
     dv_acc[...] = jnp.zeros_like(dv_acc)
-    mine = slots.at[me]
+    slot_cols = lambda d, off, width: pl.ds(pl.multiple_of(d * 384 + off, 128), width)
 
     def one_head(h, _):
         def one_block(start):
@@ -209,8 +216,6 @@
         return 0
     lax.fori_loop(0, heads, one_head, 0)
     need('cos', 'sin')
-    mine[:, qw:qw + head_dim] = dk_acc[...].astype(BF16)
-    mine[:, qw + head_dim:] = dv_acc[...].astype(BF16)
     low = lax.broadcasted_iota(jnp.int32, (BLK, 128), 1) < head_dim
 
     def turn_back(k, _):
@@ -218,13 +223,15 @@
         cos_blk, sin_blk = cos_ref[rows, :], -sin_ref[rows, :]
         for pair in range(heads // 2):
             both = jnp.concatenate([do_scr[2 * pair, rows, :], do_scr[2 * pair + 1, rows, :]], axis=1)
-            mine[rows, pair * 128:(pair + 1) * 128] = turn_halves(both.astype(F32), cos_blk, sin_blk).astype(BF16)
-        kv = mine[rows, qw:].astype(F32)
-        mine[rows, qw:] = jnp.where(low, turn_halves(kv, cos_blk, sin_blk), kv).astype(BF16)
+            pool[rows, slot_cols(me, pair * 128, 128)] = turn_halves(both.astype(F32), cos_blk, sin_blk).astype(BF16)
+        kv = jnp.concatenate([dk_acc[rows, :], dv_acc[rows, :]], axis=1).astype(BF16).astype(F32)
+        pool[rows, slot_cols(me, qw, 128)] = jnp.where(low, turn_halves(kv, cos_blk, sin_blk), kv).astype(BF16)
         return 0
     lax.fori_loop(0, seq_len // BLK, turn_back, 0)
 
-    gather = Gather(lambda d: slots.at[d], gat_send, gat_recv, where)
+    gather = Gather(lambda d: pool.at[:, slot_cols(d, 0, 384)], gat_send, gat_recv, where, pool.at[:, pl.ds(0, 7 * 384)])
+    for i in range(3):
+        pl.semaphore_wait(credit.at[i], 1)
     gather.start()
     start_bulk(3)
     du_acc[...] = jnp.zeros_like(du_acc)
@@ -237,10 +244,10 @@
 
         def add_rows(k, _):
             rows = pl.ds(pl.multiple_of(k * 512, 512), 512)
-            du_acc[rows, :] += dot(slots[d, rows, :], w_all, 1, 0)
+            du_acc[rows, :] += dot(pool[rows, slot_cols(d, 0, 384)], w_all, 1, 0)
             return 0
         lax.fori_loop(0, seq_len // 512, add_rows, 0)
-        d_w = dot(ut_ref[...], slots[d], 1, 0).T
+        d_w = dot(ut_ref[...], pool[:, slot_cols(d, 0, 384)], 1, 0).T
         dwq_ref[q_rows, :] = d_w[:qw]
         dwk_ref[kv_rows, :] = d_w[qw:qw + head_dim]
         dwv_ref[kv_rows, :] = d_w[qw + head_dim:]
@@ -264,51 +271,55 @@
     for i in range(1, 4):
         gather.got_partner(i)
     use_many(other(0, 1, 1), other(1, 1, 0), other(1, 0, 1), other(1, 1, 1))
-    du_scr[...] = du_acc[...].astype(BF16)
-    sends = []
-    for n, dest in enumerate(peers):
-        sends.append(pltpu.make_async_remote_copy(
-            src_ref=du_scr.at[tok_of(dest), :], dst_ref=ot_ref.at[:, rows_of(me)], send_sem=du_send.at[n],
-            recv_sem=du_rsem.at[n], device_id=(dest,), device_id_type=MESH))
-        sends[-1].start()
+    gather.drain()
+    du_scr = pool.at[:, 0:rows_own]
+
+    def round_du(k, _):
+        rows = pl.ds(pl.multiple_of(k * BLK, BLK), BLK)
+        pool[rows, 0:rows_own] = du_acc[rows, :].astype(BF16)
+        return 0
+    lax.fori_loop(0, seq_len // BLK, round_du, 0)
+    for dest in peers:
+        pltpu.make_async_remote_copy(
+            src_ref=du_scr.at[tok_of(dest), :], dst_ref=ot_ref.at[:, rows_of(me)], send_sem=du_send.at[0],
+            recv_sem=du_rsem.at[0], device_id=(dest,), device_id_type=MESH).start()
     start_bulk(5)
-    ot_ref[:, rows_of(me)] = du_scr[tok_of(me), :]
+    ot_ref[:, rows_of(me)] = pool[tok_of(me), 0:rows_own]
     need('g', 'dg2')
     x_load.wait()
-    for copy in sends:
-        copy.wait_recv()
+    got = ot_ref.at[:, pl.ds(0, 7 * rows_own)]
+    pltpu.make_async_copy(got, got, du_rsem.at[0]).wait()
     dg_own[...] = jnp.zeros_like(dg_own)
     dg_own[1:2, :] = dg2_ref[...]
 
     def input_grad(k, _):
         part = pl.ds(pl.multiple_of(k * 16, 16), 16)
         d_norm, d_gain = norm_backward(x_ref[part, :].astype(F32), g_ref[0:1, :], ot_ref[part, :].astype(F32))
-        dh_part = dh_ref[pl.ds(pl.multiple_of(me * tokens + k * 16, 16), 16), :]
+        dh_part = dh_own[part, :]
         dx_ref[part, :] = (dh_part.astype(F32) + d_norm).astype(BF16)
         dg_own[0:1, :] += d_gain
         return 0
     lax.fori_loop(0, tokens // 16, input_grad, 0)
-    gain_sends = []
-    for n, dest in enumerate(peers):
-        gain_sends.append(pltpu.make_async_remote_copy(
-            src_ref=dg_own.at[:, rows_of(dest)], dst_ref=dg_all.at[me], send_sem=dg_send.at[n],
-            recv_sem=dg_recv.at[n], device_id=(dest,), device_id_type=MESH))
-        gain_sends[-1].start()
+    for dest in peers:
+        pltpu.make_async_remote_copy(
+            src_ref=dg_own.at[:, rows_of(dest)], dst_ref=dg_all.at[me], send_sem=dg_send.at[0],
+            recv_sem=dg_recv.at[0], device_id=(dest,), device_id_type=MESH).start()
     dg_all[me] = dg_own[:, rows_of(me)]
-    for copy in gain_sends:
-        copy.wait_recv()
+    got = dg_all.at[pl.ds(0, 7)]
+    pltpu.make_async_copy(got, got, dg_recv.at[0]).wait()
     dg_ref[...] = jnp.sum(dg_all[...], axis=0)
-    for copy in sends + gain_sends:
-        copy.wait_send()
-    gather.drain()
-    h_gather.drain()
-    for copy in bulk:
-        copy.wait()
+    for sent, sem in ((du_scr.at[pl.ds(0, 7 * tokens), :], du_send), (dg_own.at[:, pl.ds(0, 7 * rows_own)], dg_send)):
+        pltpu.make_async_copy(sent, sent, sem.at[0]).wait()
+    need('ddown', 'y')
+    for mat, (src, dst) in enumerate(pairs):
+        sent, got = src.at[pl.ds(0, 7 * rows_own), :], dst.at[:, pl.ds(0, 7 * hid)]
+        pltpu.make_async_copy(sent, sent, bulk_send.at[mat]).wait()
+        pltpu.make_async_copy(got, got, bulk_recv.at[mat]).wait()
     for copy in local:
         copy.wait()
 
 
-def attention_backward_step(heads, dh_own, wo_own, o_t, q_rot, k_rot, v_lin, tables, d_w1, d_w3, w_q, w_k, w_v, u_t, x_in, gains, d_g2):
+def attention_backward_step(heads, dh_own, wo_own, o_t, q_rot, k_rot, v_lin, tables, d_w1, d_w3, w_q, w_k, w_v, u_t, x_in, gains, d_g2, d_down, y_out):
     seq_len, model = k_rot.shape[0], x_in.shape[1]
     head_dim = k_rot.shape[1]
     tokens = x_in.shape[0]
@@ -320,20 +331,20 @@
     early = (dh_own, wo_own, o_t, q_rot, k_rot, v_lin, *tables)
     late = (w_q, w_k, w_v, u_t, x_in, gains, d_g2)
     outs = [(wo_own.shape, F32), (w_q.shape, F32), (w_k.shape, F32), (w_v.shape, F32), ((rows_own, 8 * hid), F32),
-            ((rows_own, 8 * hid), F32), (x_in.shape, BF16), ((8, rows_own), F32)]
-    vmem = pl.BlockSpec(memory_space=pltpu.VMEM)
+            ((rows_own, 8 * hid), F32), (x_in.shape, BF16), ((8, rows_own), F32), (d_down.shape, F32), (y_out.shape, BF16)]
+    vmem, far = pl.BlockSpec(memory_space=pltpu.VMEM), pl.BlockSpec(memory_space=pltpu.HBM)
     return pl.pallas_call(
         functools.partial(attn_bwd_comm_kernel, 'sp', heads), name='attn_bwd_comm',
-        in_specs=[hbm] * 17, out_specs=[vmem] * 8,
+        in_specs=[hbm] * 17 + [far] * 2, out_specs=[vmem] * 10,
         out_shape=[pltpu.VMEM(dims, dtype) for dims, dtype in outs],
-        scratch_shapes=[vm(seq_len, model)] + [vm(*t.shape, dtype=t.dtype) for t in early[1:] + late[:4] + late[5:]] + [
-            vm(8, seq_len, 384), vm(heads, seq_len, head_dim),
+        scratch_shapes=[vm(*t.shape, dtype=t.dtype) for t in early + late[:4] + late[5:]] + [
+            vm(seq_len, 8 * 384), vm(heads, seq_len, head_dim),
             vm(8, model, dtype=F32), vm(8, 8, rows_own, dtype=F32),
             vm(seq_len, head_dim, dtype=F32), vm(seq_len, head_dim, dtype=F32),
-            vm(seq_len, rows_own, dtype=F32), vm(seq_len, rows_own),
-            dma((42,)), dma((42,)), dma((7,)), dma((7,)), dma((7,)), dma((7,)), dma((7,)), dma((7,)), dma((7,)), dma((7,)), dma((2,)), dma((15,))],
-        compiler_params=pltpu.CompilerParams(collective_id=2, has_side_effects=True, vmem_limit_bytes=43515904),
-    )(*early, d_w1, d_w3, *late)
+            vm(seq_len, rows_own, dtype=F32),
+            dma((2,)), dma((2,)), dma((1,)), dma((7,)), dma((1,)), dma((7,)), dma((1,)), dma((1,)), dma((1,)), dma((1,)), dma((2,)), dma((17,)), pltpu.SemaphoreType.REGULAR((3,))],
+        compiler_params=pltpu.CompilerParams(collective_id=2, has_side_effects=True, vmem_limit_bytes=34340864),
+    )(*early, d_w1, d_w3, *late, *[pltpu.with_memory_space_constraint(a, pltpu.HBM) for a in (d_down, y_out)])
 
 
 def mlp_comm_kernel(axis, m_ref, dout_own, w1_hbm, w3_hbm, w2_hbm, h_hbm, g_hbm,
@@ -538,7 +549,7 @@
 
     fetch(0).start()
     greet(other)
-    do_gather = Gather(lambda d: dout_ref.at[tok_of(d), :], do_send, do_recv, where, own=dout_own)
+    do_gather = Gather(lambda d: dout_ref.at[tok_of(d), :], do_send, do_recv, where, dout_ref.at[pl.ds(0, 7 * tokens), :], own=dout_own)
     do_gather.start()
     own_in.wait()
     own_out = pltpu.make_async_copy(dh_own, dout_ref.at[tok_of(me), :], own_sem.at[1])
@@ -670,7 +681,7 @@
             vm(2, tokens, model, dtype=F32), vm(4, tokens, model, dtype=F32), vm(3, tokens, model, dtype=F32),
             vm(2, tokens, model), vm(seq_len, 256), vm(seq_len, 256), vm(256, seq_len), vm(256, seq_len),
             vm(256, hid, dtype=F32), vm(256, hid, dtype=F32), vm(hid, 256, dtype=F32), vm(tokens, model),
-            dma((2, 4)), dma((2, 4)), dma((2, 3)), dma((2, 3)), dma((7,)), dma((7,)),
+            dma((2, 4)), dma((2, 4)), dma((2, 3)), dma((2, 3)), dma((1,)), dma((7,)),
             dma((2,)), dma((2,)), dma((3,)), dma((5,)), dma((5,)), pltpu.SemaphoreType.REGULAR((5,))],
         compiler_params=pltpu.CompilerParams(collective_id=1, has_side_effects=True, vmem_limit_bytes=63 * 1024 * 1024),
     )(m_all, d_out, w1, w3, w2, hidden, gains)[:6]
@@ -707,32 +718,37 @@
     hid_of = lambda d: pl.ds(pl.multiple_of(d * hid, hid), hid)
     peers = [other(r & 1, (r >> 1) & 1, r >> 2) for r in (6, 2, 4, 7, 3, 5, 1)]
 
-    def to_all(src_of, dst, send_sem, recv_sem):
-        return [pltpu.make_async_remote_copy(
-            src_ref=src_of(dest), dst_ref=dst, send_sem=send_sem.at[n], recv_sem=recv_sem.at[n],
-            device_id=(dest,), device_id_type=MESH) for n, dest in enumerate(peers)]
-
-    small = to_all(lambda dest: gain_ref, gain_all.at[me], g_send, g_recv)
+    def to_all(src_of, dst, seven, sems):
+        copies = [pltpu.make_async_remote_copy(
+            src_ref=src_of(dest), dst_ref=dst, send_sem=sems[0], recv_sem=sems[1],
+            device_id=(dest,), device_id_type=MESH) for dest in peers]
+        for copy in copies:
+            copy.start()
+        return pltpu.make_async_remote_copy(src_ref=seven, dst_ref=seven, send_sem=sems[0], recv_sem=sems[1],
+                                            device_id=(partner,), device_id_type=MESH)
+
     q_of = lambda d: pl.ds(pl.multiple_of(d * qw, qw), qw)
     kv_of = lambda d: pl.ds(pl.multiple_of(d * head_dim, head_dim), head_dim)
-    slices = (to_all(lambda dest: wq_ref.at[q_of(dest), :], w_head.at[0:qw, cols_of(me)], w_send.at[0], w_recv.at[0])
-              + to_all(lambda dest: wk_ref.at[kv_of(dest), :], w_head.at[qw:qw + head_dim, cols_of(me)], w_send.at[1], w_recv.at[1])
-              + to_all(lambda dest: wv_ref.at[kv_of(dest), :], w_head.at[qw + head_dim:, cols_of(me)], w_send.at[2], w_recv.at[2]))
-    for copy in small + slices:
-        copy.start()
-    x_gather = Gather(lambda d: x_all.at[tok_of(d), :], x_send, x_recv, where, own=x_ref)
+    seven_rows = pl.ds(0, 7 * rows_own)
+    small = [to_all(lambda dest: gain_ref, gain_all.at[me], gain_all.at[pl.ds(0, 7)], (g_send.at[0], g_recv.at[0]))]
+    slices = []
+    for i, (src, rows, low, high) in enumerate(((wq_ref, q_of, 0, qw), (wk_ref, kv_of, qw, qw + head_dim),
+                                                (wv_ref, kv_of, qw + head_dim, qw + 2 * head_dim))):
+        slices.append(to_all(lambda dest: src.at[rows(dest), :], w_head.at[low:high, cols_of(me)],
+                             w_head.at[low:high, seven_rows], (w_send.at[i], w_recv.at[i])))
+    x_gather = Gather(lambda d: x_all.at[tok_of(d), :], x_send, x_recv, where, x_all.at[pl.ds(0, 7 * tokens), :], own=x_ref)
     x_gather.start()
-    wo_gather = Gather(lambda d: wo_all.at[cols_of(d), :], wo_send, wo_recv, where, own=wo_ref)
+    wo_gather = Gather(lambda d: wo_all.at[cols_of(d), :], wo_send, wo_recv, where, wo_all.at[pl.ds(0, 7 * rows_own), :], own=wo_ref)
     bulk, parts = [], []
     quarter = rows_own // 4
-    for src, dst in ((wg_ref, w1_ref), (wu_ref, w3_ref)):
+    for mat, (src, dst) in enumerate(((wg_ref, w1_ref), (wu_ref, w3_ref))):
         for low, high in ((0, 16), (16, quarter), (quarter, 2 * quarter), (2 * quarter, 3 * quarter), (3 * quarter, rows_own)):
             parts.append(range(len(bulk), len(bulk) + len(peers)))
             for dest in peers:
                 bulk.append(pltpu.make_async_remote_copy(
                     src_ref=src.at[pl.ds(low, high - low), hid_of(dest)],
                     dst_ref=dst.at[pl.ds(pl.multiple_of(me * rows_own + low, 16), high - low), :],
-                    send_sem=bulk_send.at[len(bulk)], recv_sem=bulk_recv.at[len(bulk)], device_id=(dest,), device_id_type=MESH))
+                    send_sem=bulk_send.at[mat], recv_sem=bulk_recv.at[mat], device_id=(dest,), device_id_type=MESH))
 
     def start_bulk(*which):
         for part in which:
@@ -828,7 +844,7 @@
     lax.fori_loop(0, heads, one_head, 0)
     for h in range(heads):
         o_own[:, h * head_dim:(h + 1) * head_dim] = o_scr[h]
-    o_gather = Gather(lambda d: o_all.at[:, cols_of(d)], o_send, o_recv, where, own=o_own)
+    o_gather = Gather(lambda d: o_all.at[:, cols_of(d)], o_send, o_recv, where, o_all.at[:, pl.ds(0, 7 * rows_own)], own=o_own)
     o_gather.start()
     wo_gather.got_first()
     wo_gather.got_second()
@@ -906,8 +922,10 @@
         copy.wait_send()
     for gather in (x_gather, wo_gather, o_gather):
         gather.drain()
-    for copy in bulk:
-        copy.wait()
+    for mat, dst in enumerate((w1_ref, w3_ref)):
+        seven = dst.at[pl.ds(0, 7 * rows_own), :]
+        pltpu.make_async_remote_copy(src_ref=seven, dst_ref=seven, send_sem=bulk_send.at[mat], recv_sem=bulk_recv.at[mat],
+                                     device_id=(partner,), device_id_type=MESH).wait()
     for load, store in local:
         store.wait()
     for copy in stores:
@@ -928,8 +946,8 @@
     outs = (shape((heads, seq_len, head_dim), BF16), shape((seq_len, head_dim), BF16), shape((seq_len, head_dim), BF16),
             shape((heads * head_dim, seq_len), BF16), shape((rows_own, seq_len), BF16),
             shape((seq_len, 128), F32), shape((seq_len, 128), F32), shape((8, model), F32), shape((tokens, model), BF16))
-    pairs = [dma((7,)), dma((7,)), dma((3, 7)), dma((3, 7)), dma((7,)), dma((7,)), dma((7,)), dma((7,)),
-             dma((70,)), dma((70,)), dma((7,)), dma((7,))]
+    pairs = [dma((1,)), dma((1,)), dma((3,)), dma((3,)), dma((1,)), dma((7,)), dma((1,)), dma((7,)),
+             dma((2,)), dma((2,)), dma((1,)), dma((7,))]
     return pl.pallas_call(
         functools.partial(attention_comm_kernel, 'sp', heads), name='attention_comm',
         in_specs=[hbm] + [vmem] * 4 + [hbm] * 6, out_specs=[hbm] * 12,
@@ -943,39 +961,28 @@
     )(x_in, positions, gain1, gain2, jnp.asarray(freq), w_q, w_k, w_v, wo_own, w_gate, w_up)
 
 
-def hand_over_kernel(n_far, n_near, *refs):
-    n_in = n_far + n_near
+def hand_over_kernel(n_in, *refs):
     sources, gains, results = refs[:n_in], refs[n_in], refs[n_in + 1:2 * n_in + 1]
-    gain_outs, stages = refs[2 * n_in + 1:2 * n_in + 3], refs[2 * n_in + 3:2 * n_in + 3 + n_far]
-    in_sem, out_sem = refs[2 * n_in + 3 + n_far:]
-    loads = [pltpu.make_async_copy(sources[i], stages[i], in_sem.at[i]) for i in range(n_far)]
-    stores = [pltpu.make_async_copy(stages[i] if i < n_far else sources[i], results[i], out_sem.at[i]) for i in range(n_in)]
-    for load in loads:
-        load.start()
-    for store in stores[n_far:]:
+    gain_outs, sem = refs[2 * n_in + 1:2 * n_in + 3], refs[2 * n_in + 3]
+    stores = [pltpu.make_async_copy(sources[i], results[i], sem.at[i]) for i in range(n_in)]
+    for store in stores:
         store.start()
     for i in range(2):
         gain_outs[i][...] = gains[i, :]
-    for load, store in zip(loads, stores):
-        load.wait()
-        store.start()
     for store in stores:
         store.wait()
 
 
-def hand_over(far, near, gains):
+def hand_over(arrays, gains):
     shape = jax.ShapeDtypeStruct
-    arrays = far + near
     hbm, vmem = pl.BlockSpec(memory_space=pltpu.HBM), pl.BlockSpec(memory_space=pltpu.VMEM)
-    dma = pltpu.SemaphoreType.DMA
     return pl.pallas_call(
-        functools.partial(hand_over_kernel, len(far), len(near)), name='hand_over',
-        in_specs=[hbm] * len(far) + [vmem] * (len(near) + 1), out_specs=[hbm] * len(arrays) + [vmem] * 2,
+        functools.partial(hand_over_kernel, len(arrays)), name='hand_over',
+        in_specs=[vmem] * (len(arrays) + 1), out_specs=[hbm] * len(arrays) + [vmem] * 2,
         out_shape=[shape(a.shape, a.dtype) for a in arrays] + [shape((gains.shape[1],), F32)] * 2,
-        scratch_shapes=[pltpu.VMEM(a.shape, a.dtype) for a in far] + [dma((len(far),)), dma((len(arrays),))],
-        compiler_params=pltpu.CompilerParams(vmem_limit_bytes=12 * 1024 * 1024),
-    )(*[pltpu.with_memory_space_constraint(a, pltpu.HBM) for a in far],
-      *[pltpu.with_memory_space_constraint(a, pltpu.VMEM) for a in near + (gains,)])
+        scratch_shapes=[pltpu.SemaphoreType.DMA((len(arrays),))],
+        compiler_params=pltpu.CompilerParams(vmem_limit_bytes=1024 * 1024),
+    )(*[pltpu.with_memory_space_constraint(a, pltpu.VMEM) for a in arrays + (gains,)])
 
 
 def solution(mesh):
@@ -991,12 +998,12 @@
         (q_rot, k_rot, v_lin, o_t, u_t, cos_tab, sin_tab, g_full, hidden,
          mlp_in, w1, w3) = attention_step(heads, x_in, positions, norm1_gain, norm2_gain, flat(w_q), flat(w_k), flat(w_v), wo_own, w_gate, w_up)
         d_w1s, d_w3s, d_down, y_out, dh_own, d_g2 = mlp_step(mlp_in, d_out, w1, w3, w_down, hidden, g_full)
-        d_wo, d_wq_t, d_wk_t, d_wv_t, d_w1, d_w3, d_x, d_gains = attention_backward_step(
+        d_wo, d_wq_t, d_wk_t, d_wv_t, d_w1, d_w3, d_x, d_gains, d_down, y_out = attention_backward_step(
             heads, dh_own, wo_own, o_t, q_rot, k_rot, v_lin, (cos_tab, sin_tab),
-            d_w1s, d_w3s, flat(w_q), flat(w_k), flat(w_v), u_t, x_in, g_full, d_g2)
+            d_w1s, d_w3s, flat(w_q), flat(w_k), flat(w_v), u_t, x_in, g_full, d_g2, d_down, y_out)
         from_cols = lambda d, w: d.reshape(w.shape[1], w.shape[2], rows_own).transpose(2, 0, 1)
         (d_down, y_out, d_w1, d_w3, d_wo, d_wq_t, d_wk_t, d_wv_t, d_x, d_g1, d_g2) = hand_over(
-            (d_down, y_out), (d_w1, d_w3, d_wo, d_wq_t, d_wk_t, d_wv_t, d_x), d_gains)
+            (d_down, y_out, d_w1, d_w3, d_wo, d_wq_t, d_wk_t, d_wv_t, d_x), d_gains)
         return (y_out, d_x, d_g1, d_g2, from_cols(d_wq_t, w_q), from_cols(d_wk_t, w_k), from_cols(d_wv_t, w_v),
                 d_wo.reshape(w_o.shape), d_w1, d_w3, d_down)
 

time: 691 us -> 685 us (level)
  no operation moved by 1% of the time
where the time goes in v8:
time: 685 us
  Pallas kernels  684 us (100%)
    pallas_call x1, Pallas kernels, attention_backward_step(): pl.pallas_call(functools.partial(attn_bwd_comm_kernel, 'sp', heads), name...  281 us
    pallas_call x1, Pallas kernels, attention_step(): pl.pallas_call(functools.partial(attention_comm_kernel, 'sp', heads), nam...  216 us
    pallas_call x1, Pallas kernels, mlp_step(): pl.pallas_call(functools.partial(mlp_comm_kernel, 'sp'), name='mlp_comm',...  177 us

profile of v8, /device:TPU:0, one launch (start us, length us, event | category | flops | bytes accessed | tf_op | source)
XLA Modules:
  0.0 685.2 jit_solution(3136418723450549066)
XLA Ops:
  0.6 215.8 %attention_comm.1 = (bf16[4,2048,64]{2,1,0:T(8,128)(2,1)}, bf16[2048,64]{1,0:T(8,128)(2,1)}, bf16[2048,64]{1,0:T(8,128)(2,1)}, bf16[256,2048]{1,0:T(8,128)(2,1)}...) custom-call(bf16[256,2048]{1,0:T(8,128)(2,1)} %x_hbm.1, ...), custom_call_target="tpu_custom_call" | custom-call | tf_op jit(solution)/shard_map/attention_comm/pallas_call | solution.py:951
  216.5 176.5 %mlp_comm.1 = (f32[2048,1024]{1,0:T(8,128)}, f32[2048,1024]{1,0:T(8,128)}, f32[1024,2048]{1,0:T(8,128)}, bf16[256,2048]{1,0:T(8,128)(2,1)}, bf16[256,2048]{1,0:T...) custom-call(bf16[2048,2048]{1,0:T(8,128)(2,1)} %get-tuple-element.50.m_ref, bf16[256,2048]{1,0:T(8,128)(2,1)} %dout_own.1, ...), custom_call_target="tpu_custom_call" | custom-call | tf_op jit(solution)/shard_map/mlp_comm/pallas_call | solution.py:673
  393.0 280.7 %attn_bwd_comm.1 = (f32[256,2048]{1,0:T(8,128)S(1)}, f32[2048,256]{1,0:T(8,128)S(1)}, f32[512,256]{1,0:T(8,128)S(1)}, f32[512,256]{1,0:T(8,128)S(1)}, f32[256,81...) custom-call(bf16[256,2048]{1,0:T(8,128)(2,1)} %get-tuple-element.55., ...), custom_call_target="tpu_custom_call" | custom-call | tf_op jit(solution)/shard_map/attn_bwd_comm/pallas_call | solution.py:336
  673.7 11.3 %hand_over.1 = (f32[1024,2048]{1,0:T(8,128)}, bf16[256,2048]{1,0:T(8,128)(2,1)}, f32[256,8192]{1,0:T(8,128)}, f32[256,8192]{1,0:T(8,128)}, f32[256,2048]{1,0:T(8...) custom-call(f32[1024,2048]{1,0:T(8,128)S(1)} %get-tuple-element.68.r, ...), custom_call_target="tpu_custom_call" | custom-call | tf_op jit(solution)/shard_map/hand_over/pallas_call | solution.py:979

commit v9 on v8

--- a/solution.py
+++ b/solution.py
@@ -648,7 +648,7 @@
         dh_own[part, :] = (dh_own[part, :].astype(F32) + d_norm).astype(BF16)
         dg2_ref[...] += d_gain
         return 0
-    lax.fori_loop(0, tokens // 16, hidden_grad, 0)
+    lax.fori_loop(0, tokens // 16, hidden_grad, 0, unroll=4)
     own_out = pltpu.make_async_copy(dh_own, dh_hbm, own_sem.at[3])
     own_out.start()
     dg2_store = pltpu.make_async_copy(dg2_ref, dg2_hbm, own_sem.at[4])
@@ -695,15 +695,15 @@
     return jnp.where(low, both, pltpu.roll(both, 32, 1)), jnp.where(low, -pltpu.roll(both, 96, 1), both)
 
 
-def attention_comm_kernel(axis, heads, x_ref, pos_ref, gain1_ref, gain2_ref, freq_ref, wq_ref, wk_ref, wv_ref, wo_ref, wg_ref, wu_ref,
+def attention_comm_kernel(axis, heads, x_ref, pos_hbm, gain1_hbm, gain2_hbm, freq_hbm, wq_ref, wk_ref, wv_ref, wo_ref, wg_ref, wu_ref,
                           q_hbm, k_hbm, v_hbm, ot_hbm, ut_hbm, cos_hbm, sin_hbm, gfull_hbm, h_hbm, m_ref, w1_ref, w3_ref,
-                          q_ref, k_ref, v_ref, ot_ref, ut_ref, cos_ref, sin_ref, gfull_ref, h_ref, gain_ref, x_all, gain_all, w_head, wo_all, o_all, u_blk, qkv_blk, o_scr, o_own, h_scr, m_out, stage,
+                          q_ref, k_ref, v_ref, ot_ref, ut_ref, cos_ref, sin_ref, gfull_ref, h_ref, pos_ref, gain1_ref, gain2_ref, freq_ref, gain_ref, x_all, gain_all, w_head, wo_all, o_all, u_blk, qkv_blk, o_scr, o_own, h_scr, m_out, stage,
                           g_send, g_recv, w_send, w_recv, x_send, x_recv, wo_send, wo_recv, bulk_send, bulk_recv,
                           o_send, o_recv, m_loc, m_send, m_recv, loc_sem, own_sem, st_sem):
-    gain_ref[...] = jnp.zeros_like(gain_ref)
-    gain_ref[0:1, :] = gain1_ref[...].astype(F32).reshape(1, -1)
-    gain_ref[1:2, :] = gain2_ref[...].astype(F32).reshape(1, -1)
-    gain_ref[2:3, :] = pos_ref[...].astype(F32).reshape(1, -1)
+    tiny = [pltpu.make_async_copy(src, dst, own_sem.at[8 + i]) for i, (src, dst) in enumerate((
+        (gain1_hbm, gain1_ref), (gain2_hbm, gain2_ref), (pos_hbm, pos_ref), (freq_hbm, freq_ref)))]
+    for copy in tiny:
+        copy.start()
     where = place(axis)
     me, other, first, second = where
     core = lax.rem(me, 2)
@@ -730,7 +730,6 @@
     q_of = lambda d: pl.ds(pl.multiple_of(d * qw, qw), qw)
     kv_of = lambda d: pl.ds(pl.multiple_of(d * head_dim, head_dim), head_dim)
     seven_rows = pl.ds(0, 7 * rows_own)
-    small = [to_all(lambda dest: gain_ref, gain_all.at[me], gain_all.at[pl.ds(0, 7)], (g_send.at[0], g_recv.at[0]))]
     slices = []
     for i, (src, rows, low, high) in enumerate(((wq_ref, q_of, 0, qw), (wk_ref, kv_of, qw, qw + head_dim),
                                                 (wv_ref, kv_of, qw + head_dim, qw + 2 * head_dim))):
@@ -738,6 +737,13 @@
                              w_head.at[low:high, seven_rows], (w_send.at[i], w_recv.at[i])))
     x_gather = Gather(lambda d: x_all.at[tok_of(d), :], x_send, x_recv, where, x_all.at[pl.ds(0, 7 * tokens), :], own=x_ref)
     x_gather.start()
+    for copy in tiny:
+        copy.wait()
+    gain_ref[...] = jnp.zeros_like(gain_ref)
+    gain_ref[0:1, :] = gain1_ref[...].astype(F32).reshape(1, -1)
+    gain_ref[1:2, :] = gain2_ref[...].astype(F32).reshape(1, -1)
+    gain_ref[2:3, :] = pos_ref[...].astype(F32).reshape(1, -1)
+    small = [to_all(lambda dest: gain_ref, gain_all.at[me], gain_all.at[pl.ds(0, 7)], (g_send.at[0], g_recv.at[0]))]
     wo_gather = Gather(lambda d: wo_all.at[cols_of(d), :], wo_send, wo_recv, where, wo_all.at[pl.ds(0, 7 * rows_own), :], own=wo_ref)
     bulk, parts = [], []
     quarter = rows_own // 4
@@ -938,7 +944,7 @@
     head_dim = wo_own.shape[0] // heads
     rows_own, hid = w_gate.shape[0], w_gate.shape[1] // 8
     shape = jax.ShapeDtypeStruct
-    hbm, vmem = pl.BlockSpec(memory_space=pl.ANY), pl.BlockSpec(memory_space=pltpu.VMEM)
+    hbm = pl.BlockSpec(memory_space=pl.ANY)
     dma = pltpu.SemaphoreType.DMA
     vm = lambda *dims, dtype=BF16: pltpu.VMEM(dims, dtype)
     steps = np.arange(head_dim // 2, dtype=np.float32) * np.float32(2.0 / head_dim)
@@ -950,13 +956,14 @@
              dma((2,)), dma((2,)), dma((1,)), dma((7,))]
     return pl.pallas_call(
         functools.partial(attention_comm_kernel, 'sp', heads), name='attention_comm',
-        in_specs=[hbm] + [vmem] * 4 + [hbm] * 6, out_specs=[hbm] * 12,
+        in_specs=[hbm] * 11, out_specs=[hbm] * 12,
         out_shape=[*outs, shape((seq_len, model), BF16), shape((model, hid), BF16), shape((model, hid), BF16)],
         scratch_shapes=[vm(*t.shape, dtype=t.dtype) for t in outs] + [
+            vm(tokens, dtype=jnp.int32), vm(rows_own), vm(rows_own), vm(1, 2 * head_dim, dtype=F32),
             vm(8, rows_own, dtype=F32), vm(seq_len, model), vm(8, 8, rows_own, dtype=F32),
             vm(384, model), vm(model, model), vm(seq_len, model), vm(tokens, model), vm(tokens, 384), vm(heads, seq_len, head_dim),
             vm(seq_len, heads * head_dim), vm(tokens, model, dtype=F32), vm(2, tokens, model), vm(2, rows_own, hid)] + pairs + [
-            dma((2,)), dma((4,)), dma((4,)), dma((4,)), dma((8,)), dma((9,))],
+            dma((2,)), dma((4,)), dma((4,)), dma((4,)), dma((12,)), dma((9,))],
         compiler_params=pltpu.CompilerParams(collective_id=0, has_side_effects=True, vmem_limit_bytes=63 * 1024 * 1024),
     )(x_in, positions, gain1, gain2, jnp.asarray(freq), w_q, w_k, w_v, wo_own, w_gate, w_up)
 

time: 685 us -> 684 us (level)
  no operation moved by 1% of the time
where the time goes in v9:
time: 684 us
  Pallas kernels  683 us (100%)
    pallas_call x1, Pallas kernels, attention_backward_step(): pl.pallas_call(functools.partial(attn_bwd_comm_kernel, 'sp', heads), name...  281 us
    pallas_call x1, Pallas kernels, attention_step(): pl.pallas_call(functools.partial(attention_comm_kernel, 'sp', heads), nam...  216 us
    pallas_call x1, Pallas kernels, mlp_step(): pl.pallas_call(functools.partial(mlp_comm_kernel, 'sp'), name='mlp_comm',...  175 us

profile of v9, /device:TPU:0, one launch (start us, length us, event | category | flops | bytes accessed | tf_op | source)
XLA Modules:
  0.0 683.9 jit_solution(4741763209880853753)
XLA Ops:
  0.6 215.6 %attention_comm.1 = (bf16[4,2048,64]{2,1,0:T(8,128)(2,1)}, bf16[2048,64]{1,0:T(8,128)(2,1)}, bf16[2048,64]{1,0:T(8,128)(2,1)}, bf16[256,2048]{1,0:T(8,128)(2,1)}...) custom-call(bf16[256,2048]{1,0:T(8,128)(2,1)} %x_hbm.1, ...), custom_call_target="tpu_custom_call" | custom-call | tf_op jit(solution)/shard_map/attention_comm/pallas_call | solution.py:957
  216.2 175.4 %mlp_comm.1 = (f32[2048,1024]{1,0:T(8,128)}, f32[2048,1024]{1,0:T(8,128)}, f32[1024,2048]{1,0:T(8,128)}, bf16[256,2048]{1,0:T(8,128)(2,1)}, bf16[256,2048]{1,0:T...) custom-call(bf16[2048,2048]{1,0:T(8,128)(2,1)} %get-tuple-element.50.m_ref, bf16[256,2048]{1,0:T(8,128)(2,1)} %dout_own.1, ...), custom_call_target="tpu_custom_call" | custom-call | tf_op jit(solution)/shard_map/mlp_comm/pallas_call | solution.py:673
  391.6 280.7 %attn_bwd_comm.1 = (f32[256,2048]{1,0:T(8,128)S(1)}, f32[2048,256]{1,0:T(8,128)S(1)}, f32[512,256]{1,0:T(8,128)S(1)}, f32[512,256]{1,0:T(8,128)S(1)}, f32[256,81...) custom-call(bf16[256,2048]{1,0:T(8,128)(2,1)} %get-tuple-element.55., ...), custom_call_target="tpu_custom_call" | custom-call | tf_op jit(solution)/shard_map/attn_bwd_comm/pallas_call | solution.py:336
  672.3 11.3 %hand_over.1 = (f32[1024,2048]{1,0:T(8,128)}, bf16[256,2048]{1,0:T(8,128)(2,1)}, f32[256,8192]{1,0:T(8,128)}, f32[256,8192]{1,0:T(8,128)}, f32[256,2048]{1,0:T(8...) custom-call(f32[1024,2048]{1,0:T(8,128)S(1)} %get-tuple-element.68.r, ...), custom_call_target="tpu_custom_call" | custom-call | tf_op jit(solution)/shard_map/hand_over/pallas_call | solution.py:986

commit v10 on v9

--- a/solution.py
+++ b/solution.py
@@ -13,6 +13,7 @@
 F32 = jnp.float32
 BF16 = jnp.bfloat16
 BLK = 256
+EARLY_ROWS = 8
 
 
 def dot(lhs, rhs, lhs_dim, rhs_dim):
@@ -116,7 +117,7 @@
 
 
 def attn_bwd_comm_kernel(axis, heads, dh_hbm, wo_hbm, ot_hbm, q_hbm, k_hbm, v_hbm, cos_hbm, sin_hbm,
-                         dw1_ref, dw3_ref, wq_hbm, wk_hbm, wv_hbm, ut_hbm, x_hbm, g_hbm, dg2_hbm, ddown_hbm, y_hbm,
+                         dw1_ref, dw3_ref, wq_hbm, wk_hbm, wv_hbm, ut_hbm, x_hbm, g_hbm, dg2_hbm, ddown_hbm, y_hbm, early_hbm,
                          dwo_ref, dwq_ref, dwk_ref, dwv_ref, out1_ref, out3_ref, dx_ref, dg_ref, ddown_ref, y_ref,
                          dh_own, wo_ref, ot_ref, q_ref, k_ref, v_ref, cos_ref, sin_ref, wq_ref, wk_ref, wv_ref, ut_ref, g_ref, dg2_ref,
                          pool, do_scr, dg_own, dg_all, dk_acc, dv_acc, du_acc,
@@ -148,7 +149,8 @@
     peers = [other(r & 1, (r >> 1) & 1, r >> 2) for r in (2, 4, 6, 3, 5, 7, 1)]
     bulk, parts = [], []
     for mat, (src, dst) in enumerate(pairs):
-        for low, high in ((0, 8), (8, rows_own // 2), (rows_own // 2, rows_own)):
+        skip = (EARLY_ROWS, 0)[mat]
+        for low, high in ((skip, skip + 8), (skip + 8, rows_own // 2), (rows_own // 2, rows_own)):
             parts.append(range(len(bulk), len(bulk) + len(peers)))
             for dest in peers:
                 bulk.append(pltpu.make_async_remote_copy(
@@ -168,6 +170,8 @@
     local = [pltpu.make_async_copy(src.at[rows_of(me), :], dst.at[:, hid_of(me)], loc_sem.at[i]) for i, (src, dst) in enumerate(pairs)]
     for copy in local:
         copy.start()
+    for dest in peers:
+        pltpu.make_async_copy(early_hbm.at[:, hid_of(dest)], out1_ref.at[0:EARLY_ROWS, hid_of(dest)], loc_sem.at[2]).start()
     need('dh', 'wo', 'ot')
     pool[tok_of(me), 0:model] = dh_own[...]
     h_gather.got_first()
@@ -312,14 +316,17 @@
         pltpu.make_async_copy(sent, sent, sem.at[0]).wait()
     need('ddown', 'y')
     for mat, (src, dst) in enumerate(pairs):
-        sent, got = src.at[pl.ds(0, 7 * rows_own), :], dst.at[:, pl.ds(0, 7 * hid)]
+        rows = rows_own - (EARLY_ROWS, 0)[mat]
+        sent, got = src.at[pl.ds(0, 7 * rows), :], dst.at[0:rows, pl.ds(0, 7 * hid)]
         pltpu.make_async_copy(sent, sent, bulk_send.at[mat]).wait()
         pltpu.make_async_copy(got, got, bulk_recv.at[mat]).wait()
     for copy in local:
         copy.wait()
-
-
-def attention_backward_step(heads, dh_own, wo_own, o_t, q_rot, k_rot, v_lin, tables, d_w1, d_w3, w_q, w_k, w_v, u_t, x_in, gains, d_g2, d_down, y_out):
+    seven = out1_ref.at[0:EARLY_ROWS, pl.ds(0, 7 * hid)]
+    pltpu.make_async_copy(seven, seven, loc_sem.at[2]).wait()
+
+
+def attention_backward_step(heads, dh_own, wo_own, o_t, q_rot, k_rot, v_lin, tables, d_w1, d_w3, w_q, w_k, w_v, u_t, x_in, gains, d_g2, d_down, y_out, early_rows):
     seq_len, model = k_rot.shape[0], x_in.shape[1]
     head_dim = k_rot.shape[1]
     tokens = x_in.shape[0]
@@ -335,24 +342,24 @@
     vmem, far = pl.BlockSpec(memory_space=pltpu.VMEM), pl.BlockSpec(memory_space=pltpu.HBM)
     return pl.pallas_call(
         functools.partial(attn_bwd_comm_kernel, 'sp', heads), name='attn_bwd_comm',
-        in_specs=[hbm] * 17 + [far] * 2, out_specs=[vmem] * 10,
+        in_specs=[hbm] * 17 + [far] * 3, out_specs=[vmem] * 10,
         out_shape=[pltpu.VMEM(dims, dtype) for dims, dtype in outs],
         scratch_shapes=[vm(*t.shape, dtype=t.dtype) for t in early + late[:4] + late[5:]] + [
             vm(seq_len, 8 * 384), vm(heads, seq_len, head_dim),
             vm(8, model, dtype=F32), vm(8, 8, rows_own, dtype=F32),
             vm(seq_len, head_dim, dtype=F32), vm(seq_len, head_dim, dtype=F32),
             vm(seq_len, rows_own, dtype=F32),
-            dma((2,)), dma((2,)), dma((1,)), dma((7,)), dma((1,)), dma((7,)), dma((1,)), dma((1,)), dma((1,)), dma((1,)), dma((2,)), dma((17,)), pltpu.SemaphoreType.REGULAR((3,))],
+            dma((2,)), dma((2,)), dma((1,)), dma((7,)), dma((1,)), dma((7,)), dma((1,)), dma((1,)), dma((1,)), dma((1,)), dma((3,)), dma((17,)), pltpu.SemaphoreType.REGULAR((3,))],
         compiler_params=pltpu.CompilerParams(collective_id=2, has_side_effects=True, vmem_limit_bytes=34340864),
-    )(*early, d_w1, d_w3, *late, *[pltpu.with_memory_space_constraint(a, pltpu.HBM) for a in (d_down, y_out)])
+    )(*early, d_w1, d_w3, *late, *[pltpu.with_memory_space_constraint(a, pltpu.HBM) for a in (d_down, y_out, early_rows)])
 
 
 def mlp_comm_kernel(axis, m_ref, dout_own, w1_hbm, w3_hbm, w2_hbm, h_hbm, g_hbm,
-                    dw1_ref, dw3_ref, dw2_ref, y_hbm, dh_hbm, dg2_hbm, dout_ref,
+                    dw1_ref, dw3_ref, dw2_ref, y_hbm, dh_hbm, dg2_hbm, early_ref, dout_ref,
                     w1_ref, w3_ref, w2_ref, h_ref, g_ref, y_ref, dg2_ref,
                     glu, gate_s, up_s, outbox, chip_sum, inbox, blk, m_col, do_col, mt_scr, dot_scr, st1, st3, st2, dh_own,
                     part_send, part_recv, mail_send, mail_recv, do_send, do_recv,
-                    in_sem, col_sem, out_sem, own_sem, ld_sem, credit):
+                    in_sem, col_sem, out_sem, own_sem, ld_sem, early_sem, credit):
     loads = [pltpu.make_async_copy(src, dst, ld_sem.at[i]) for i, (src, dst) in enumerate((
         (w1_hbm, w1_ref), (w3_hbm, w3_ref), (w2_hbm, w2_ref), (h_hbm, h_ref), (g_hbm, g_ref)))]
     own_in = pltpu.make_async_copy(dout_own, dh_own, own_sem.at[0])
@@ -637,6 +644,13 @@
         return 0
     lax.fori_loop(2, 4, grad_step, 0)
     weight_grads(2, 8)
+    rows = early_ref.shape[0]
+    for r in (2, 4, 6, 3, 5, 7, 1):
+        dest = other(r & 1, (r >> 1) & 1, r >> 2)
+        pltpu.make_async_remote_copy(
+            src_ref=dw1_ref.at[pl.ds(pl.multiple_of(dest * 256, 256), rows), :],
+            dst_ref=early_ref.at[:, pl.ds(pl.multiple_of(me * hid, hid), hid)], send_sem=early_sem.at[0],
+            recv_sem=early_sem.at[1], device_id=(dest,), device_id_type=MESH).start()
     grad_round.mail(1).wait_recv()
     grad_round.mail(2).wait_recv()
     dg2_ref[...] = jnp.zeros_like(dg2_ref)
@@ -657,6 +671,9 @@
         grad_round.to_partner(step).wait_send()
     for kind in range(3):
         grad_round.mail(kind).wait_send()
+    seven = early_ref.at[:, pl.ds(0, 7 * hid)]
+    for i in range(2):
+        pltpu.make_async_copy(seven, seven, early_sem.at[i]).wait()
     do_gather.drain()
     own_out.wait()
     y_store.wait()
@@ -672,9 +689,10 @@
     vm = lambda *dims, dtype=BF16: pltpu.VMEM(dims, dtype)
     return pl.pallas_call(
         functools.partial(mlp_comm_kernel, 'sp'), name='mlp_comm',
-        in_specs=[hbm] * 7, out_specs=[hbm] * 7,
+        in_specs=[hbm] * 7, out_specs=[hbm] * 8,
         out_shape=[shape((model, hid), F32), shape((model, hid), F32), shape((hid, model), F32),
-                   shape(hidden.shape, BF16), shape(hidden.shape, BF16), shape((1, model), F32), shape((seq_len, model), BF16)],
+                   shape(hidden.shape, BF16), shape(hidden.shape, BF16), shape((1, model), F32), shape((EARLY_ROWS, 8 * hid), F32),
+                   shape((seq_len, model), BF16)],
         scratch_shapes=[vm(*t.shape, dtype=t.dtype) for t in (w1, w3, w2, hidden, gains)] + [
             vm(tokens, model), vm(1, model, dtype=F32),
             vm(seq_len, hid), vm(seq_len, hid), vm(seq_len, hid),
@@ -682,9 +700,9 @@
             vm(2, tokens, model), vm(seq_len, 256), vm(seq_len, 256), vm(256, seq_len), vm(256, seq_len),
             vm(256, hid, dtype=F32), vm(256, hid, dtype=F32), vm(hid, 256, dtype=F32), vm(tokens, model),
             dma((2, 4)), dma((2, 4)), dma((2, 3)), dma((2, 3)), dma((1,)), dma((7,)),
-            dma((2,)), dma((2,)), dma((3,)), dma((5,)), dma((5,)), pltpu.SemaphoreType.REGULAR((5,))],
+            dma((2,)), dma((2,)), dma((3,)), dma((5,)), dma((5,)), dma((2,)), pltpu.SemaphoreType.REGULAR((5,))],
         compiler_params=pltpu.CompilerParams(collective_id=1, has_side_effects=True, vmem_limit_bytes=63 * 1024 * 1024),
-    )(m_all, d_out, w1, w3, w2, hidden, gains)[:6]
+    )(m_all, d_out, w1, w3, w2, hidden, gains)[:7]
 
 
 def spread_tables(packed, upper):
@@ -1004,10 +1022,10 @@
         wo_own = w_o.reshape(-1, model)
         (q_rot, k_rot, v_lin, o_t, u_t, cos_tab, sin_tab, g_full, hidden,
          mlp_in, w1, w3) = attention_step(heads, x_in, positions, norm1_gain, norm2_gain, flat(w_q), flat(w_k), flat(w_v), wo_own, w_gate, w_up)
-        d_w1s, d_w3s, d_down, y_out, dh_own, d_g2 = mlp_step(mlp_in, d_out, w1, w3, w_down, hidden, g_full)
+        d_w1s, d_w3s, d_down, y_out, dh_own, d_g2, early = mlp_step(mlp_in, d_out, w1, w3, w_down, hidden, g_full)
         d_wo, d_wq_t, d_wk_t, d_wv_t, d_w1, d_w3, d_x, d_gains, d_down, y_out = attention_backward_step(
             heads, dh_own, wo_own, o_t, q_rot, k_rot, v_lin, (cos_tab, sin_tab),
-            d_w1s, d_w3s, flat(w_q), flat(w_k), flat(w_v), u_t, x_in, g_full, d_g2, d_down, y_out)
+            d_w1s, d_w3s, flat(w_q), flat(w_k), flat(w_v), u_t, x_in, g_full, d_g2, d_down, y_out, early)
         from_cols = lambda d, w: d.reshape(w.shape[1], w.shape[2], rows_own).transpose(2, 0, 1)
         (d_down, y_out, d_w1, d_w3, d_wo, d_wq_t, d_wk_t, d_wv_t, d_x, d_g1, d_g2) = hand_over(
             (d_down, y_out, d_w1, d_w3, d_wo, d_wq_t, d_wk_t, d_wv_t, d_x), d_gains)

time: 684 us -> 682 us (level)
  no operation moved by 1% of the time
where the time goes in v10:
time: 682 us
  Pallas kernels  681 us (100%)
    pallas_call x1, Pallas kernels, attention_backward_step(): pl.pallas_call(functools.partial(attn_bwd_comm_kernel, 'sp', heads), name...  278 us
    pallas_call x1, Pallas kernels, attention_step(): pl.pallas_call(functools.partial(attention_comm_kernel, 'sp', heads), nam...  216 us
    pallas_call x1, Pallas kernels, mlp_step(): pl.pallas_call(functools.partial(mlp_comm_kernel, 'sp'), name='mlp_comm',...  176 us

profile of v10, /device:TPU:0, one launch (start us, length us, event | category | flops | bytes accessed | tf_op | source)
XLA Modules:
  0.0 681.6 jit_solution(555473104687039452)
XLA Ops:
  0.6 215.6 %attention_comm.1 = (bf16[4,2048,64]{2,1,0:T(8,128)(2,1)}, bf16[2048,64]{1,0:T(8,128)(2,1)}, bf16[2048,64]{1,0:T(8,128)(2,1)}, bf16[256,2048]{1,0:T(8,128)(2,1)}...) custom-call(bf16[256,2048]{1,0:T(8,128)(2,1)} %x_hbm.1, ...), custom_call_target="tpu_custom_call" | custom-call | tf_op jit(solution)/shard_map/attention_comm/pallas_call | solution.py:975
  216.2 175.9 %mlp_comm.1 = (f32[2048,1024]{1,0:T(8,128)}, f32[2048,1024]{1,0:T(8,128)}, f32[1024,2048]{1,0:T(8,128)}, bf16[256,2048]{1,0:T(8,128)(2,1)}, bf16[256,2048]{1,0:T...) custom-call(bf16[2048,2048]{1,0:T(8,128)(2,1)} %get-tuple-element.51.m_ref, ...), custom_call_target="tpu_custom_call" | custom-call | tf_op jit(solution)/shard_map/mlp_comm/pallas_call | solution.py:690
  392.1 277.9 %attn_bwd_comm.1 = (f32[256,2048]{1,0:T(8,128)S(1)}, f32[2048,256]{1,0:T(8,128)S(1)}, f32[512,256]{1,0:T(8,128)S(1)}, f32[512,256]{1,0:T(8,128)S(1)}, f32[256,81...) custom-call(bf16[256,2048]{1,0:T(8,128)(2,1)} %get-tuple-element.56., ...), custom_call_target="tpu_custom_call" | custom-call | tf_op jit(solution)/shard_map/attn_bwd_comm/pallas_call | solution.py:343
  670.0 11.3 %hand_over.1 = (f32[1024,2048]{1,0:T(8,128)}, bf16[256,2048]{1,0:T(8,128)(2,1)}, f32[256,8192]{1,0:T(8,128)}, f32[256,8192]{1,0:T(8,128)}, f32[256,2048]{1,0:T(8...) custom-call(f32[1024,2048]{1,0:T(8,128)S(1)} %get-tuple-element.70.r, ...), custom_call_target="tpu_custom_call" | custom-call | tf_op jit(solution)/shard_map/hand_over/pallas_call | solution.py:1004

commit v11 on v10

--- a/solution.py
+++ b/solution.py
@@ -150,7 +150,7 @@
     bulk, parts = [], []
     for mat, (src, dst) in enumerate(pairs):
         skip = (EARLY_ROWS, 0)[mat]
-        for low, high in ((skip, skip + 8), (skip + 8, rows_own // 2), (rows_own // 2, rows_own)):
+        for low, high in ((skip, skip + 16), (skip + 16, rows_own // 2), (rows_own // 2, rows_own)):
             parts.append(range(len(bulk), len(bulk) + len(peers)))
             for dest in peers:
                 bulk.append(pltpu.make_async_remote_copy(
@@ -315,15 +315,15 @@
     for sent, sem in ((du_scr.at[pl.ds(0, 7 * tokens), :], du_send), (dg_own.at[:, pl.ds(0, 7 * rows_own)], dg_send)):
         pltpu.make_async_copy(sent, sent, sem.at[0]).wait()
     need('ddown', 'y')
+    for copy in local:
+        copy.wait()
+    seven = out1_ref.at[0:EARLY_ROWS, pl.ds(0, 7 * hid)]
+    pltpu.make_async_copy(seven, seven, loc_sem.at[2]).wait()
     for mat, (src, dst) in enumerate(pairs):
         rows = rows_own - (EARLY_ROWS, 0)[mat]
         sent, got = src.at[pl.ds(0, 7 * rows), :], dst.at[0:rows, pl.ds(0, 7 * hid)]
         pltpu.make_async_copy(sent, sent, bulk_send.at[mat]).wait()
         pltpu.make_async_copy(got, got, bulk_recv.at[mat]).wait()
-    for copy in local:
-        copy.wait()
-    seven = out1_ref.at[0:EARLY_ROWS, pl.ds(0, 7 * hid)]
-    pltpu.make_async_copy(seven, seven, loc_sem.at[2]).wait()
 
 
 def attention_backward_step(heads, dh_own, wo_own, o_t, q_rot, k_rot, v_lin, tables, d_w1, d_w3, w_q, w_k, w_v, u_t, x_in, gains, d_g2, d_down, y_out, early_rows):
@@ -946,14 +946,14 @@
         copy.wait_send()
     for gather in (x_gather, wo_gather, o_gather):
         gather.drain()
+    for load, store in local:
+        store.wait()
+    for copy in stores:
+        copy.wait()
     for mat, dst in enumerate((w1_ref, w3_ref)):
         seven = dst.at[pl.ds(0, 7 * rows_own), :]
         pltpu.make_async_remote_copy(src_ref=seven, dst_ref=seven, send_sem=bulk_send.at[mat], recv_sem=bulk_recv.at[mat],
                                      device_id=(partner,), device_id_type=MESH).wait()
-    for load, store in local:
-        store.wait()
-    for copy in stores:
-        copy.wait()
 
 
 def attention_step(heads, x_in, positions, gain1, gain2, w_q, w_k, w_v, wo_own, w_gate, w_up):
@@ -988,12 +988,14 @@
 
 def hand_over_kernel(n_in, *refs):
     sources, gains, results = refs[:n_in], refs[n_in], refs[n_in + 1:2 * n_in + 1]
-    gain_outs, sem = refs[2 * n_in + 1:2 * n_in + 3], refs[2 * n_in + 3]
+    gain_outs, lines, sem = refs[2 * n_in + 1:2 * n_in + 3], refs[2 * n_in + 3:2 * n_in + 5], refs[2 * n_in + 5]
     stores = [pltpu.make_async_copy(sources[i], results[i], sem.at[i]) for i in range(n_in)]
     for store in stores:
         store.start()
     for i in range(2):
-        gain_outs[i][...] = gains[i, :]
+        lines[i][...] = gains[i, :]
+        stores.append(pltpu.make_async_copy(lines[i], gain_outs[i], sem.at[n_in + i]))
+        stores[-1].start()
     for store in stores:
         store.wait()
 
@@ -1003,9 +1005,9 @@
     hbm, vmem = pl.BlockSpec(memory_space=pltpu.HBM), pl.BlockSpec(memory_space=pltpu.VMEM)
     return pl.pallas_call(
         functools.partial(hand_over_kernel, len(arrays)), name='hand_over',
-        in_specs=[vmem] * (len(arrays) + 1), out_specs=[hbm] * len(arrays) + [vmem] * 2,
+        in_specs=[vmem] * (len(arrays) + 1), out_specs=[hbm] * (len(arrays) + 2),
         out_shape=[shape(a.shape, a.dtype) for a in arrays] + [shape((gains.shape[1],), F32)] * 2,
-        scratch_shapes=[pltpu.SemaphoreType.DMA((len(arrays),))],
+        scratch_shapes=[pltpu.VMEM((gains.shape[1],), F32)] * 2 + [pltpu.SemaphoreType.DMA((len(arrays) + 2,))],
         compiler_params=pltpu.CompilerParams(vmem_limit_bytes=1024 * 1024),
     )(*[pltpu.with_memory_space_constraint(a, pltpu.VMEM) for a in arrays + (gains,)])
 

time: 682 us -> 681 us (level)
  no operation moved by 1% of the time
where the time goes in v11:
time: 681 us
  Pallas kernels  680 us (100%)
    pallas_call x1, Pallas kernels, attention_backward_step(): pl.pallas_call(functools.partial(attn_bwd_comm_kernel, 'sp', heads), name...  278 us
    pallas_call x1, Pallas kernels, attention_step(): pl.pallas_call(functools.partial(attention_comm_kernel, 'sp', heads), nam...  216 us
    pallas_call x1, Pallas kernels, mlp_step(): pl.pallas_call(functools.partial(mlp_comm_kernel, 'sp'), name='mlp_comm',...  176 us

profile of v11, /device:TPU:0, one launch (start us, length us, event | category | flops | bytes accessed | tf_op | source)
XLA Modules:
  0.0 680.8 jit_solution(13753736247694491491)
XLA Ops:
  0.6 215.6 %attention_comm.1 = (bf16[4,2048,64]{2,1,0:T(8,128)(2,1)}, bf16[2048,64]{1,0:T(8,128)(2,1)}, bf16[2048,64]{1,0:T(8,128)(2,1)}, bf16[256,2048]{1,0:T(8,128)(2,1)}...) custom-call(bf16[256,2048]{1,0:T(8,128)(2,1)} %x_hbm.1, ...), custom_call_target="tpu_custom_call" | custom-call | tf_op jit(solution)/shard_map/attention_comm/pallas_call | solution.py:975
  216.2 175.9 %mlp_comm.1 = (f32[2048,1024]{1,0:T(8,128)}, f32[2048,1024]{1,0:T(8,128)}, f32[1024,2048]{1,0:T(8,128)}, bf16[256,2048]{1,0:T(8,128)(2,1)}, bf16[256,2048]{1,0:T...) custom-call(bf16[2048,2048]{1,0:T(8,128)(2,1)} %get-tuple-element.51.m_ref, ...), custom_call_target="tpu_custom_call" | custom-call | tf_op jit(solution)/shard_map/mlp_comm/pallas_call | solution.py:690
  392.1 277.7 %attn_bwd_comm.1 = (f32[256,2048]{1,0:T(8,128)S(1)}, f32[2048,256]{1,0:T(8,128)S(1)}, f32[512,256]{1,0:T(8,128)S(1)}, f32[512,256]{1,0:T(8,128)S(1)}, f32[256,81...) custom-call(bf16[256,2048]{1,0:T(8,128)(2,1)} %get-tuple-element.56., ...), custom_call_target="tpu_custom_call" | custom-call | tf_op jit(solution)/shard_map/attn_bwd_comm/pallas_call | solution.py:343
  669.8 10.8 %hand_over.1 = (f32[1024,2048]{1,0:T(8,128)}, bf16[256,2048]{1,0:T(8,128)(2,1)}, f32[256,8192]{1,0:T(8,128)}, f32[256,8192]{1,0:T(8,128)}, f32[256,2048]{1,0:T(8...) custom-call(f32[1024,2048]{1,0:T(8,128)S(1)} %get-tuple-element.70.r, ...), custom_call_target="tpu_custom_call" | custom-call | tf_op jit(solution)/shard_map/hand_over/pallas_call | solution.py:1006

commit v12 on v11

--- a/solution.py
+++ b/solution.py
@@ -55,11 +55,23 @@
     return me, other, first, second
 
 
-def greet(other):
+def greet(where):
+    _, other, first, second = where
     barrier = pltpu.get_barrier_semaphore()
-    for r in range(1, 8):
-        pl.semaphore_signal(barrier, inc=1, device_id=(other(r & 1, (r >> 1) & 1, r >> 2),), device_id_type=MESH)
-    pl.semaphore_wait(barrier, 7)
+    for device in (first, second, other(1, 0, 0)):
+        pl.semaphore_signal(barrier, inc=1, device_id=(device,), device_id_type=MESH)
+    pl.semaphore_wait(barrier, 3)
+
+
+def relay(where, sem, base):
+    _, other, first, second = where
+    partner = other(1, 0, 0)
+    for i, device in enumerate((first, second, partner)):
+        pl.semaphore_signal(sem.at[base + i], inc=1, device_id=(device,), device_id_type=MESH)
+    for i in range(3):
+        pl.semaphore_wait(sem.at[base + i], 1)
+    pl.semaphore_signal(sem.at[base + 3], inc=1, device_id=(partner,), device_id_type=MESH)
+    pl.semaphore_wait(sem.at[base + 3], 1)
 
 
 class Gather:
@@ -137,7 +149,7 @@
 
     where = place(axis)
     me, other, first, second = where
-    greet(other)
+    greet(where)
     seq_len, head_dim = k_ref.shape
     rows_own, hid = out1_ref.shape[0], dw1_ref.shape[1]
     tokens, model = x_hbm.shape
@@ -166,6 +178,7 @@
     dh_ref = pool.at[:, 0:model]
     h_gather = Gather(lambda d: dh_ref.at[tok_of(d), :], hg_send, hg_recv, where, dh_ref.at[pl.ds(0, 7 * tokens), :], own=dh_hbm)
     h_gather.start()
+    relay(where, credit, 3)
     start_bulk(0)
     local = [pltpu.make_async_copy(src.at[rows_of(me), :], dst.at[:, hid_of(me)], loc_sem.at[i]) for i, (src, dst) in enumerate(pairs)]
     for copy in local:
@@ -349,7 +362,7 @@
             vm(8, model, dtype=F32), vm(8, 8, rows_own, dtype=F32),
             vm(seq_len, head_dim, dtype=F32), vm(seq_len, head_dim, dtype=F32),
             vm(seq_len, rows_own, dtype=F32),
-            dma((2,)), dma((2,)), dma((1,)), dma((7,)), dma((1,)), dma((7,)), dma((1,)), dma((1,)), dma((1,)), dma((1,)), dma((3,)), dma((17,)), pltpu.SemaphoreType.REGULAR((3,))],
+            dma((2,)), dma((2,)), dma((1,)), dma((7,)), dma((1,)), dma((7,)), dma((1,)), dma((1,)), dma((1,)), dma((1,)), dma((3,)), dma((17,)), pltpu.SemaphoreType.REGULAR((7,))],
         compiler_params=pltpu.CompilerParams(collective_id=2, has_side_effects=True, vmem_limit_bytes=34340864),
     )(*early, d_w1, d_w3, *late, *[pltpu.with_memory_space_constraint(a, pltpu.HBM) for a in (d_down, y_out, early_rows)])
 
@@ -555,7 +568,7 @@
             copy.wait()
 
     fetch(0).start()
-    greet(other)
+    greet(where)
     do_gather = Gather(lambda d: dout_ref.at[tok_of(d), :], do_send, do_recv, where, dout_ref.at[pl.ds(0, 7 * tokens), :], own=dout_own)
     do_gather.start()
     own_in.wait()
@@ -564,6 +577,7 @@
     for copy in loads:
         copy.wait()
 
+    relay(where, credit, 5)
     def out_step(step, _):
         @pl.when(step >= 2)
         def _():
@@ -700,7 +714,7 @@
             vm(2, tokens, model), vm(seq_len, 256), vm(seq_len, 256), vm(256, seq_len), vm(256, seq_len),
             vm(256, hid, dtype=F32), vm(256, hid, dtype=F32), vm(hid, 256, dtype=F32), vm(tokens, model),
             dma((2, 4)), dma((2, 4)), dma((2, 3)), dma((2, 3)), dma((1,)), dma((7,)),
-            dma((2,)), dma((2,)), dma((3,)), dma((5,)), dma((5,)), dma((2,)), pltpu.SemaphoreType.REGULAR((5,))],
+            dma((2,)), dma((2,)), dma((3,)), dma((5,)), dma((5,)), dma((2,)), pltpu.SemaphoreType.REGULAR((9,))],
         compiler_params=pltpu.CompilerParams(collective_id=1, has_side_effects=True, vmem_limit_bytes=63 * 1024 * 1024),
     )(m_all, d_out, w1, w3, w2, hidden, gains)[:7]
 
@@ -717,7 +731,7 @@
                           q_hbm, k_hbm, v_hbm, ot_hbm, ut_hbm, cos_hbm, sin_hbm, gfull_hbm, h_hbm, m_ref, w1_ref, w3_ref,
                           q_ref, k_ref, v_ref, ot_ref, ut_ref, cos_ref, sin_ref, gfull_ref, h_ref, pos_ref, gain1_ref, gain2_ref, freq_ref, gain_ref, x_all, gain_all, w_head, wo_all, o_all, u_blk, qkv_blk, o_scr, o_own, h_scr, m_out, stage,
                           g_send, g_recv, w_send, w_recv, x_send, x_recv, wo_send, wo_recv, bulk_send, bulk_recv,
-                          o_send, o_recv, m_loc, m_send, m_recv, loc_sem, own_sem, st_sem):
+                          o_send, o_recv, m_loc, m_send, m_recv, loc_sem, own_sem, st_sem, entry):
     tiny = [pltpu.make_async_copy(src, dst, own_sem.at[8 + i]) for i, (src, dst) in enumerate((
         (gain1_hbm, gain1_ref), (gain2_hbm, gain2_ref), (pos_hbm, pos_ref), (freq_hbm, freq_ref)))]
     for copy in tiny:
@@ -726,7 +740,7 @@
     me, other, first, second = where
     core = lax.rem(me, 2)
     partner = other(1, 0, 0)
-    greet(other)
+    greet(where)
     tokens, model = x_ref.shape
     seq_len, head_dim = k_ref.shape
     qw = heads * head_dim
@@ -748,13 +762,14 @@
     q_of = lambda d: pl.ds(pl.multiple_of(d * qw, qw), qw)
     kv_of = lambda d: pl.ds(pl.multiple_of(d * head_dim, head_dim), head_dim)
     seven_rows = pl.ds(0, 7 * rows_own)
+    x_gather = Gather(lambda d: x_all.at[tok_of(d), :], x_send, x_recv, where, x_all.at[pl.ds(0, 7 * tokens), :], own=x_ref)
+    x_gather.start()
+    relay(where, entry, 0)
     slices = []
     for i, (src, rows, low, high) in enumerate(((wq_ref, q_of, 0, qw), (wk_ref, kv_of, qw, qw + head_dim),
                                                 (wv_ref, kv_of, qw + head_dim, qw + 2 * head_dim))):
         slices.append(to_all(lambda dest: src.at[rows(dest), :], w_head.at[low:high, cols_of(me)],
                              w_head.at[low:high, seven_rows], (w_send.at[i], w_recv.at[i])))
-    x_gather = Gather(lambda d: x_all.at[tok_of(d), :], x_send, x_recv, where, x_all.at[pl.ds(0, 7 * tokens), :], own=x_ref)
-    x_gather.start()
     for copy in tiny:
         copy.wait()
     gain_ref[...] = jnp.zeros_like(gain_ref)
@@ -981,7 +996,7 @@
             vm(8, rows_own, dtype=F32), vm(seq_len, model), vm(8, 8, rows_own, dtype=F32),
             vm(384, model), vm(model, model), vm(seq_len, model), vm(tokens, model), vm(tokens, 384), vm(heads, seq_len, head_dim),
             vm(seq_len, heads * head_dim), vm(tokens, model, dtype=F32), vm(2, tokens, model), vm(2, rows_own, hid)] + pairs + [
-            dma((2,)), dma((4,)), dma((4,)), dma((4,)), dma((12,)), dma((9,))],
+            dma((2,)), dma((4,)), dma((4,)), dma((4,)), dma((12,)), dma((9,)), pltpu.SemaphoreType.REGULAR((4,))],
         compiler_params=pltpu.CompilerParams(collective_id=0, has_side_effects=True, vmem_limit_bytes=63 * 1024 * 1024),
     )(x_in, positions, gain1, gain2, jnp.asarray(freq), w_q, w_k, w_v, wo_own, w_gate, w_up)
 

time: 681 us -> 680 us (level)
  no operation moved by 1% of the time
where the time goes in v12:
time: 680 us; the launch traced here: 679 us
  Pallas kernels  679 us (100%)
    pallas_call x1, Pallas kernels, attention_backward_step(): pl.pallas_call(functools.partial(attn_bwd_comm_kernel, 'sp', heads), name...  277 us
    pallas_call x1, Pallas kernels, attention_step(): pl.pallas_call(functools.partial(attention_comm_kernel, 'sp', heads), nam...  215 us
    pallas_call x1, Pallas kernels, mlp_step(): pl.pallas_call(functools.partial(mlp_comm_kernel, 'sp'), name='mlp_comm',...  176 us

profile of v12, /device:TPU:0, one launch (start us, length us, event | category | flops | bytes accessed | tf_op | source)
XLA Modules:
  0.0 679.5 jit_solution(16938896678101349757)
XLA Ops:
  0.6 215.3 %attention_comm.1 = (bf16[4,2048,64]{2,1,0:T(8,128)(2,1)}, bf16[2048,64]{1,0:T(8,128)(2,1)}, bf16[2048,64]{1,0:T(8,128)(2,1)}, bf16[256,2048]{1,0:T(8,128)(2,1)}...) custom-call(bf16[256,2048]{1,0:T(8,128)(2,1)} %x_hbm.1, ...), custom_call_target="tpu_custom_call" | custom-call | tf_op jit(solution)/shard_map/attention_comm/pallas_call | solution.py:990
  215.9 175.7 %mlp_comm.1 = (f32[2048,1024]{1,0:T(8,128)}, f32[2048,1024]{1,0:T(8,128)}, f32[1024,2048]{1,0:T(8,128)}, bf16[256,2048]{1,0:T(8,128)(2,1)}, bf16[256,2048]{1,0:T...) custom-call(bf16[2048,2048]{1,0:T(8,128)(2,1)} %get-tuple-element.51.m_ref, ...), custom_call_target="tpu_custom_call" | custom-call | tf_op jit(solution)/shard_map/mlp_comm/pallas_call | solution.py:704
  391.6 276.8 %attn_bwd_comm.1 = (f32[256,2048]{1,0:T(8,128)S(1)}, f32[2048,256]{1,0:T(8,128)S(1)}, f32[512,256]{1,0:T(8,128)S(1)}, f32[512,256]{1,0:T(8,128)S(1)}, f32[256,81...) custom-call(bf16[256,2048]{1,0:T(8,128)(2,1)} %get-tuple-element.56., ...), custom_call_target="tpu_custom_call" | custom-call | tf_op jit(solution)/shard_map/attn_bwd_comm/pallas_call | solution.py:356
  668.5 10.8 %hand_over.1 = (f32[1024,2048]{1,0:T(8,128)}, bf16[256,2048]{1,0:T(8,128)(2,1)}, f32[256,8192]{1,0:T(8,128)}, f32[256,8192]{1,0:T(8,128)}, f32[256,2048]{1,0:T(8...) custom-call(f32[1024,2048]{1,0:T(8,128)S(1)} %get-tuple-element.70.r, ...), custom_call_target="tpu_custom_call" | custom-call | tf_op jit(solution)/shard_map/hand_over/pallas_call | solution.py:1021

commit v13 on v12

--- a/solution.py
+++ b/solution.py
@@ -1004,9 +1004,12 @@
 def hand_over_kernel(n_in, *refs):
     sources, gains, results = refs[:n_in], refs[n_in], refs[n_in + 1:2 * n_in + 1]
     gain_outs, lines, sem = refs[2 * n_in + 1:2 * n_in + 3], refs[2 * n_in + 3:2 * n_in + 5], refs[2 * n_in + 5]
-    stores = [pltpu.make_async_copy(sources[i], results[i], sem.at[i]) for i in range(n_in)]
-    for store in stores:
-        store.start()
+    stores = []
+    for i, (src, dst) in enumerate(zip(sources, results)):
+        rows = max(16, min(src.shape[0], (1 << 21) // (src.shape[1] * src.dtype.itemsize)))
+        for low in range(0, src.shape[0], rows):
+            pltpu.make_async_copy(src.at[pl.ds(low, rows)], dst.at[pl.ds(low, rows)], sem.at[i]).start()
+        stores.append(pltpu.make_async_copy(src, dst, sem.at[i]))
     for i in range(2):
         lines[i][...] = gains[i, :]
         stores.append(pltpu.make_async_copy(lines[i], gain_outs[i], sem.at[n_in + i]))

time: 680 us -> 680 us (level)
  no operation moved by 1% of the time
where the time goes in v13:
time: 680 us; the launch traced here: 679 us
  Pallas kernels  678 us (100%)
    pallas_call x1, Pallas kernels, attention_backward_step(): pl.pallas_call(functools.partial(attn_bwd_comm_kernel, 'sp', heads), name...  277 us
    pallas_call x1, Pallas kernels, attention_step(): pl.pallas_call(functools.partial(attention_comm_kernel, 'sp', heads), nam...  215 us
    pallas_call x1, Pallas kernels, mlp_step(): pl.pallas_call(functools.partial(mlp_comm_kernel, 'sp'), name='mlp_comm',...  176 us

profile of v13, /device:TPU:0, one launch (start us, length us, event | category | flops | bytes accessed | tf_op | source)
XLA Modules:
  0.0 679.3 jit_solution(255553326888044143)
XLA Ops:
  0.6 215.3 %attention_comm.1 = (bf16[4,2048,64]{2,1,0:T(8,128)(2,1)}, bf16[2048,64]{1,0:T(8,128)(2,1)}, bf16[2048,64]{1,0:T(8,128)(2,1)}, bf16[256,2048]{1,0:T(8,128)(2,1)}...) custom-call(bf16[256,2048]{1,0:T(8,128)(2,1)} %x_hbm.1, ...), custom_call_target="tpu_custom_call" | custom-call | tf_op jit(solution)/shard_map/attention_comm/pallas_call | solution.py:990
  215.9 175.7 %mlp_comm.1 = (f32[2048,1024]{1,0:T(8,128)}, f32[2048,1024]{1,0:T(8,128)}, f32[1024,2048]{1,0:T(8,128)}, bf16[256,2048]{1,0:T(8,128)(2,1)}, bf16[256,2048]{1,0:T...) custom-call(bf16[2048,2048]{1,0:T(8,128)(2,1)} %get-tuple-element.51.m_ref, ...), custom_call_target="tpu_custom_call" | custom-call | tf_op jit(solution)/shard_map/mlp_comm/pallas_call | solution.py:704
  391.6 276.8 %attn_bwd_comm.1 = (f32[256,2048]{1,0:T(8,128)S(1)}, f32[2048,256]{1,0:T(8,128)S(1)}, f32[512,256]{1,0:T(8,128)S(1)}, f32[512,256]{1,0:T(8,128)S(1)}, f32[256,81...) custom-call(bf16[256,2048]{1,0:T(8,128)(2,1)} %get-tuple-element.56., ...), custom_call_target="tpu_custom_call" | custom-call | tf_op jit(solution)/shard_map/attn_bwd_comm/pallas_call | solution.py:356
  668.5 10.7 %hand_over.1 = (f32[1024,2048]{1,0:T(8,128)}, bf16[256,2048]{1,0:T(8,128)(2,1)}, f32[256,8192]{1,0:T(8,128)}, f32[256,8192]{1,0:T(8,128)}, f32[256,2048]{1,0:T(8...) custom-call(f32[1024,2048]{1,0:T(8,128)S(1)} %get-tuple-element.70.r, ...), custom_call_target="tpu_custom_call" | custom-call | tf_op jit(solution)/shard_map/hand_over/pallas_call | solution.py:1024
